TPU v7x, 32 devices: a whole 2x2x4 slice. The times are simulated.
32 devices in a mesh: seq: 8 (over y, x, core), tp: 4 (over z).
Axes of the slice: x: 2, y: 2, z: 4, core: 2. Of those that a mesh axis runs over, the one named last changes fastest.
Arguments:
- hidden_in: bfloat16 [4096, 2048], P('seq', 'tp'), may hold values from -60 to 60
- w_query: bfloat16 [2048, 2048], P(None, 'tp'), may hold values from -0.125 to 0.125
- w_key: bfloat16 [2048, 2048], P(None, 'tp'), may hold values from -0.125 to 0.125
- w_value: bfloat16 [2048, 2048], P(None, 'tp'), may hold values from -0.8984375 to 0.8984375
- w_pos: bfloat16 [2048, 2048], P(None, 'tp'), may hold values from -0.125 to 0.125
- w_out: bfloat16 [2048, 2048], P('tp'), may hold values from -0.125 to 0.125
- bias_content: float32 [16, 128], P('tp'), may hold values from -4 to 4
- bias_pos: float32 [16, 128], P('tp'), may hold values from -4 to 4
- norm_gain: float32 [2048], P('tp'), may hold values from 0.1 to 1.9
- norm_bias: float32 [2048], P('tp'), may hold values from -3 to 3
Outputs:
- hidden_out: bfloat16 [4096, 2048], P('seq', 'tp')
All inputs are finite; a program needn't handle non-finite values.
Results may differ from a plain program's by a relative error of at most 0.014.
The roundings to bfloat16 on the way count: a program that leaves them out, or rounds other values in their place, can miss the bound.
Values may be sent and summed in bfloat16 or wider, within the bound.
No kernel may reach another device: no remote copies, remote signals or barrier semaphores. Data moves between devices by JAX's collectives and lax.ppermute only.
A program may use at most 128 MiB of HBM per device.

v0:
```python
import jax
import jax.numpy as jnp
from jax import lax
from jax.sharding import PartitionSpec as P


def shifted(block, axis, distance):
    devices = range(lax.axis_size(axis))
    route = [(i - distance, i) for i in devices if i - distance in devices]
    return lax.ppermute(block, axis, route)


def relative_table(span, width):
    half = width // 2
    freq = jnp.exp(-jnp.log(10000.0) * jnp.arange(half).astype(jnp.float32) / half)
    distance = (span - 1 - jnp.arange(span)).astype(jnp.float32)
    angle = distance[:, None] * freq[None, :]
    return jnp.concatenate([jnp.sin(angle), jnp.cos(angle)], 1).astype(jnp.bfloat16)


def shift_rows(table, seg, span):
    heads = table.shape[0]
    padded = jnp.pad(table, ((0, 0), (0, 0), (0, 1)))
    flat = padded.reshape(heads, seg * (span + 1))
    return flat[:, seg - 1 : seg - 1 + seg * span].reshape(heads, seg, span)


def shards(
    hidden_in, w_query, w_key, w_value, w_pos, w_out, bias_content, bias_pos, norm_gain, norm_bias
):
    seg = hidden_in.shape[0]
    heads = bias_content.shape[0]
    head_dim = bias_content.shape[1]
    width = heads * head_dim
    model_width = w_query.shape[0]
    span = 3 * seg
    memory = 2 * seg
    place = lax.axis_index("seq")
    own = lax.all_gather(hidden_in, "tp", axis=1, tiled=True)
    query = jnp.dot(own, w_query, preferred_element_type=jnp.float32).astype(jnp.bfloat16)
    own_keys = jnp.dot(own, w_key, preferred_element_type=jnp.float32).astype(jnp.bfloat16)
    own_values = jnp.dot(own, w_value, preferred_element_type=jnp.float32).astype(jnp.bfloat16)
    key_parts = []
    value_parts = []
    for distance in (2, 1):
        earlier_keys, earlier_values = shifted((own_keys, own_values), "seq", distance)
        key_parts.append(earlier_keys)
        value_parts.append(earlier_values)
    keys = jnp.concatenate(key_parts + [own_keys], 0)
    values = jnp.concatenate(value_parts + [own_values], 0)
    rel = jnp.dot(
        relative_table(span, model_width), w_pos, preferred_element_type=jnp.float32
    ).astype(jnp.bfloat16)
    rel = rel.reshape(span, heads, head_dim)
    keys = keys.reshape(span, heads, head_dim)
    values = values.reshape(span, heads, head_dim)
    q_rows = query.astype(jnp.float32).reshape(seg, heads, head_dim)
    content_q = (q_rows + bias_content[None]).astype(jnp.bfloat16)
    pos_q = (q_rows + bias_pos[None]).astype(jnp.bfloat16)
    content = jnp.einsum("ihd,jhd->hij", content_q, keys, preferred_element_type=jnp.float32)
    position = jnp.einsum("ihd,ehd->hie", pos_q, rel, preferred_element_type=jnp.float32)
    position = shift_rows(position, seg, span)
    score = (content + position) * (1.0 / jnp.sqrt(jnp.float32(head_dim)))
    row = jnp.arange(seg)[:, None]
    col = jnp.arange(span)[None, :]
    allowed = (col <= row + memory) & (place * seg - memory + col >= 0)
    score = jnp.where(allowed[None], score, jnp.float32(-1e30))
    probs = jax.nn.softmax(score, axis=-1).astype(jnp.bfloat16)
    attended = jnp.einsum("hij,jhd->ihd", probs, values, preferred_element_type=jnp.float32)
    attended = attended.astype(jnp.bfloat16).reshape(seg, width)
    partial_out = jnp.dot(attended, w_out, preferred_element_type=jnp.float32)
    branch = lax.psum_scatter(
        partial_out.astype(jnp.bfloat16), "tp", scatter_dimension=1, tiled=True
    ).astype(jnp.float32)
    summed = hidden_in.astype(jnp.float32) + branch
    total = lax.psum(jnp.sum(summed, axis=1), "tp")
    center = total / model_width
    centred = summed - center[:, None]
    spread = lax.psum(jnp.sum(centred * centred, axis=1), "tp") / model_width
    normed = centred / jnp.sqrt(spread[:, None] + 1e-05)
    return (normed * norm_gain[None] + norm_bias[None]).astype(jnp.bfloat16)


def solution(mesh):
    in_specs = (
        P("seq", "tp"),
        P(None, "tp"),
        P(None, "tp"),
        P(None, "tp"),
        P(None, "tp"),
        P("tp", None),
        P("tp", None),
        P("tp", None),
        P("tp"),
        P("tp"),
    )
    out_specs = P("seq", "tp")
    return jax.shard_map(shards, mesh=mesh, in_specs=in_specs, out_specs=out_specs, check_vma=False)
```

profile of v0, /device:TPU:12, one launch (start us, length us, event | category | flops | bytes accessed | tf_op | source)
XLA Modules:
  0.0 255.1 jit_solution(2363888968351827985)
XLA Ops:
  6.5 0.7 all-gather.2.cloned.1.call-update
  7.3 0.0 reduce-scatter.2.cloned.1.call-start
  7.4 0.6 fusion.10
  8.0 23.2 %fusion.3 = (bf16[1536,1024]{1,0:T(8,128)(2,1)S(1)}, bf16[1536,1024]{1,0:T(8,128)(2,1)S(1)}) fusion(f32[1024]{0:T(1024)S(1)} %multiply_exponential_fusion, f32[1536]{0:T(1024)S(1)} %subtract_convert_fusion), kind=kLoop, calls=%fused_computation.8 | loop fusion | flops 4718592 | bytes 6301696 | tf_op jit(solution)/shard_map/convert.1
  31.2 4.8 %fusion.11 = bf16[1536,512]{0,1:T(8,128)(2,1)} fusion(bf16[2048,512]{1,0:T(8,128)(2,1)S(1)} %copy-done.7, bf16[1536,1024]{1,0:T(8,128)(2,1)S(1)} %get-tuple-element.6, bf16[1536,1024]{1,0:T(8,128)(2,1)S(1)} %get-tuple-element.5), kind=kOutput, calls=%fused_computation.17 | convolution fusion | flops 3234594816 | bytes 9961472 | tf_op jit(solution)/shard_map/dot_general | solution.py:51
  36.1 18.3 %all-gather.2.cloned.1.call-done = bf16[512,2048]{1,0:T(8,128)(2,1)} async-done(((bf16[512,512]{1,0:T(8,128)(2,1)}), bf16[512,2048]{1,0:T(8,128)(2,1)}) %all-gather.2.cloned.1.call-update) | async-done | bytes 2097168 | tf_op jit(solution)/shard_map/all_gather | solution.py:39
  54.4 3.6 %convolution_convert_fusion.1 = bf16[512,512]{1,0:T(8,128)(2,1)S(1)} fusion(bf16[512,2048]{1,0:T(8,128)(2,1)} %all-gather.2.cloned.1.call-done, bf16[2048,512]{1,0:T(8,128)(2,1)} %param.12), kind=kOutput, calls=%fused_computation.23 | convolution fusion | flops 1074003968 | bytes 4718592 | tf_op jit(solution)/shard_map/dot_general | solution.py:41
  58.0 3.5 %collective-permute-start.2 = (bf16[512,512]{1,0:T(8,128)(2,1)S(1)}, bf16[512,512]{1,0:T(8,128)(2,1)}, u32[]{:S(2)}, u32[]{:S(2)}) collective-permute-start(bf16[512,512]{1,0:T(8,128)(2,1)S(1)} %convolution_convert_fusion.1), channel_id=1, source_target_pairs={{0,8},{4,12},{8,16},{12,20},{16,24},{20,28},{1,9},{5,13},{9,17},{1... | collective-permute-start | bytes 1572872 | tf_op jit(solution)/shard_map/ppermute | solution.py:10
  61.5 1.9 collective-permute-start.3
  63.5 2.0 convolution_convert_fusion.3
  65.5 2.0 collective-permute-start
  67.6 1.9 collective-permute-start.1
  69.5 2.1 convolution_convert_fusion.2
  71.6 2.2 copy.16
  73.9 8.1 %fusion.19 = f32[4,512,1536]{2,1,0:T(8,128)} fusion(bf16[1536,4,128]{0,2,1:T(8,128)(2,1)} %bitcast.35, f32[512,4,128]{2,0,1:T(8,128)} %copy.16, f32[4,128]{1,0:T(4,128)S(1)} %copy-done.3), kind=kOutput, calls=%fused_computation.34 | convolution fusion | flops 805830656 | bytes 15206400 | tf_op jit(solution)/shard_map/ihd,ehd->hie/dot_general | solution.py:61
  82.0 10.7 %pad.4 = f32[4,512,1537]{2,1,0:T(8,128)} pad(f32[4,512,1536]{2,1,0:T(8,128)} %fusion.19, f32[]{:T(128)} %constant.13.clone.1), padding=0_0x0_0x0_1 | pad | bytes 25174020 | tf_op jit(solution)/shard_map/jit(_pad)/pad | solution.py:23
  92.6 20.2 %reshape.101 = f32[3147776]{0:T(1024)} reshape(f32[4,512,1537]{2,1,0:T(8,128)} %pad.4) | data formatting | bytes 25182208
  112.8 15.0 %reshape.96 = f32[4,786944]{1,0:T(4,128)} reshape(f32[3147776]{0:T(1024)} %reshape.101) | data formatting | bytes 25182208 | tf_op jit(solution)/shard_map/reshape | solution.py:24
  127.8 9.7 %slice.4 = f32[4,786432]{1,0:T(4,128)S(1)} slice(f32[4,786944]{1,0:T(4,128)} %reshape.96), slice={[0:4], [511:786943]} | slice | bytes 25165824 | tf_op jit(solution)/shard_map/slice | solution.py:25
  137.5 11.5 %fusion.2 = f32[4,512,1536]{2,1,0:T(8,128)} fusion(f32[1,4,512,1536]{3,1,2,0:T(4,128)S(1)} %bitcast.34, pred[512,1536]{1,0:T(8,128)(4,1)S(1)} %fusion.10, f32[512,4,128]{2,0,1:T(8,128)S(1)} %copy-done.1, f32[4,128]{1,0:T(4,128)S(1)} %copy-done.4, bf16[512,512]{1,0:T(8,128)(2,1)S(1)} %convolution_convert_fusion.1, ...), kind=kOutput, calls=%fused_computation.3 | convolution fusion | flops 819986432 | bytes 28575744 | tf_op jit(solution)/shard_map/ihd,jhd->hij/dot_general | solution.py:60
  149.1 10.4 %fusion.24 = f32[4,512]{1,0:T(4,128)S(1)} fusion(f32[4,512,1536]{2,1,0:T(8,128)} %fusion.2), kind=kOutput, calls=%fused_computation.45 | output fusion | flops 6292991 | bytes 12591104 | tf_op jit(solution)/shard_map/sub | solution.py:68
  159.6 2.6 %pad_maximum_fusion = bf16[1536,512]{1,0:T(8,128)(2,1)} fusion(bf16[512,512]{1,0:T(8,128)(2,1)} %convolution_convert_fusion.3, bf16[512,512]{1,0:T(8,128)(2,1)} %collective-permute-done.1, bf16[512,512]{1,0:T(8,128)(2,1)} %collective-permute-done), kind=kLoop, calls=%fused_computation.21 | loop fusion | flops 4718592 | bytes 3145728 | tf_op jit(solution)/shard_map/concatenate | solution.py:50
  162.2 2.6 %copy.22 = bf16[1536,512]{0,1:T(8,128)(2,1)} copy(bf16[1536,512]{1,0:T(8,128)(2,1)} %pad_maximum_fusion) | data formatting | bytes 3145728 | tf_op jit(solution)/shard_map/reshape | solution.py:56
  164.8 10.9 %fusion.16 = bf16[4,128,512]{2,1,0:T(8,128)(2,1)S(1)} fusion(bf16[1536,4,128]{0,2,1:T(8,128)(2,1)} %bitcast.36, f32[4,512]{1,0:T(4,128)S(1)} %fusion.24, f32[4,512,1536]{2,1,0:T(8,128)} %fusion.2), kind=kOutput, calls=%fused_computation.26 | convolution fusion | flops 815009280 | bytes 14688256 | tf_op jit(solution)/shard_map/hij,jhd->ihd/dot_general | solution.py:69
  175.7 2.6 %convolution_convert_fusion = bf16[512,2048]{1,0:T(8,128)(2,1)} fusion(bf16[512,512]{0,1:T(8,128)(2,1)S(1)} %bitcast.38, bf16[512,2048]{1,0:T(8,128)(2,1)S(1)} %copy-done), kind=kOutput, calls=%fused_computation.18 | convolution fusion | flops 1074790400 | bytes 4718592 | tf_op jit(solution)/shard_map/dot_general | solution.py:71
  178.3 0.0 reduce-scatter.2.cloned.1.call-update
  178.4 45.6 %reduce-scatter.2.cloned.1.call-done = bf16[512,512]{1,0:T(8,128)(2,1)} async-done(((bf16[512,2048]{1,0:T(8,128)(2,1)}), bf16[512,512]{1,0:T(8,128)(2,1)}) %reduce-scatter.2.cloned.1.call-update) | async-done | bytes 524304 | tf_op jit(solution)/shard_map/reduce_scatter | solution.py:72
  223.9 1.3 fusion.18
  225.2 9.7 %psum.14 = f32[512]{0:T(512)S(1)} all-reduce(f32[512]{0:T(512)S(1)} %fusion.18), channel_id=1, replica_groups=mesh['seq'=8,'tp'=4] {'tp'}, use_global_device_ids=true, to_apply=%region_4.5 | all-reduce | flops 512 | bytes 4096 | tf_op jit(solution)/shard_map/psum | solution.py:76
  234.9 1.3 multiply_reduce_fusion
  236.2 9.9 %psum.15 = f32[512]{0:T(512)S(1)} all-reduce(f32[512]{0:T(512)S(1)} %multiply_reduce_fusion), channel_id=1, replica_groups=mesh['seq'=8,'tp'=4] {'tp'}, use_global_device_ids=true, to_apply=%region_6.7 | all-reduce | flops 512 | bytes 4096 | tf_op jit(solution)/shard_map/psum | solution.py:79
  246.1 2.1 add_convert_fusion
  (33 shorter events, 0.1 us)
Async XLA Ops:
  6.5 169.2 %copy-start = (bf16[512,2048]{1,0:T(8,128)(2,1)S(1)}, bf16[512,2048]{1,0:T(8,128)(2,1)}, u32[]{:S(2)}) copy-start(bf16[512,2048]{1,0:T(8,128)(2,1)} %param.15) | copy-start | bytes 6291460
  6.5 47.9 %all-gather.2.cloned.1.call-start = ((), (), s32[]{:S(2)}) async-start(), calls=%async_computation.1 | async-start | bytes 2621440 | tf_op jit(solution)/shard_map/all_gather | solution.py:39
  7.3 216.7 %reduce-scatter.2.cloned.1.call-start = ((), (), s32[]{:S(2)}) async-start(), calls=%async_computation.2 | async-start | bytes 2621440 | tf_op jit(solution)/shard_map/reduce_scatter | solution.py:72
  7.9 23.3 %copy-start.7 = (bf16[2048,512]{1,0:T(8,128)(2,1)S(1)}, bf16[2048,512]{1,0:T(8,128)(2,1)}, u32[]{:S(2)}) copy-start(bf16[2048,512]{1,0:T(8,128)(2,1)} %param.14) | copy-start | bytes 6291460
  54.4 9.1 %copy-start.8 = (bf16[2048,512]{1,0:T(8,128)(2,1)S(1)}, bf16[2048,512]{1,0:T(8,128)(2,1)}, u32[]{:S(2)}) copy-start(bf16[2048,512]{1,0:T(8,128)(2,1)} %param.13) | copy-start | bytes 6291460
  54.4 9.1 %copy-start.10 = (bf16[512,2048]{1,0:T(8,128)(2,1)S(1)}, bf16[512,2048]{1,0:T(8,128)(2,1)}, u32[]{:S(2)}) copy-start(bf16[512,2048]{1,0:T(8,128)(2,1)} %all-gather.2.cloned.1.call-done) | copy-start | bytes 6291460
  58.0 11.5 %copy-start.9 = (bf16[2048,512]{1,0:T(8,128)(2,1)S(1)}, bf16[2048,512]{1,0:T(8,128)(2,1)}, u32[]{:S(2)}) copy-start(bf16[2048,512]{1,0:T(8,128)(2,1)} %param.11) | copy-start | bytes 6291460
  58.0 79.5 %collective-permute-start.2 = (bf16[512,512]{1,0:T(8,128)(2,1)S(1)}, bf16[512,512]{1,0:T(8,128)(2,1)}, u32[]{:S(2)}, u32[]{:S(2)}) collective-permute-start(bf16[512,512]{1,0:T(8,128)(2,1)S(1)} %convolution_convert_fusion.1), channel_id=1, source_target_pairs={{0,8},{4,12},{8,16},{12,20},{16,24},{20,28},{1,9},{5,13},{9,17},{1... | collective-permute-start | bytes 1572872 | tf_op jit(solution)/shard_map/ppermute | solution.py:10
  61.5 76.0 %collective-permute-start.3 = (bf16[512,512]{1,0:T(8,128)(2,1)S(1)}, bf16[512,512]{1,0:T(8,128)(2,1)}, u32[]{:S(2)}, u32[]{:S(2)}) collective-permute-start(bf16[512,512]{1,0:T(8,128)(2,1)S(1)} %convolution_convert_fusion.1), channel_id=1, source_target_pairs={{0,4},{4,8},{8,12},{12,16},{16,20},{20,24},{24,28},{1,5},{5,9},{9,... | collective-permute-start | bytes 1572872 | tf_op jit(solution)/shard_map/ppermute | solution.py:10
  65.5 8.3 %copy-start.3 = (f32[4,128]{1,0:T(4,128)S(1)}, f32[4,128]{1,0:T(4,128)}, u32[]{:S(2)}) copy-start(f32[4,128]{1,0:T(4,128)} %param.17) | copy-start | bytes 6148
  65.5 94.0 %collective-permute-start = (bf16[512,512]{1,0:T(8,128)(2,1)}, bf16[512,512]{1,0:T(8,128)(2,1)}, u32[]{:S(2)}, u32[]{:S(2)}) collective-permute-start(bf16[512,512]{1,0:T(8,128)(2,1)} %convolution_convert_fusion.3), channel_id=1, source_target_pairs={{0,8},{4,12},{8,16},{12,20},{16,24},{20,28},{1,9},{5,13},{9,17},{1... | collective-permute-start | bytes 1572872 | tf_op jit(solution)/shard_map/ppermute | solution.py:10
  67.6 92.0 %collective-permute-start.1 = (bf16[512,512]{1,0:T(8,128)(2,1)}, bf16[512,512]{1,0:T(8,128)(2,1)}, u32[]{:S(2)}, u32[]{:S(2)}) collective-permute-start(bf16[512,512]{1,0:T(8,128)(2,1)} %convolution_convert_fusion.3), channel_id=1, source_target_pairs={{0,4},{4,8},{8,12},{12,16},{16,20},{20,24},{24,28},{1,5},{5,9},{9,... | collective-permute-start | bytes 1572872 | tf_op jit(solution)/shard_map/ppermute | solution.py:10
  127.8 9.7 %copy-start.1 = (f32[512,4,128]{2,0,1:T(8,128)S(1)}, f32[512,4,128]{2,0,1:T(8,128)}, u32[]{:S(2)}) copy-start(f32[512,4,128]{2,0,1:T(8,128)} %copy.16) | copy-start | bytes 3145732
  127.8 9.7 %copy-start.4 = (f32[4,128]{1,0:T(4,128)S(1)}, f32[4,128]{1,0:T(4,128)}, u32[]{:S(2)}) copy-start(f32[4,128]{1,0:T(4,128)} %param.16) | copy-start | bytes 6148
  175.7 48.2 %copy-start.2 = (bf16[512,512]{1,0:T(8,128)(2,1)S(1)}, bf16[512,512]{1,0:T(8,128)(2,1)}, u32[]{:S(2)}) copy-start(bf16[512,512]{1,0:T(8,128)(2,1)} %param.10) | copy-start | bytes 1572868
  178.3 67.8 %copy-start.5 = (f32[512]{0:T(512)S(1)}, f32[512]{0:T(512)}, u32[]{:S(2)}) copy-start(f32[512]{0:T(512)} %param.19) | copy-start | bytes 6148
  178.3 67.8 %copy-start.6 = (f32[512]{0:T(512)S(1)}, f32[512]{0:T(512)}, u32[]{:S(2)}) copy-start(f32[512]{0:T(512)} %param.18) | copy-start | bytes 6148
Sparse Core Ops, SparseCore 0:
  8.9 45.4 all-gather.1
  178.5 45.3 reduce-scatter.1
where the time goes:
time: 257 us; the launch traced here: 255 us
  waiting for transfers between devices  64.6 us (25%)
  local copies, waits for them, and re-layouts  60.4 us (24%)
  matrix products  45.8 us (18%)
  other arithmetic  41.6 us (16%)
  blocking collectives  19.6 us (8%)
  between operations  13.6 us (5%)
  starting transfers between devices  9.43 us (4%)
    reduce_scatter x1, waiting for transfers between devices, shards(): lax.psum_scatter(partial_out.astype(jnp.bfloat16), 'tp', scatter_dimensio...  45.6 us
    another operation x1, other arithmetic  23.2 us
    unnamed x23, local copies, waits for them, and re-layouts  20.3 us
    all_gather x1, waiting for transfers between devices, shards(): own = lax.all_gather(hidden_in, 'tp', axis=1, tiled=True)  18.3 us
    reshape x1, local copies, waits for them, and re-layouts, shift_rows(): flat = padded.reshape(heads, seg * (span + 1))  15 us
    dot_general x1, matrix products, shards(): jnp.einsum('ihd,jhd->hij', content_q, keys, preferred_element_type=jnp.fl...  11.5 us
    dot_general x1, matrix products, shards(): jnp.einsum('hij,jhd->ihd', probs, values, preferred_element_type=jnp.floa...  10.9 us
    pad x1, local copies, waits for them, and re-layouts, shift_rows(): padded = jnp.pad(table, ((0, 0), (0, 0), (0, 1)))  10.7 us
  transfers between devices with their start and end apart: 6, of which 2 were waited for; matrix products, arithmetic and copies ran while one was open for 47% of the time, Pallas kernels for 0%

commit v1 on v0

v1 whole, which is shorter than its diff:
```python
import functools

import jax
import jax.numpy as jnp
from jax import lax
from jax.experimental import pallas as pl
from jax.experimental.pallas import tpu as pltpu
from jax.sharding import PartitionSpec as P

ROWS = 128


def relative_table(span, width):
    half = width // 2
    freq = jnp.exp(-jnp.log(10000.0) * jnp.arange(half).astype(jnp.float32) / half)
    distance = (span - 1 - jnp.arange(span)).astype(jnp.float32)
    angle = distance[:, None] * freq[None, :]
    return jnp.concatenate([jnp.sin(angle), jnp.cos(angle)], 1).astype(jnp.bfloat16)


def project_kernel(order, *refs, parts):
    hidden = refs[:parts]
    weights = refs[parts : parts + 3]
    outs = refs[parts + 3 : parts + 6]
    sums = refs[parts + 6 : parts + 9]
    step = pl.program_id(0)
    for part in range(parts):

        @pl.when(step == part)
        def _():
            block = hidden[part][...]
            for weight, total, out in zip(weights, sums, outs):
                value = jnp.dot(block, weight[...], preferred_element_type=jnp.float32)
                if part > 0:
                    value = total[...] + value
                if part < parts - 1:
                    total[...] = value
                else:
                    out[...] = value.astype(jnp.bfloat16)


def project(order, hidden, weights):
    parts = len(hidden)
    rows, block = hidden[0].shape
    width = weights[0].shape[1]
    grid_spec = pltpu.PrefetchScalarGridSpec(
        num_scalar_prefetch=1,
        grid=(parts,),
        in_specs=[pl.BlockSpec((rows, block), lambda k, o: (0, 0)) for _ in hidden]
        + [pl.BlockSpec((block, width), lambda k, o: (o[k], 0)) for _ in weights],
        out_specs=[pl.BlockSpec((rows, width), lambda k, o: (0, 0)) for _ in weights],
        scratch_shapes=[pltpu.VMEM((rows, width), jnp.float32) for _ in weights],
    )
    return pl.pallas_call(
        functools.partial(project_kernel, parts=parts),
        grid_spec=grid_spec,
        out_shape=[jax.ShapeDtypeStruct((rows, width), jnp.bfloat16) for _ in weights],
        cost_estimate=pl.CostEstimate(
            flops=6 * rows * parts * block * width,
            transcendentals=0,
            bytes_accessed=6 * parts * block * width,
        ),
        name="project",
    )(order, *hidden, *weights)


def attend_kernel(place, q, bias_c, bias_p, rel, *refs, first, counts, seg):
    parts = len(counts)
    keys = refs[:parts]
    values = refs[parts : 2 * parts]
    out = refs[2 * parts]
    head = pl.program_id(0)
    head_dim = q.shape[1]
    span = 3 * seg
    log2 = 1.4426950408889634 / head_dim**0.5
    content_bias = bias_c[pl.ds(head, 1), :]
    pos_bias = bias_p[pl.ds(head, 1), :]
    nt = (((1,), (1,)), ((), ()))
    for block in range(q.shape[0] // ROWS):
        top = first + block * ROWS
        width = 2 * seg + top + ROWS
        rows = q[block * ROWS : (block + 1) * ROWS, :].astype(jnp.float32)
        content_q = (rows + content_bias).astype(jnp.bfloat16)
        pos_q = (rows + pos_bias).astype(jnp.bfloat16)
        position = lax.dot_general(
            pos_q, rel[span - width :, :], nt, preferred_element_type=jnp.float32
        )
        position = pltpu.roll(position, width - (ROWS - 1), 1, stride=1, stride_axis=0)
        scores = []
        start = 0
        used = []
        for part in range(parts):
            count = min(counts[part], width - start)
            if count <= 0:
                break
            content = lax.dot_general(
                content_q, keys[part][:count, :], nt, preferred_element_type=jnp.float32
            )
            score = content + position[:, start : start + count]
            back = 2 - start // seg
            if back > 0:
                score = score + jnp.where(place[0] >= back, jnp.float32(0.0), jnp.float32(-1e30))
            if start + count == width:
                row = lax.broadcasted_iota(jnp.int32, (ROWS, ROWS), 0)
                col = lax.broadcasted_iota(jnp.int32, (ROWS, ROWS), 1)
                tail = jnp.where(col <= row, score[:, count - ROWS :], jnp.float32(-1e30))
                score = tail if count == ROWS else jnp.concatenate([score[:, : count - ROWS], tail], 1)
            scores.append(score)
            used.append(count)
            start += count
        score = jnp.concatenate(scores, 1)
        peak = jnp.max(score, axis=1, keepdims=True)
        weight = jnp.exp2((score - peak) * log2)
        total = jnp.sum(weight, axis=1, keepdims=True)
        probs = (weight * (1.0 / total)).astype(jnp.bfloat16)
        result = None
        start = 0
        for part, count in enumerate(used):
            piece = jnp.dot(
                probs[:, start : start + count],
                values[part][:count, :],
                preferred_element_type=jnp.float32,
            )
            result = piece if result is None else result + piece
            start += count
        out[block * ROWS : (block + 1) * ROWS, :] = result.astype(jnp.bfloat16)


def attend(place, query, bias_c, bias_p, rel, keys, values, first, seg):
    heads, head_dim = bias_c.shape
    counts = tuple(k.shape[0] for k in keys)
    rows = query.shape[0]
    column = lambda n: pl.BlockSpec((n, head_dim), lambda h, p: (0, h))
    whole = pl.BlockSpec((heads, head_dim), lambda h, p: (0, 0))
    grid_spec = pltpu.PrefetchScalarGridSpec(
        num_scalar_prefetch=1,
        grid=(heads,),
        in_specs=[column(rows), whole, whole, column(3 * seg)]
        + [column(n) for n in counts]
        + [column(n) for n in counts],
        out_specs=column(rows),
    )
    return pl.pallas_call(
        functools.partial(attend_kernel, first=first, counts=counts, seg=seg),
        grid_spec=grid_spec,
        out_shape=jax.ShapeDtypeStruct((rows, heads * head_dim), jnp.bfloat16),
        cost_estimate=pl.CostEstimate(
            flops=6 * rows * 3 * seg * heads * head_dim,
            transcendentals=rows * 3 * seg * heads,
            bytes_accessed=18 * seg * heads * head_dim,
        ),
        name="attend",
    )(place, query, bias_c, bias_p, rel, *keys, *values)


def shards(
    hidden_in, w_query, w_key, w_value, w_pos, w_out, bias_content, bias_pos, norm_gain, norm_bias
):
    seg, block = hidden_in.shape
    model_width = w_query.shape[0]
    span = 3 * seg
    tp = lax.axis_size("tp")
    seqs = lax.axis_size("seq")
    place = lax.axis_index("seq")
    rank = lax.axis_index("tp")

    def across(x, k):
        return lax.ppermute(x, "tp", [(i, i ^ k) for i in range(tp)])

    def later(x, k):
        return lax.ppermute(x, "seq", [(i, i + k) for i in range(seqs - k)])

    order = jnp.bitwise_xor(rank, jnp.arange(tp)).astype(jnp.int32)
    hidden = [hidden_in] + [across(hidden_in, k) for k in range(1, tp)]
    rel = jnp.dot(
        relative_table(span, model_width), w_pos, preferred_element_type=jnp.float32
    ).astype(jnp.bfloat16)
    query, own_keys, own_values = project(order, hidden, (w_query, w_key, w_value))
    keys = [later(own_keys, k) for k in (2, 1)] + [own_keys]
    values = [later(own_values, k) for k in (2, 1)] + [own_values]
    attended = attend(
        place.reshape(1).astype(jnp.int32), query, bias_content, bias_pos, rel, keys, values, 0, seg
    )
    partial_out = jnp.dot(attended, w_out, preferred_element_type=jnp.float32).astype(jnp.bfloat16)

    def columns(index):
        return lax.dynamic_slice_in_dim(partial_out, index * block, block, 1)

    summed = hidden_in.astype(jnp.float32) + columns(rank).astype(jnp.float32)
    for k in range(1, tp):
        summed = summed + across(columns(rank ^ k), k).astype(jnp.float32)
    total = jnp.sum(summed, axis=1)
    center = total / block
    centred = summed - center[:, None]
    spread = jnp.sum(centred * centred, axis=1)
    stats = jnp.stack([center, spread])
    stats = [stats] + [across(stats, k) for k in range(1, tp)]
    mean = sum(s[0] for s in stats) / tp
    spread = sum(s[1] + block * (s[0] - mean) ** 2 for s in stats) / model_width
    normed = (summed - mean[:, None]) / jnp.sqrt(spread[:, None] + 1e-05)
    return (normed * norm_gain[None] + norm_bias[None]).astype(jnp.bfloat16)


def solution(mesh):
    in_specs = (
        P("seq", "tp"),
        P(None, "tp"),
        P(None, "tp"),
        P(None, "tp"),
        P(None, "tp"),
        P("tp", None),
        P("tp", None),
        P("tp", None),
        P("tp"),
        P("tp"),
    )
    out_specs = P("seq", "tp")
    return jax.shard_map(shards, mesh=mesh, in_specs=in_specs, out_specs=out_specs, check_vma=False)
```

time: 257 us -> 162 us (0.63)
  local copies, waits for them, and re-layouts: 60.4 us -> 2.55 us
  matrix products: 45.8 us -> 10.3 us
  Pallas kernels: 0 us -> 22.1 us
  blocking collectives: 19.6 us -> 0 us
  other arithmetic: 41.6 us -> 28.1 us
  between operations: 13.6 us -> 0.11 us
  starting transfers between devices: 9.43 us -> 22.2 us
  waiting for transfers between devices: 64.6 us -> 75.9 us
    ppermute x4 -> x13, waiting for transfers between devices: 0.01 us -> 75.9 us  [the longest x9 55.2 us: across(): return lax.ppermute(x, 'tp', [(i, i ^ k) for i in range(tp)])]
    reduce_scatter x1 -> x0, waiting for transfers between devices: 45.6 us -> none  [shards(): lax.psum_scatter(partial_out.astype(jnp.bfloat16), 'tp', scatter_dimensio...]
    dot_general x7 -> x1, matrix products: 40.9 us -> 2.3 us  [shards(): jnp.dot(attended, w_out, preferred_element_type=jnp.float32)]
    pallas_call x0 -> x2, Pallas kernels: none -> 22.1 us  [the longest x1 13.6 us: attend(): pl.pallas_call(functools.partial(attend_kernel, first=first, counts=count...]
    reshape x3 -> x0, local copies, waits for them, and re-layouts: 19.8 us -> none  [the longest x1 15 us: shift_rows(): flat = padded.reshape(heads, seg * (span + 1))]
    psum x2 -> x0, blocking collectives: 19.6 us -> none  [the longest x1 9.92 us: shards(): spread = lax.psum(jnp.sum(centred * centred, axis=1), 'tp') / model_width]
    unnamed x23 -> x18, local copies, waits for them, and re-layouts: 20.3 us -> 1.36 us
    all_gather x1 -> x0, waiting for transfers between devices: 18.3 us -> none  [shards(): own = lax.all_gather(hidden_in, 'tp', axis=1, tiled=True)]
  transfers between devices with their start and end apart: 6 -> 13, of which waited for: 2 -> 10; matrix products, arithmetic and copies ran while one was open for 47% -> 20% of each run, Pallas kernels for 0% -> 0%
where the time goes in v1:
time: 162 us; the launch traced here: 161 us
  waiting for transfers between devices  75.9 us (47%)
  other arithmetic  28.1 us (17%)
  starting transfers between devices  22.2 us (14%)
  Pallas kernels  22.1 us (14%)
  matrix products  10.3 us (6%)
  local copies, waits for them, and re-layouts  2.55 us (2%)
    ppermute x9, waiting for transfers between devices, across(): return lax.ppermute(x, 'tp', [(i, i ^ k) for i in range(tp)])  55.2 us
    another operation x1, other arithmetic  24.4 us
    ppermute x4, waiting for transfers between devices, later(): return lax.ppermute(x, 'seq', [(i, i + k) for i in range(seqs - k)])  20.8 us
    pallas_call x1, Pallas kernels, attend(): pl.pallas_call(functools.partial(attend_kernel, first=first, counts=count...  13.6 us
    ppermute x9, starting transfers between devices, across(): return lax.ppermute(x, 'tp', [(i, i ^ k) for i in range(tp)])  12.9 us
    ppermute x4, starting transfers between devices, later(): return lax.ppermute(x, 'seq', [(i, i + k) for i in range(seqs - k)])  9.33 us
    pallas_call x1, Pallas kernels, project(): pl.pallas_call(functools.partial(project_kernel, parts=parts), grid_spec=...  8.54 us
    dot_general x1, matrix products, shards(): jnp.dot(relative_table(span, model_width), w_pos, preferred_element_type=...  8.04 us
  transfers between devices with their start and end apart: 13, of which 10 were waited for; matrix products, arithmetic and copies ran while one was open for 20% of the time, Pallas kernels for 0%

profile of v1, /device:TPU:12, one launch (start us, length us, event | category | flops | bytes accessed | tf_op | source)
XLA Modules:
  0.0 161.4 jit_solution(15077718329768927144)
XLA Ops:
  0.0 0.4 collective-permute-start
  0.5 2.6 %collective-permute-start.1 = (bf16[512,512]{1,0:T(8,128)(2,1)}, bf16[512,512]{1,0:T(8,128)(2,1)S(1)}, u32[]{:S(2)}, u32[]{:S(2)}) collective-permute-start(bf16[512,512]{1,0:T(8,128)(2,1)} %refs_0_.1), channel_id=1, source_target_pairs={{0,2},{1,3},{2,0},{3,1},{4,6},{5,7},{6,4},{7,5},{8,10},{9,11},{10,... | collective-permute-start | bytes 1572872 | tf_op jit(solution)/shard_map/ppermute | solution.py:168
  3.0 0.5 collective-permute-start.2
  3.5 0.5 iota_xor_fusion.order
  4.1 24.4 %fusion = (bf16[1536,1024]{1,0:T(8,128)(2,1)}, bf16[1536,1024]{1,0:T(8,128)(2,1)}) fusion(f32[1024]{0:T(1024)S(1)} %multiply_exponential_fusion, f32[1536]{0:T(1024)S(1)} %subtract_convert_fusion), kind=kLoop, calls=%fused_computation.2 | loop fusion | flops 4718592 | bytes 6301696 | tf_op jit(solution)/shard_map/convert
  28.5 9.7 %collective-permute-done.1.refs_2_ = bf16[512,512]{1,0:T(8,128)(2,1)S(1)} collective-permute-done((bf16[512,512]{1,0:T(8,128)(2,1)}, bf16[512,512]{1,0:T(8,128)(2,1)S(1)}, u32[]{:S(2)}, u32[]{:S(2)}) %collective-permute-start.1) | collective-permute-done | bytes 524320 | tf_op jit(solution)/shard_map/ppermute | solution.py:168
  38.1 10.8 %collective-permute-done.2.refs_3_ = bf16[512,512]{1,0:T(8,128)(2,1)} collective-permute-done((bf16[512,512]{1,0:T(8,128)(2,1)}, bf16[512,512]{1,0:T(8,128)(2,1)}, u32[]{:S(2)}, u32[]{:S(2)}) %collective-permute-start.2) | collective-permute-done | bytes 524320 | tf_op jit(solution)/shard_map/ppermute | solution.py:168
  48.9 8.5 %project.1 = (bf16[512,512]{1,0:T(8,128)(2,1)}, bf16[512,512]{1,0:T(8,128)(2,1)}, bf16[512,512]{1,0:T(8,128)(2,1)}) custom-call(s32[4]{0:T(128)} %iota_xor_fusion.order, bf16[512,512]{1,0:T(8,128)(2,1)} %refs_0_.1, bf16[512,512]{1,0:T(8,128)(2,1)} %copy-done.5, bf16[512,512]{1,0:T(8,128)(2,1)} %copy-done.6, bf16[512,512]{1,0:T(8,128)(2,1)} %collective-permute-done.2.refs_3_, ...), custom_call_target="tpu_custom_call" | custom-call | flops 3221225472 | bytes 6291456 | tf_op jit(solution)/shard_map/project/pallas_call | solution.py:54
  57.5 3.4 %collective-permute-start.3 = (bf16[512,512]{1,0:T(8,128)(2,1)}, bf16[512,512]{1,0:T(8,128)(2,1)S(1)}, u32[]{:S(2)}, u32[]{:S(2)}) collective-permute-start(bf16[512,512]{1,0:T(8,128)(2,1)} %get-tuple-element.9.refs_2_), channel_id=1, source_target_pairs={{0,8},{4,12},{8,16},{12,20},{16,24},{20,28},{1,9},{5,13},{9,17},{1... | collective-permute-start | bytes 1572872 | tf_op jit(solution)/shard_map/ppermute | solution.py:171
  60.9 1.9 %collective-permute-start.4 = (bf16[512,512]{1,0:T(8,128)(2,1)}, bf16[512,512]{1,0:T(8,128)(2,1)S(1)}, u32[]{:S(2)}, u32[]{:S(2)}) collective-permute-start(bf16[512,512]{1,0:T(8,128)(2,1)} %get-tuple-element.9.refs_2_), channel_id=1, source_target_pairs={{0,4},{4,8},{8,12},{12,16},{16,20},{20,24},{24,28},{1,5},{5,9},{9,... | collective-permute-start | bytes 1572872 | tf_op jit(solution)/shard_map/ppermute | solution.py:171
  62.8 1.9 %collective-permute-start.5 = (bf16[512,512]{1,0:T(8,128)(2,1)}, bf16[512,512]{1,0:T(8,128)(2,1)}, u32[]{:S(2)}, u32[]{:S(2)}) collective-permute-start(bf16[512,512]{1,0:T(8,128)(2,1)} %get-tuple-element.10.refs_5_), channel_id=1, source_target_pairs={{0,8},{4,12},{8,16},{12,20},{16,24},{20,28},{1,9},{5,13},{9,17},{1... | collective-permute-start | bytes 1572872 | tf_op jit(solution)/shard_map/ppermute | solution.py:171
  64.7 2.1 %collective-permute-start.6 = (bf16[512,512]{1,0:T(8,128)(2,1)}, bf16[512,512]{1,0:T(8,128)(2,1)}, u32[]{:S(2)}, u32[]{:S(2)}) collective-permute-start(bf16[512,512]{1,0:T(8,128)(2,1)} %get-tuple-element.10.refs_5_), channel_id=1, source_target_pairs={{0,4},{4,8},{8,12},{12,16},{16,20},{20,24},{24,28},{1,5},{5,9},{9,... | collective-permute-start | bytes 1572872 | tf_op jit(solution)/shard_map/ppermute | solution.py:171
  66.8 8.0 %fusion.6.rel = bf16[1536,512]{1,0:T(8,128)(2,1)} fusion(bf16[2048,512]{1,0:T(8,128)(2,1)} %param.14, bf16[1536,1024]{1,0:T(8,128)(2,1)} %get-tuple-element.17, bf16[1536,1024]{1,0:T(8,128)(2,1)} %get-tuple-element.16), kind=kOutput, calls=%fused_computation.8 | convolution fusion | flops 3234594816 | bytes 9961472 | tf_op jit(solution)/shard_map/dot_general | solution.py:175
  74.9 0.4 collective-permute-done.3.refs_0_
  75.3 6.8 %collective-permute-done.4.refs_1_ = bf16[512,512]{1,0:T(8,128)(2,1)S(1)} collective-permute-done((bf16[512,512]{1,0:T(8,128)(2,1)}, bf16[512,512]{1,0:T(8,128)(2,1)S(1)}, u32[]{:S(2)}, u32[]{:S(2)}) %collective-permute-start.4) | collective-permute-done | bytes 524320 | tf_op jit(solution)/shard_map/ppermute | solution.py:171
  82.1 4.5 %collective-permute-done.5.refs_3_ = bf16[512,512]{1,0:T(8,128)(2,1)} collective-permute-done((bf16[512,512]{1,0:T(8,128)(2,1)}, bf16[512,512]{1,0:T(8,128)(2,1)}, u32[]{:S(2)}, u32[]{:S(2)}) %collective-permute-start.5) | collective-permute-done | bytes 524320 | tf_op jit(solution)/shard_map/ppermute | solution.py:171
  86.6 9.0 %collective-permute-done.6.refs_4_ = bf16[512,512]{1,0:T(8,128)(2,1)} collective-permute-done((bf16[512,512]{1,0:T(8,128)(2,1)}, bf16[512,512]{1,0:T(8,128)(2,1)}, u32[]{:S(2)}, u32[]{:S(2)}) %collective-permute-start.6) | collective-permute-done | bytes 524320 | tf_op jit(solution)/shard_map/ppermute | solution.py:171
  95.6 13.6 %attend.1 = bf16[512,512]{1,0:T(8,128)(2,1)} custom-call(s32[1]{0:T(128)} %bitcast.place, bf16[512,512]{1,0:T(8,128)(2,1)} %get-tuple-element.8.q, f32[4,128]{1,0:T(4,128)} %bias_c.1, f32[4,128]{1,0:T(4,128)} %bias_p.1, bf16[1536,512]{1,0:T(8,128)(2,1)} %fusion.6.rel, bf16[512,512]{1,0:T(8,128)(2,1)} %copy-done.7, bf16[512,512]{1,0:T(8,128)(2,1)} %copy-done.8, ...), custom_call_target="tpu_custom_call" | custom-call | flops 2415919104 | bytes 4718592 | tf_op jit(solution)/shard_map/attend/pallas_call | solution.py:143
  109.2 2.3 %convolution_convert_fusion = bf16[512,2048]{1,0:T(8,128)(2,1)S(1)} fusion(bf16[512,512]{1,0:T(8,128)(2,1)} %attend.1, bf16[512,2048]{1,0:T(8,128)(2,1)S(1)} %copy-done), kind=kOutput, calls=%fused_computation.9 | convolution fusion | flops 1074790400 | bytes 4718592 | tf_op jit(solution)/shard_map/dot_general | solution.py:184
  111.5 1.3 copy-done.1
  112.9 1.2 constant_dynamic-slice_fusion.2
  114.0 1.5 collective-permute-start.9
  115.6 1.9 %collective-permute-start.7 = (bf16[512,512]{1,0:T(8,128)(2,1)}, bf16[512,512]{1,0:T(8,128)(2,1)}, u32[]{:S(2)}, u32[]{:S(2)}) collective-permute-start(bf16[512,512]{1,0:T(8,128)(2,1)} %get-tuple-element.13), channel_id=1, source_target_pairs={{0,1},{1,0},{2,3},{3,2},{4,5},{5,4},{6,7},{7,6},{8,9},{9,8},{10,11... | collective-permute-start | bytes 1572872 | tf_op jit(solution)/shard_map/ppermute | solution.py:168
  117.5 22.2 %collective-permute-done.9 = bf16[512,512]{1,0:T(8,128)(2,1)S(1)} collective-permute-done((bf16[512,512]{1,0:T(8,128)(2,1)}, bf16[512,512]{1,0:T(8,128)(2,1)S(1)}, u32[]{:S(2)}, u32[]{:S(2)}) %collective-permute-start.9) | collective-permute-done | bytes 524320 | tf_op jit(solution)/shard_map/ppermute | solution.py:168
  139.7 9.0 %collective-permute-done.8 = bf16[512,512]{1,0:T(8,128)(2,1)} collective-permute-done((bf16[512,512]{1,0:T(8,128)(2,1)}, bf16[512,512]{1,0:T(8,128)(2,1)}, u32[]{:S(2)}, u32[]{:S(2)}) %collective-permute-start.8) | collective-permute-done | bytes 524320 | tf_op jit(solution)/shard_map/ppermute | solution.py:168
  148.7 1.8 %fusion.10 = (f32[512]{0:T(512)S(1)}, f32[512,512]{1,0:T(8,128)S(1)}) fusion(bf16[512,512]{1,0:T(8,128)(2,1)S(1)} %collective-permute-done.9, bf16[512,512]{1,0:T(8,128)(2,1)} %collective-permute-done.8, bf16[512,512]{1,0:T(8,128)(2,1)} %collective-permute-done.7, bf16[512,2048]{1,0:T(8,128)(2,1)} %copy-done.1, s32[]{:T(128)S(6)} %select_n.12, ...), kind=kLoop, calls=%fused_computation.24 | loop fusion | flops 2620928 | bytes 3672068 | tf_op jit(solution)/shard_map/reduce_sum | solution.py:192
  150.5 0.3 multiply_reduce_fusion
  150.8 1.7 %collective-permute-start.12 = (f32[2,512]{1,0:T(2,128)S(1)}, f32[2,512]{1,0:T(2,128)S(1)}, u32[]{:S(2)}, u32[]{:S(2)}) collective-permute-start(f32[2,512]{1,0:T(2,128)S(1)} %pad_maximum_fusion), channel_id=1, source_target_pairs={{0,3},{1,2},{2,1},{3,0},{4,7},{5,6},{6,5},{7,4},{8,11},{9,10},{10,... | collective-permute-start | bytes 12296 | tf_op jit(solution)/shard_map/ppermute | solution.py:168
  152.4 4.3 %collective-permute-start.11 = (f32[2,512]{1,0:T(2,128)S(1)}, f32[2,512]{1,0:T(2,128)S(1)}, u32[]{:S(2)}, u32[]{:S(2)}) collective-permute-start(f32[2,512]{1,0:T(2,128)S(1)} %pad_maximum_fusion), channel_id=1, source_target_pairs={{0,2},{1,3},{2,0},{3,1},{4,6},{5,7},{6,4},{7,5},{8,10},{9,11},{10,... | collective-permute-start | bytes 12296 | tf_op jit(solution)/shard_map/ppermute | solution.py:168
  156.7 1.6 collective-permute-done.11
  158.3 2.0 %collective-permute-done.10 = f32[2,512]{1,0:T(2,128)S(1)} collective-permute-done((f32[2,512]{1,0:T(2,128)S(1)}, f32[2,512]{1,0:T(2,128)S(1)}, u32[]{:S(2)}, u32[]{:S(2)}) %collective-permute-start.10) | collective-permute-done | bytes 4128 | tf_op jit(solution)/shard_map/ppermute | solution.py:168
  160.3 1.0 add_convert_fusion
  (30 shorter events, 0.1 us)
Async XLA Ops:
  0.0 109.2 %copy-start = (bf16[512,2048]{1,0:T(8,128)(2,1)S(1)}, bf16[512,2048]{1,0:T(8,128)(2,1)}, u32[]{:S(2)}) copy-start(bf16[512,2048]{1,0:T(8,128)(2,1)} %param.15) | copy-start | bytes 6291460
  0.0 28.5 %collective-permute-start = (bf16[512,512]{1,0:T(8,128)(2,1)}, bf16[512,512]{1,0:T(8,128)(2,1)S(1)}, u32[]{:S(2)}, u32[]{:S(2)}) collective-permute-start(bf16[512,512]{1,0:T(8,128)(2,1)} %refs_0_.1), channel_id=1, source_target_pairs={{0,1},{1,0},{2,3},{3,2},{4,5},{5,4},{6,7},{7,6},{8,9},{9,8},{10,11... | collective-permute-start | bytes 1572872 | tf_op jit(solution)/shard_map/ppermute | solution.py:168
  0.5 37.7 %collective-permute-start.1 = (bf16[512,512]{1,0:T(8,128)(2,1)}, bf16[512,512]{1,0:T(8,128)(2,1)S(1)}, u32[]{:S(2)}, u32[]{:S(2)}) collective-permute-start(bf16[512,512]{1,0:T(8,128)(2,1)} %refs_0_.1), channel_id=1, source_target_pairs={{0,2},{1,3},{2,0},{3,1},{4,6},{5,7},{6,4},{7,5},{8,10},{9,11},{10,... | collective-permute-start | bytes 1572872 | tf_op jit(solution)/shard_map/ppermute | solution.py:168
  3.0 45.9 %collective-permute-start.2 = (bf16[512,512]{1,0:T(8,128)(2,1)}, bf16[512,512]{1,0:T(8,128)(2,1)}, u32[]{:S(2)}, u32[]{:S(2)}) collective-permute-start(bf16[512,512]{1,0:T(8,128)(2,1)} %refs_0_.1), channel_id=1, source_target_pairs={{0,3},{1,2},{2,1},{3,0},{4,7},{5,6},{6,5},{7,4},{8,11},{9,10},{10,... | collective-permute-start | bytes 1572872 | tf_op jit(solution)/shard_map/ppermute | solution.py:168
  28.5 20.5 %copy-start.5 = (bf16[512,512]{1,0:T(8,128)(2,1)}, bf16[512,512]{1,0:T(8,128)(2,1)S(1)}, u32[]{:S(2)}) copy-start(bf16[512,512]{1,0:T(8,128)(2,1)S(1)} %collective-permute-done.refs_1_) | copy-start | bytes 1572868
  38.1 10.8 %copy-start.6 = (bf16[512,512]{1,0:T(8,128)(2,1)}, bf16[512,512]{1,0:T(8,128)(2,1)S(1)}, u32[]{:S(2)}) copy-start(bf16[512,512]{1,0:T(8,128)(2,1)S(1)} %collective-permute-done.1.refs_2_) | copy-start | bytes 1572868
  57.5 17.8 %collective-permute-start.3 = (bf16[512,512]{1,0:T(8,128)(2,1)}, bf16[512,512]{1,0:T(8,128)(2,1)S(1)}, u32[]{:S(2)}, u32[]{:S(2)}) collective-permute-start(bf16[512,512]{1,0:T(8,128)(2,1)} %get-tuple-element.9.refs_2_), channel_id=1, source_target_pairs={{0,8},{4,12},{8,16},{12,20},{16,24},{20,28},{1,9},{5,13},{9,17},{1... | collective-permute-start | bytes 1572872 | tf_op jit(solution)/shard_map/ppermute | solution.py:171
  60.9 21.2 %collective-permute-start.4 = (bf16[512,512]{1,0:T(8,128)(2,1)}, bf16[512,512]{1,0:T(8,128)(2,1)S(1)}, u32[]{:S(2)}, u32[]{:S(2)}) collective-permute-start(bf16[512,512]{1,0:T(8,128)(2,1)} %get-tuple-element.9.refs_2_), channel_id=1, source_target_pairs={{0,4},{4,8},{8,12},{12,16},{16,20},{20,24},{24,28},{1,5},{5,9},{9,... | collective-permute-start | bytes 1572872 | tf_op jit(solution)/shard_map/ppermute | solution.py:171
  62.8 23.8 %collective-permute-start.5 = (bf16[512,512]{1,0:T(8,128)(2,1)}, bf16[512,512]{1,0:T(8,128)(2,1)}, u32[]{:S(2)}, u32[]{:S(2)}) collective-permute-start(bf16[512,512]{1,0:T(8,128)(2,1)} %get-tuple-element.10.refs_5_), channel_id=1, source_target_pairs={{0,8},{4,12},{8,16},{12,20},{16,24},{20,28},{1,9},{5,13},{9,17},{1... | collective-permute-start | bytes 1572872 | tf_op jit(solution)/shard_map/ppermute | solution.py:171
  64.7 30.9 %collective-permute-start.6 = (bf16[512,512]{1,0:T(8,128)(2,1)}, bf16[512,512]{1,0:T(8,128)(2,1)}, u32[]{:S(2)}, u32[]{:S(2)}) collective-permute-start(bf16[512,512]{1,0:T(8,128)(2,1)} %get-tuple-element.10.refs_5_), channel_id=1, source_target_pairs={{0,4},{4,8},{8,12},{12,16},{16,20},{20,24},{24,28},{1,5},{5,9},{9,... | collective-permute-start | bytes 1572872 | tf_op jit(solution)/shard_map/ppermute | solution.py:171
  75.3 20.4 %copy-start.7 = (bf16[512,512]{1,0:T(8,128)(2,1)}, bf16[512,512]{1,0:T(8,128)(2,1)S(1)}, u32[]{:S(2)}) copy-start(bf16[512,512]{1,0:T(8,128)(2,1)S(1)} %collective-permute-done.3.refs_0_) | copy-start | bytes 1572868
  82.1 13.6 %copy-start.8 = (bf16[512,512]{1,0:T(8,128)(2,1)}, bf16[512,512]{1,0:T(8,128)(2,1)S(1)}, u32[]{:S(2)}) copy-start(bf16[512,512]{1,0:T(8,128)(2,1)S(1)} %collective-permute-done.4.refs_1_) | copy-start | bytes 1572868
  111.5 1.3 copy-start.1
  112.9 35.8 %copy-start.2 = (bf16[512,512]{1,0:T(8,128)(2,1)S(1)}, bf16[512,512]{1,0:T(8,128)(2,1)}, u32[]{:S(2)}) copy-start(bf16[512,512]{1,0:T(8,128)(2,1)} %refs_0_.1) | copy-start | bytes 1572868
  114.0 46.3 %copy-start.3 = (f32[512]{0:T(512)S(1)}, f32[512]{0:T(512)}, u32[]{:S(2)}) copy-start(f32[512]{0:T(512)} %param.19) | copy-start | bytes 6148
  114.0 46.3 %copy-start.4 = (f32[512]{0:T(512)S(1)}, f32[512]{0:T(512)}, u32[]{:S(2)}) copy-start(f32[512]{0:T(512)} %param.18) | copy-start | bytes 6148
  114.0 25.7 %collective-permute-start.9 = (bf16[512,512]{1,0:T(8,128)(2,1)}, bf16[512,512]{1,0:T(8,128)(2,1)S(1)}, u32[]{:S(2)}, u32[]{:S(2)}) collective-permute-start(bf16[512,512]{1,0:T(8,128)(2,1)} %get-tuple-element.14), channel_id=1, source_target_pairs={{0,3},{1,2},{2,1},{3,0},{4,7},{5,6},{6,5},{7,4},{8,11},{9,10},{10,... | collective-permute-start | bytes 1572872 | tf_op jit(solution)/shard_map/ppermute | solution.py:168
  115.6 33.1 %collective-permute-start.8 = (bf16[512,512]{1,0:T(8,128)(2,1)}, bf16[512,512]{1,0:T(8,128)(2,1)}, u32[]{:S(2)}, u32[]{:S(2)}) collective-permute-start(bf16[512,512]{1,0:T(8,128)(2,1)} %get-tuple-element.15), channel_id=1, source_target_pairs={{0,2},{1,3},{2,0},{3,1},{4,6},{5,7},{6,4},{7,5},{8,10},{9,11},{10,... | collective-permute-start | bytes 1572872 | tf_op jit(solution)/shard_map/ppermute | solution.py:168
  115.6 33.1 %collective-permute-start.7 = (bf16[512,512]{1,0:T(8,128)(2,1)}, bf16[512,512]{1,0:T(8,128)(2,1)}, u32[]{:S(2)}, u32[]{:S(2)}) collective-permute-start(bf16[512,512]{1,0:T(8,128)(2,1)} %get-tuple-element.13), channel_id=1, source_target_pairs={{0,1},{1,0},{2,3},{3,2},{4,5},{5,4},{6,7},{7,6},{8,9},{9,8},{10,11... | collective-permute-start | bytes 1572872 | tf_op jit(solution)/shard_map/ppermute | solution.py:168
  150.8 5.9 %collective-permute-start.12 = (f32[2,512]{1,0:T(2,128)S(1)}, f32[2,512]{1,0:T(2,128)S(1)}, u32[]{:S(2)}, u32[]{:S(2)}) collective-permute-start(f32[2,512]{1,0:T(2,128)S(1)} %pad_maximum_fusion), channel_id=1, source_target_pairs={{0,3},{1,2},{2,1},{3,0},{4,7},{5,6},{6,5},{7,4},{8,11},{9,10},{10,... | collective-permute-start | bytes 12296 | tf_op jit(solution)/shard_map/ppermute | solution.py:168
  152.4 5.9 %collective-permute-start.11 = (f32[2,512]{1,0:T(2,128)S(1)}, f32[2,512]{1,0:T(2,128)S(1)}, u32[]{:S(2)}, u32[]{:S(2)}) collective-permute-start(f32[2,512]{1,0:T(2,128)S(1)} %pad_maximum_fusion), channel_id=1, source_target_pairs={{0,2},{1,3},{2,0},{3,1},{4,6},{5,7},{6,4},{7,5},{8,10},{9,11},{10,... | collective-permute-start | bytes 12296 | tf_op jit(solution)/shard_map/ppermute | solution.py:168
  156.7 3.6 %collective-permute-start.10 = (f32[2,512]{1,0:T(2,128)S(1)}, f32[2,512]{1,0:T(2,128)S(1)}, u32[]{:S(2)}, u32[]{:S(2)}) collective-permute-start(f32[2,512]{1,0:T(2,128)S(1)} %pad_maximum_fusion), channel_id=1, source_target_pairs={{0,1},{1,0},{2,3},{3,2},{4,5},{5,4},{6,7},{7,6},{8,9},{9,8},{10,11... | collective-permute-start | bytes 12296 | tf_op jit(solution)/shard_map/ppermute | solution.py:168

commit v2 on v0

v2 whole, which is shorter than its diff:
```python
import functools

import jax
import jax.numpy as jnp
from jax import lax
from jax.experimental import pallas as pl
from jax.experimental.pallas import tpu as pltpu
from jax.sharding import PartitionSpec as P

TILE = 128
ROWS = 256
HP = 2
VMEM = pltpu.CompilerParams(vmem_limit_bytes=16 * 2**20)
NT = (((1,), (1,)), ((), ()))
LOW = -1e30


def angles(distance, width):
    half = width // 2
    freq = jnp.exp(-jnp.log(10000.0) * jnp.arange(half).astype(jnp.float32) / half)
    angle = distance.astype(jnp.float32)[:, None] * freq[None, :]
    return jnp.sin(angle), jnp.cos(angle)


def relative_kernel(far_sin, far_cos, near_sin, near_cos, weight, out):
    block = pl.program_id(0)
    fs = far_sin[pl.ds(block, 1), :]
    fc = far_cos[pl.ds(block, 1), :]
    ns = near_sin[...]
    nc = near_cos[...]
    sin = (fs * nc + fc * ns).astype(jnp.bfloat16)
    cos = (fc * nc - fs * ns).astype(jnp.bfloat16)
    emb = jnp.concatenate([sin, cos], 1)
    out[...] = jnp.dot(emb, weight[...], preferred_element_type=jnp.float32).astype(jnp.bfloat16)


def relative(span, w_pos):
    model_width, width = w_pos.shape
    blocks = span // TILE
    far_sin, far_cos = angles(span - TILE - TILE * jnp.arange(blocks), model_width)
    near_sin, near_cos = angles(TILE - 1 - jnp.arange(TILE), model_width)
    whole = lambda a: pl.BlockSpec(a.shape, lambda b: (0, 0))
    return pl.pallas_call(
        relative_kernel,
        grid=(blocks,),
        in_specs=[whole(a) for a in (far_sin, far_cos, near_sin, near_cos, w_pos)],
        out_specs=pl.BlockSpec((TILE, width), lambda b: (b, 0)),
        out_shape=jax.ShapeDtypeStruct((span, width), jnp.bfloat16),
        compiler_params=VMEM,
        cost_estimate=pl.CostEstimate(
            flops=2 * span * model_width * width, transcendentals=0, bytes_accessed=4 * 2**20
        ),
        name="relative",
    )(far_sin, far_cos, near_sin, near_cos, w_pos)


def project_kernel(rank, own, one, two, near, relay, w_q, w_k, w_v, query, pairs, steps):
    block = own.shape[1]
    hidden = [own[...], one[...], two[...], near[...] + relay[...]]
    cols = query.shape[1]
    for weight, out in (
        (w_k, pairs.at[:, :cols]),
        (w_v, pairs.at[:, cols:]),
        (w_q, query),
    ):
        total = None
        for k, rows in enumerate(hidden):
            piece = weight[pl.ds(pl.multiple_of((rank[0] ^ k) * block, block), block), :]
            value = jnp.dot(rows, piece, preferred_element_type=jnp.float32)
            total = value if total is None else total + value
        out[...] = total.astype(jnp.bfloat16)


def project(rank, hidden, weights, steps=2):
    rows, block = hidden[0].shape
    depth, width = weights[0].shape
    cols = width // steps
    out_specs = [pl.BlockSpec((rows, cols), lambda n, o: (0, n)) for _ in range(3)]
    grid_spec = pltpu.PrefetchScalarGridSpec(
        num_scalar_prefetch=1,
        grid=(steps,),
        in_specs=[pl.BlockSpec((rows, block), lambda n, o: (0, 0)) for _ in hidden]
        + [pl.BlockSpec((depth, cols), lambda n, o: (0, n)) for _ in weights],
        out_specs=[
            pl.BlockSpec((rows, cols), lambda n, o: (0, n)),
            pl.BlockSpec((rows, 2 * cols), lambda n, o: (0, n)),
        ],
    )
    return pl.pallas_call(
        functools.partial(project_kernel, steps=steps),
        grid_spec=grid_spec,
        out_shape=[
            jax.ShapeDtypeStruct((rows, width), jnp.bfloat16),
            jax.ShapeDtypeStruct((rows, 2 * width), jnp.bfloat16),
        ],
        compiler_params=VMEM,
        cost_estimate=pl.CostEstimate(
            flops=6 * rows * depth * width, transcendentals=0, bytes_accessed=6 * depth * width
        ),
        name="project",
    )(rank, *hidden, *weights)


def attend_kernel(
    place, bias_c, bias_p, rel, *refs, first, count, pieces, seg, final, head_dim
):
    queries = refs[:count]
    pairs = refs[count : count + len(pieces)]
    refs = refs[count + len(pieces) :]
    wide = HP * head_dim
    span = 3 * seg
    log2 = 1.4426950408889634 / head_dim**0.5
    lane = lax.broadcasted_iota(jnp.int32, (ROWS, head_dim), 1)
    for local in range(HP):
        head = pl.program_id(0) * HP + local
        mine = slice(local * head_dim, (local + 1) * head_dim)
        theirs = slice(wide + local * head_dim, wide + (local + 1) * head_dim)
        content_bias = bias_c[pl.ds(head, 1), :]
        pos_bias = bias_p[pl.ds(head, 1), :]
        for block, q in enumerate(queries):
            here = slice(block * ROWS, (block + 1) * ROWS)
            top = first + block * ROWS
            end = 2 * seg + top + ROWS
            rows = q[:, mine].astype(jnp.float32)
            content_q = (rows + content_bias).astype(jnp.bfloat16)
            pos_q = (rows + pos_bias).astype(jnp.bfloat16)
            scores = []
            used = []
            for part, start in enumerate(pieces):
                width = min(pairs[part].shape[0], end - start)
                if width <= 0:
                    continue
                edge = start + width == end
                window = width if edge else width + ROWS
                low = seg - ROWS - top + start
                position = lax.dot_general(
                    pos_q, rel[low : low + window, mine], NT, preferred_element_type=jnp.float32
                )
                position = pltpu.roll(position, window - (ROWS - 1), 1, stride=1, stride_axis=0)
                content = lax.dot_general(
                    content_q, pairs[part][:width, mine], NT, preferred_element_type=jnp.float32
                )
                score = content + position[:, :width]
                back = 2 - start // seg
                if back > 0:
                    score = score + jnp.where(place[0] >= back, jnp.float32(0.0), jnp.float32(LOW))
                if edge:
                    row = lax.broadcasted_iota(jnp.int32, (ROWS, ROWS), 0)
                    col = lax.broadcasted_iota(jnp.int32, (ROWS, ROWS), 1)
                    tail = jnp.where(col <= row, score[:, width - ROWS :], jnp.float32(LOW))
                    score = tail if width == ROWS else jnp.concatenate([score[:, :-ROWS], tail], 1)
                scores.append(score)
                used.append((part, width))
            score = jnp.concatenate(scores, 1)
            peak = jnp.max(score, axis=1, keepdims=True)
            if final:
                before = refs[0][here, mine]
                old_peak = before[:, :1]
                old_total = before[:, head_dim // 2 : head_dim // 2 + 1]
                peak = jnp.maximum(peak, old_peak)
                keep = jnp.exp2((old_peak - peak) * log2)
            weight = jnp.exp2((score - peak) * log2)
            total = jnp.sum(weight, axis=1, keepdims=True)
            if final:
                total = total + old_total * keep
                scale = 1.0 / total
                weight = weight * scale
                result = refs[1][here, mine] * (keep * scale)
            else:
                result = None
            probs = weight.astype(jnp.bfloat16)
            start = 0
            for part, width in used:
                piece = jnp.dot(
                    probs[:, start : start + width],
                    pairs[part][:width, theirs],
                    preferred_element_type=jnp.float32,
                )
                result = piece if result is None else result + piece
                start += width
            if final:
                refs[2][here, mine] = result.astype(jnp.bfloat16)
            else:
                refs[0][here, mine] = jnp.where(lane < head_dim // 2, peak, total)
                refs[1][here, mine] = result


def attend(place, queries, bias_c, bias_p, rel, pairs, pieces, first, seg, before=()):
    heads, head_dim = bias_c.shape
    rows = len(queries) * ROWS
    wide = HP * head_dim
    final = len(before) > 0
    column = lambda n: pl.BlockSpec((n, wide), lambda h, p: (0, h))
    whole = pl.BlockSpec((heads, head_dim), lambda h, p: (0, 0))
    shape = lambda kind: jax.ShapeDtypeStruct((rows, heads * head_dim), kind)
    grid_spec = pltpu.PrefetchScalarGridSpec(
        num_scalar_prefetch=1,
        grid=(heads // HP,),
        in_specs=[whole, whole, column(3 * seg)]
        + [column(ROWS) for _ in queries]
        + [pl.BlockSpec((n.shape[0], 2 * wide), lambda h, p: (0, h)) for n in pairs]
        + [pl.BlockSpec((rows, wide), lambda h, p: (first // rows, h)) for _ in before],
        out_specs=column(rows) if final else [column(rows), column(rows)],
    )
    size = sum(k.shape[0] for k in pairs)
    return pl.pallas_call(
        functools.partial(
            attend_kernel,
            first=first,
            count=len(queries),
            pieces=pieces,
            seg=seg,
            final=final,
            head_dim=head_dim,
        ),
        grid_spec=grid_spec,
        out_shape=shape(jnp.bfloat16) if final else [shape(jnp.float32), shape(jnp.float32)],
        compiler_params=VMEM,
        cost_estimate=pl.CostEstimate(
            flops=16 * rows * size * heads * head_dim,
            transcendentals=rows * size * heads,
            bytes_accessed=6 * size * heads * head_dim,
        ),
        name="finish" if final else "begin",
    )(place, bias_c, bias_p, rel, *queries, *pairs, *before)


def output_kernel(where, own, other, w_mine, w_send, got, swapped, mine, send):
    first = jnp.where(where[2] == 0, got[...], swapped[...])
    second = jnp.where(where[2] == 0, swapped[...], got[...])

    def both(a, b):
        x = jnp.dot(own[...], a, preferred_element_type=jnp.float32).astype(jnp.bfloat16)
        y = jnp.dot(other[...], b, preferred_element_type=jnp.float32).astype(jnp.bfloat16)
        return x.astype(jnp.float32) + y.astype(jnp.float32)

    send[...] = both(w_send[...], second).astype(jnp.bfloat16)
    mine[...] = both(w_mine[...], first)


def output(where, own, other, w_out, got, swapped):
    rows, depth = own.shape
    block = got.shape[1]
    whole = lambda a: pl.BlockSpec(a.shape, lambda i, o: (0, 0))
    grid_spec = pltpu.PrefetchScalarGridSpec(
        num_scalar_prefetch=1,
        grid=(1,),
        in_specs=[whole(own), whole(other)]
        + [pl.BlockSpec((depth, block), lambda i, o, k=k: (0, o[k])) for k in (0, 1)]
        + [whole(got), whole(swapped)],
        out_specs=[pl.BlockSpec((rows, block), lambda i, o: (0, 0)) for _ in range(2)],
    )
    return pl.pallas_call(
        output_kernel,
        grid_spec=grid_spec,
        out_shape=[
            jax.ShapeDtypeStruct((rows, block), jnp.float32),
            jax.ShapeDtypeStruct((rows, block), jnp.bfloat16),
        ],
        compiler_params=VMEM,
        cost_estimate=pl.CostEstimate(
            flops=8 * rows * depth * block, transcendentals=0, bytes_accessed=10 * depth * block
        ),
        name="output",
    )(where, own, other, w_out, w_out, got, swapped)


def shards(
    hidden_in, w_query, w_key, w_value, w_pos, w_out, bias_content, bias_pos, norm_gain, norm_bias
):
    seg, block = hidden_in.shape
    model_width = w_query.shape[0]
    span = 3 * seg
    tp = lax.axis_size("tp")
    seqs = lax.axis_size("seq")
    assert tp == 4 and seqs % 2 == 0
    place = lax.axis_index("seq").astype(jnp.int32)
    rank = lax.axis_index("tp").astype(jnp.int32)
    core = place % 2
    half = seg // 2

    def across(x, k):
        return lax.ppermute(x, "tp", [(i, i ^ k) for i in range(tp)])

    def later(x, k):
        return lax.ppermute(x, "seq", [(i, i + k) for i in range(seqs - k)])

    def after(x, *others):
        return lax.optimization_barrier((x,) + others)[0]

    rel = relative(span, w_pos)

    halves = [hidden_in[:half], hidden_in[half:]]
    gathered = []
    for h in halves:
        x = after(h, gathered[0][2], rel) if gathered else h
        two = across(x, 2)
        one = across(x, 1)
        near = lax.ppermute(x, "tp", [(1, 2), (2, 1)])
        relay = lax.ppermute(two, "tp", [(1, 0), (2, 3)])
        gathered.append((h, one, two, near, relay))

    foreign = lax.dynamic_slice_in_dim(w_out, (rank ^ 2 ^ core) * block, block, 1)
    foreign = after(foreign, gathered[1][4])
    got = across(foreign, 2)
    swapped = lax.ppermute(got, "seq", [(i, i ^ 1) for i in range(seqs)])

    spot = place.reshape(1)
    query, pairs, early = [], [], []
    for g in gathered:
        q, kv = project(rank.reshape(1), g, (w_query, w_key, w_value))
        query.append(q)
        pairs.append(kv)
        early.append([later(kv, d) for d in (2, 1)])
    state = attend(
        spot, query, bias_content, bias_pos, rel,
        early[0] + pairs,
        (0, seg, 2 * seg, 2 * seg + half), 0, seg,
    )
    where = jnp.stack([rank, rank ^ 1, core])
    summed = []
    for i in range(2):
        attended = attend(
            spot, query[i : i + 1], bias_content, bias_pos, rel,
            early[1],
            (half, seg + half), i * half, seg,
            before=state,
        )
        other = across(attended, 2)
        mine, send = output(where, attended, other, w_out, got, swapped)
        received = across(send, 1)
        summed.append(halves[i].astype(jnp.float32) + mine + received.astype(jnp.float32))
    summed = jnp.concatenate(summed, 0)
    total = jnp.sum(summed, axis=1)
    center = total / block
    centred = summed - center[:, None]
    spread = jnp.sum(centred * centred, axis=1)
    stats = jnp.stack([center, spread])
    stats = [stats] + [across(stats, k) for k in range(1, tp)]
    mean = sum(s[0] for s in stats) / tp
    spread = sum(s[1] + block * (s[0] - mean) ** 2 for s in stats) / model_width
    normed = (summed - mean[:, None]) / jnp.sqrt(spread[:, None] + 1e-05)
    return (normed * norm_gain[None] + norm_bias[None]).astype(jnp.bfloat16)


def solution(mesh):
    in_specs = (
        P("seq", "tp"),
        P(None, "tp"),
        P(None, "tp"),
        P(None, "tp"),
        P(None, "tp"),
        P("tp", None),
        P("tp", None),
        P("tp", None),
        P("tp"),
        P("tp"),
    )
    out_specs = P("seq", "tp")
    return jax.shard_map(shards, mesh=mesh, in_specs=in_specs, out_specs=out_specs, check_vma=False)
```

time: 257 us -> 133 us (0.52)
  local copies, waits for them, and re-layouts: 60.4 us -> 7.25 us
  matrix products: 45.8 us -> 0 us
  other arithmetic: 41.6 us -> 3.98 us
  starting transfers between devices: 9.43 us -> 46.9 us
  Pallas kernels: 0 us -> 32 us
  waiting for transfers between devices: 64.6 us -> 41.9 us
  blocking collectives: 19.6 us -> 0 us
  between operations: 13.6 us -> 0.35 us
    dot_general x8 -> x0, matrix products: 45.8 us -> none  [the longest x1 11.5 us: shards(): jnp.einsum('ihd,jhd->hij', content_q, keys, preferred_element_type=jnp.fl...]
    reduce_scatter x1 -> x0, waiting for transfers between devices: 45.6 us -> none  [shards(): lax.psum_scatter(partial_out.astype(jnp.bfloat16), 'tp', scatter_dimensio...]
    ppermute x4 -> x21, waiting for transfers between devices: 0.01 us -> 41.9 us  [the longest x12 35.5 us: across(): return lax.ppermute(x, 'tp', [(i, i ^ k) for i in range(tp)])]
    ppermute x4 -> x21, starting transfers between devices: 9.39 us -> 46.9 us  [the longest x12 21.5 us: across(): return lax.ppermute(x, 'tp', [(i, i ^ k) for i in range(tp)])]
    pallas_call x0 -> x8, Pallas kernels: none -> 32 us  [the longest x3 16 us: attend(): pl.pallas_call(functools.partial(attend_kernel, first=first, count=len(qu...]
    another operation x1 -> x2, other arithmetic: 23.2 us -> 0.09 us  [the longest x1 0.08 us: shards(): where = jnp.stack([rank, rank ^ 1, core])]
    reshape x3 -> x0, local copies, waits for them, and re-layouts: 19.8 us -> none  [the longest x1 15 us: shift_rows(): flat = padded.reshape(heads, seg * (span + 1))]
    psum x2 -> x0, blocking collectives: 19.6 us -> none  [the longest x1 9.92 us: shards(): spread = lax.psum(jnp.sum(centred * centred, axis=1), 'tp') / model_width]
  transfers between devices with their start and end apart: 6 -> 21, of which waited for: 2 -> 11; matrix products, arithmetic and copies ran while one was open for 47% -> 2% of each run, Pallas kernels for 0% -> 24%
where the time goes in v2:
time: 133 us; the launch traced here: 132 us
  starting transfers between devices  46.9 us (35%)
  waiting for transfers between devices  41.9 us (32%)
  Pallas kernels  32 us (24%)
  local copies, waits for them, and re-layouts  7.25 us (5%)
  other arithmetic  3.98 us (3%)
    ppermute x12, waiting for transfers between devices, across(): return lax.ppermute(x, 'tp', [(i, i ^ k) for i in range(tp)])  35.5 us
    ppermute x12, starting transfers between devices, across(): return lax.ppermute(x, 'tp', [(i, i ^ k) for i in range(tp)])  21.5 us
    pallas_call x3, Pallas kernels, attend(): pl.pallas_call(functools.partial(attend_kernel, first=first, count=len(qu...  16 us
    ppermute x2, starting transfers between devices, shards(): relay = lax.ppermute(two, 'tp', [(1, 0), (2, 3)])  12 us
    ppermute x4, starting transfers between devices, later(): return lax.ppermute(x, 'seq', [(i, i + k) for i in range(seqs - k)])  9.56 us
    ppermute x4, waiting for transfers between devices, later(): return lax.ppermute(x, 'seq', [(i, i + k) for i in range(seqs - k)])  6.12 us
    pallas_call x2, Pallas kernels, project(): pl.pallas_call(functools.partial(project_kernel, steps=steps), grid_spec=...  5.99 us
    unnamed x30, local copies, waits for them, and re-layouts  5.98 us
  transfers between devices with their start and end apart: 21, of which 11 were waited for; matrix products, arithmetic and copies ran while one was open for 2% of the time, Pallas kernels for 24%

profile of v2, /device:TPU:12, one launch (start us, length us, event | category | flops | bytes accessed | tf_op | source)
XLA Modules:
  0.0 132.5 jit_solution(2570114452577023076)
XLA Ops:
  1.2 2.7 %collective-permute-start.1 = (bf16[256,512]{1,0:T(8,128)(2,1)S(1)}, bf16[256,512]{1,0:T(8,128)(2,1)S(1)}, u32[]{:S(2)}, u32[]{:S(2)}) collective-permute-start(bf16[256,512]{1,0:T(8,128)(2,1)S(1)} %get-tuple-element.31.own), channel_id=1, source_target_pairs={{0,2},{1,3},{2,0},{3,1},{4,6},{5,7},{6,4},{7,5},{8,10},{9,11},{10,... | collective-permute-start | bytes 786440 | tf_op jit(solution)/shard_map/ppermute | solution.py:283
  4.2 1.9 %multiply_cosine_fusion = (f32[128,1024]{1,0:T(8,128)S(1)}, f32[128,1024]{1,0:T(8,128)S(1)}) fusion(f32[1024]{0:T(1024)S(1)} %multiply_exponential_fusion, f32[128]{0:T(128)S(1)} %subtract_convert_fusion), kind=kLoop, calls=%fused_computation.3 | loop fusion | flops 131072 | bytes 1053184 | tf_op jit(solution)/shard_map/cos | solution.py:22
  6.1 5.5 %relative.1.rel = bf16[1536,512]{1,0:T(8,128)(2,1)S(1)} custom-call(f32[12,1024]{1,0:T(8,128)S(1)} %get-tuple-element.38.far_sin, f32[12,1024]{1,0:T(8,128)S(1)} %get-tuple-element.37.far_cos, f32[128,1024]{1,0:T(8,128)S(1)} %get-tuple-element.36.near_sin, f32[128,1024]{1,0:T(8,128)S(1)} %get-tuple-element.35.near_cos, bf16[2048,512]{1,0:T(8,128)(2,1)S(1)} %copy-done.11), custom_call_target="tpu_custom_call" | custom-call | flops 3221225472 | bytes 4194304 | tf_op jit(solution)/shard_map/relative/pallas_call | solution.py:43
  12.8 2.1 %collective-permute-done.1.two = bf16[256,512]{1,0:T(8,128)(2,1)S(1)} collective-permute-done((bf16[256,512]{1,0:T(8,128)(2,1)S(1)}, bf16[256,512]{1,0:T(8,128)(2,1)S(1)}, u32[]{:S(2)}, u32[]{:S(2)}) %collective-permute-start.1) | collective-permute-done | bytes 262176 | tf_op jit(solution)/shard_map/ppermute | solution.py:283
  14.9 3.4 %collective-permute-start.5 = (bf16[256,512]{1,0:T(8,128)(2,1)S(1)}, bf16[256,512]{1,0:T(8,128)(2,1)S(1)}, u32[]{:S(2)}, u32[]{:S(2)}) collective-permute-start(bf16[256,512]{1,0:T(8,128)(2,1)S(1)} %get-tuple-element.18.own), channel_id=1, source_target_pairs={{0,2},{1,3},{2,0},{3,1},{4,6},{5,7},{6,4},{7,5},{8,10},{9,11},{10,... | collective-permute-start | bytes 786440 | tf_op jit(solution)/shard_map/ppermute | solution.py:283
  18.3 1.9 %collective-permute-start.2 = (bf16[256,512]{1,0:T(8,128)(2,1)S(1)}, bf16[256,512]{1,0:T(8,128)(2,1)S(1)}, u32[]{:S(2)}, u32[]{:S(2)}) collective-permute-start(bf16[256,512]{1,0:T(8,128)(2,1)S(1)} %get-tuple-element.31.own), channel_id=1, source_target_pairs={{1,2},{2,1},{5,6},{6,5},{9,10},{10,9},{13,14},{14,13},{17,18},{18,... | collective-permute-start | bytes 786440 | tf_op jit(solution)/shard_map/ppermute | solution.py:299
  20.3 4.6 %collective-permute-start.3 = (bf16[256,512]{1,0:T(8,128)(2,1)S(1)}, bf16[256,512]{1,0:T(8,128)(2,1)}, u32[]{:S(2)}, u32[]{:S(2)}) collective-permute-start(bf16[256,512]{1,0:T(8,128)(2,1)S(1)} %collective-permute-done.1.two), channel_id=1, source_target_pairs={{1,0},{2,3},{5,4},{6,7},{9,8},{10,11},{13,12},{14,15},{17,16},{18,... | collective-permute-start | bytes 786440 | tf_op jit(solution)/shard_map/ppermute | solution.py:300
  26.5 7.4 %collective-permute-start.7 = (bf16[256,512]{1,0:T(8,128)(2,1)S(1)}, bf16[256,512]{1,0:T(8,128)(2,1)S(1)}, u32[]{:S(2)}, u32[]{:S(2)}) collective-permute-start(bf16[256,512]{1,0:T(8,128)(2,1)S(1)} %collective-permute-done.5.two), channel_id=1, source_target_pairs={{1,0},{2,3},{5,4},{6,7},{9,8},{10,11},{13,12},{14,15},{17,16},{18,... | collective-permute-start | bytes 786440 | tf_op jit(solution)/shard_map/ppermute | solution.py:300
  34.0 1.9 %collective-permute-start.6 = (bf16[256,512]{1,0:T(8,128)(2,1)S(1)}, bf16[256,512]{1,0:T(8,128)(2,1)S(1)}, u32[]{:S(2)}, u32[]{:S(2)}) collective-permute-start(bf16[256,512]{1,0:T(8,128)(2,1)S(1)} %get-tuple-element.18.own), channel_id=1, source_target_pairs={{1,2},{2,1},{5,6},{6,5},{9,10},{10,9},{13,14},{14,13},{17,18},{18,... | collective-permute-start | bytes 786440 | tf_op jit(solution)/shard_map/ppermute | solution.py:299
  36.3 1.6 %copy-done.1 = bf16[2048,512]{1,0:T(8,128)(2,1)S(1)} copy-done((bf16[2048,512]{1,0:T(8,128)(2,1)S(1)}, bf16[2048,512]{1,0:T(8,128)(2,1)}, u32[]{:S(2)}) %copy-start.1) | copy-done | bytes 2097176
  37.9 1.6 %copy-done.3 = bf16[2048,512]{1,0:T(8,128)(2,1)S(1)} copy-done((bf16[2048,512]{1,0:T(8,128)(2,1)S(1)}, bf16[2048,512]{1,0:T(8,128)(2,1)}, u32[]{:S(2)}) %copy-start.3) | copy-done | bytes 2097176
  41.1 3.5 %project.2 = (bf16[256,512]{1,0:T(8,128)(2,1)S(1)}, bf16[256,1024]{1,0:T(8,128)(2,1)S(1)}) custom-call(s32[1]{0:T(128)} %bitcast.rank, bf16[256,512]{1,0:T(8,128)(2,1)S(1)} %get-tuple-element.31.own, bf16[256,512]{1,0:T(8,128)(2,1)} %collective-permute-done.one, bf16[256,512]{1,0:T(8,128)(2,1)S(1)} %collective-permute-done.1.two, ...), custom_call_target="tpu_custom_call" | custom-call | flops 1610612736 | bytes 6291456 | tf_op jit(solution)/shard_map/project/pallas_call | solution.py:89
  44.5 5.0 %collective-permute-start.13 = (bf16[512,512]{1,0:T(8,128)(2,1)S(1)}, bf16[512,512]{1,0:T(8,128)(2,1)S(1)}, u32[]{:S(2)}, u32[]{:S(2)}) collective-permute-start(bf16[512,512]{1,0:T(8,128)(2,1)S(1)} %constant_dynamic-slice_fusion), channel_id=1, source_target_pairs={{0,2},{1,3},{2,0},{3,1},{4,6},{5,7},{6,4},{7,5},{8,10},{9,11},{10,... | collective-permute-start | bytes 1572872 | tf_op jit(solution)/shard_map/ppermute | solution.py:283
  49.5 2.0 %collective-permute-start.11 = (bf16[256,1024]{1,0:T(8,128)(2,1)S(1)}, bf16[256,1024]{1,0:T(8,128)(2,1)S(1)}, u32[]{:S(2)}, u32[]{:S(2)}) collective-permute-start(bf16[256,1024]{1,0:T(8,128)(2,1)S(1)} %get-tuple-element.21.refs_4_), channel_id=1, source_target_pairs={{0,4},{4,8},{8,12},{12,16},{16,20},{20,24},{24,28},{1,5},{5,9},{9,... | collective-permute-start | bytes 1572872 | tf_op jit(solution)/shard_map/ppermute | solution.py:286
  51.6 3.4 %collective-permute-start.10 = (bf16[256,1024]{1,0:T(8,128)(2,1)S(1)}, bf16[256,1024]{1,0:T(8,128)(2,1)S(1)}, u32[]{:S(2)}, u32[]{:S(2)}) collective-permute-start(bf16[256,1024]{1,0:T(8,128)(2,1)S(1)} %get-tuple-element.21.refs_4_), channel_id=1, source_target_pairs={{0,8},{4,12},{8,16},{12,20},{16,24},{20,28},{1,9},{5,13},{9,17},{1... | collective-permute-start | bytes 1572872 | tf_op jit(solution)/shard_map/ppermute | solution.py:286
  55.0 2.5 %project.3 = (bf16[256,512]{1,0:T(8,128)(2,1)S(1)}, bf16[256,1024]{1,0:T(8,128)(2,1)S(1)}) custom-call(s32[1]{0:T(128)} %bitcast.rank, bf16[256,512]{1,0:T(8,128)(2,1)S(1)} %get-tuple-element.18.own, bf16[256,512]{1,0:T(8,128)(2,1)S(1)} %collective-permute-done.4.one, bf16[256,512]{1,0:T(8,128)(2,1)S(1)} %collective-permute-done.5.two, ...), custom_call_target="tpu_custom_call" | custom-call | flops 1610612736 | bytes 6291456 | tf_op jit(solution)/shard_map/project/pallas_call | solution.py:89
  57.6 2.0 %collective-permute-start.9 = (bf16[256,1024]{1,0:T(8,128)(2,1)S(1)}, bf16[256,1024]{1,0:T(8,128)(2,1)S(1)}, u32[]{:S(2)}, u32[]{:S(2)}) collective-permute-start(bf16[256,1024]{1,0:T(8,128)(2,1)S(1)} %get-tuple-element.19.refs_5_), channel_id=1, source_target_pairs={{0,4},{4,8},{8,12},{12,16},{16,20},{20,24},{24,28},{1,5},{5,9},{9,... | collective-permute-start | bytes 1572872 | tf_op jit(solution)/shard_map/ppermute | solution.py:286
  59.6 2.1 %collective-permute-start.8 = (bf16[256,1024]{1,0:T(8,128)(2,1)S(1)}, bf16[256,1024]{1,0:T(8,128)(2,1)S(1)}, u32[]{:S(2)}, u32[]{:S(2)}) collective-permute-start(bf16[256,1024]{1,0:T(8,128)(2,1)S(1)} %get-tuple-element.19.refs_5_), channel_id=1, source_target_pairs={{0,8},{4,12},{8,16},{12,20},{16,24},{20,28},{1,9},{5,13},{9,17},{1... | collective-permute-start | bytes 1572872 | tf_op jit(solution)/shard_map/ppermute | solution.py:286
  61.7 8.9 %collective-permute-done.13.got = bf16[512,512]{1,0:T(8,128)(2,1)S(1)} collective-permute-done((bf16[512,512]{1,0:T(8,128)(2,1)S(1)}, bf16[512,512]{1,0:T(8,128)(2,1)S(1)}, u32[]{:S(2)}, u32[]{:S(2)}) %collective-permute-start.13) | collective-permute-done | bytes 524320 | tf_op jit(solution)/shard_map/ppermute | solution.py:283
  70.7 6.7 %begin.1 = (f32[512,512]{1,0:T(8,128)S(1)}, f32[512,512]{1,0:T(8,128)S(1)}) custom-call(s32[1]{0:T(128)} %bitcast.3.place, f32[4,128]{1,0:T(4,128)S(1)} %copy-done.9, f32[4,128]{1,0:T(4,128)S(1)} %copy-done.10, bf16[1536,512]{1,0:T(8,128)(2,1)S(1)} %copy-done.8, bf16[256,512]{1,0:T(8,128)(2,1)S(1)} %get-tuple-element.17.refs_0_, ...), custom_call_target="tpu_custom_call" | custom-call | flops 4294967296 | bytes 3145728 | tf_op jit(solution)/shard_map/begin/pallas_call | solution.py:206
  77.4 6.1 %collective-permute-done.9.refs_2_ = bf16[256,1024]{1,0:T(8,128)(2,1)S(1)} collective-permute-done((bf16[256,1024]{1,0:T(8,128)(2,1)S(1)}, bf16[256,1024]{1,0:T(8,128)(2,1)S(1)}, u32[]{:S(2)}, u32[]{:S(2)}) %collective-permute-start.9) | collective-permute-done | bytes 524320 | tf_op jit(solution)/shard_map/ppermute | solution.py:286
  83.5 5.0 %finish.3.own = bf16[256,512]{1,0:T(8,128)(2,1)} custom-call(s32[1]{0:T(128)} %bitcast.3.place, f32[4,128]{1,0:T(4,128)S(1)} %copy-done.9, f32[4,128]{1,0:T(4,128)S(1)} %copy-done.10, bf16[1536,512]{1,0:T(8,128)(2,1)S(1)} %copy-done.8, bf16[256,512]{1,0:T(8,128)(2,1)S(1)} %get-tuple-element.20.refs_1_.refs_0_, ...), custom_call_target="tpu_custom_call" | custom-call | flops 1073741824 | bytes 1572864 | tf_op jit(solution)/shard_map/finish/pallas_call | solution.py:206
  88.6 4.3 %finish.2.own = bf16[256,512]{1,0:T(8,128)(2,1)S(1)} custom-call(s32[1]{0:T(128)} %bitcast.3.place, f32[4,128]{1,0:T(4,128)S(1)} %copy-done.9, f32[4,128]{1,0:T(4,128)S(1)} %copy-done.10, bf16[1536,512]{1,0:T(8,128)(2,1)S(1)} %copy-done.8, bf16[256,512]{1,0:T(8,128)(2,1)S(1)} %get-tuple-element.17.refs_0_, ...), custom_call_target="tpu_custom_call" | custom-call | flops 1073741824 | bytes 1572864 | tf_op jit(solution)/shard_map/finish/pallas_call | solution.py:206
  92.9 2.9 %collective-permute-start.12 = (bf16[256,512]{1,0:T(8,128)(2,1)S(1)}, bf16[256,512]{1,0:T(8,128)(2,1)}, u32[]{:S(2)}, u32[]{:S(2)}) collective-permute-start(bf16[256,512]{1,0:T(8,128)(2,1)S(1)} %finish.2.own), channel_id=1, source_target_pairs={{0,2},{1,3},{2,0},{3,1},{4,6},{5,7},{6,4},{7,5},{8,10},{9,11},{10,... | collective-permute-start | bytes 786440 | tf_op jit(solution)/shard_map/ppermute | solution.py:283
  95.9 9.2 %collective-permute-done.16.other = bf16[256,512]{1,0:T(8,128)(2,1)} collective-permute-done((bf16[256,512]{1,0:T(8,128)(2,1)}, bf16[256,512]{1,0:T(8,128)(2,1)}, u32[]{:S(2)}, u32[]{:S(2)}) %collective-permute-start.16) | collective-permute-done | bytes 262176 | tf_op jit(solution)/shard_map/ppermute | solution.py:283
  105.1 2.3 %output.3 = (f32[256,512]{1,0:T(8,128)S(1)}, bf16[256,512]{1,0:T(8,128)(2,1)S(1)}) custom-call(s32[3]{0:T(128)S(1)} %pad_add_fusion.where, bf16[256,512]{1,0:T(8,128)(2,1)} %finish.3.own, bf16[256,512]{1,0:T(8,128)(2,1)} %collective-permute-done.16.other, bf16[512,2048]{1,0:T(8,128)(2,1)S(1)} %copy-done, bf16[512,2048]{1,0:T(8,128)(2,1)S(1)} %copy-done, ...), custom_call_target="tpu_custom_call" | custom-call | flops 536870912 | bytes 2621440 | tf_op jit(solution)/shard_map/output/pallas_call | solution.py:253
  107.5 3.1 %collective-permute-done.12.other = bf16[256,512]{1,0:T(8,128)(2,1)} collective-permute-done((bf16[256,512]{1,0:T(8,128)(2,1)S(1)}, bf16[256,512]{1,0:T(8,128)(2,1)}, u32[]{:S(2)}, u32[]{:S(2)}) %collective-permute-start.12) | collective-permute-done | bytes 262176 | tf_op jit(solution)/shard_map/ppermute | solution.py:283
  110.6 2.2 %output.2 = (f32[256,512]{1,0:T(8,128)S(1)}, bf16[256,512]{1,0:T(8,128)(2,1)S(1)}) custom-call(s32[3]{0:T(128)S(1)} %pad_add_fusion.where, bf16[256,512]{1,0:T(8,128)(2,1)S(1)} %finish.2.own, bf16[256,512]{1,0:T(8,128)(2,1)} %collective-permute-done.12.other, bf16[512,2048]{1,0:T(8,128)(2,1)S(1)} %copy-done, bf16[512,2048]{1,0:T(8,128)(2,1)S(1)} %copy-done, ...), custom_call_target="tpu_custom_call" | custom-call | flops 536870912 | bytes 2621440 | tf_op jit(solution)/shard_map/output/pallas_call | solution.py:253
  112.8 2.7 %collective-permute-start.15 = (bf16[256,512]{1,0:T(8,128)(2,1)S(1)}, bf16[256,512]{1,0:T(8,128)(2,1)S(1)}, u32[]{:S(2)}, u32[]{:S(2)}) collective-permute-start(bf16[256,512]{1,0:T(8,128)(2,1)S(1)} %get-tuple-element.26), channel_id=1, source_target_pairs={{0,1},{1,0},{2,3},{3,2},{4,5},{5,4},{6,7},{7,6},{8,9},{9,8},{10,11... | collective-permute-start | bytes 786440 | tf_op jit(solution)/shard_map/ppermute | solution.py:283
  116.5 6.0 %collective-permute-done.15 = bf16[256,512]{1,0:T(8,128)(2,1)S(1)} collective-permute-done((bf16[256,512]{1,0:T(8,128)(2,1)S(1)}, bf16[256,512]{1,0:T(8,128)(2,1)S(1)}, u32[]{:S(2)}, u32[]{:S(2)}) %collective-permute-start.15) | collective-permute-done | bytes 262176 | tf_op jit(solution)/shard_map/ppermute | solution.py:283
  124.4 3.3 %collective-permute-start.19 = (f32[2,512]{1,0:T(2,128)S(1)}, f32[2,512]{1,0:T(2,128)S(1)}, u32[]{:S(2)}, u32[]{:S(2)}) collective-permute-start(f32[2,512]{1,0:T(2,128)S(1)} %pad_maximum_fusion.1), channel_id=1, source_target_pairs={{0,2},{1,3},{2,0},{3,1},{4,6},{5,7},{6,4},{7,5},{8,10},{9,11},{10,... | collective-permute-start | bytes 12296 | tf_op jit(solution)/shard_map/ppermute | solution.py:283
  129.4 2.0 %collective-permute-done.18 = f32[2,512]{1,0:T(2,128)S(1)} collective-permute-done((f32[2,512]{1,0:T(2,128)S(1)}, f32[2,512]{1,0:T(2,128)S(1)}, u32[]{:S(2)}, u32[]{:S(2)}) %collective-permute-start.18) | collective-permute-done | bytes 4128 | tf_op jit(solution)/shard_map/ppermute | solution.py:283
  (66 shorter events, 12.2 us)
Async XLA Ops:
  0.0 6.1 %copy-start.11 = (bf16[2048,512]{1,0:T(8,128)(2,1)S(1)}, bf16[2048,512]{1,0:T(8,128)(2,1)}, u32[]{:S(2)}) copy-start(bf16[2048,512]{1,0:T(8,128)(2,1)} %weight.1) | copy-start | bytes 6291460
  1.2 13.7 %collective-permute-start.1 = (bf16[256,512]{1,0:T(8,128)(2,1)S(1)}, bf16[256,512]{1,0:T(8,128)(2,1)S(1)}, u32[]{:S(2)}, u32[]{:S(2)}) collective-permute-start(bf16[256,512]{1,0:T(8,128)(2,1)S(1)} %get-tuple-element.31.own), channel_id=1, source_target_pairs={{0,2},{1,3},{2,0},{3,1},{4,6},{5,7},{6,4},{7,5},{8,10},{9,11},{10,... | collective-permute-start | bytes 786440 | tf_op jit(solution)/shard_map/ppermute | solution.py:283
  6.1 27.8 %copy-start = (bf16[512,2048]{1,0:T(8,128)(2,1)S(1)}, bf16[512,2048]{1,0:T(8,128)(2,1)}, u32[]{:S(2)}) copy-start(bf16[512,2048]{1,0:T(8,128)(2,1)} %w_send.3) | copy-start | bytes 6291460
  14.9 11.6 %collective-permute-start.5 = (bf16[256,512]{1,0:T(8,128)(2,1)S(1)}, bf16[256,512]{1,0:T(8,128)(2,1)S(1)}, u32[]{:S(2)}, u32[]{:S(2)}) collective-permute-start(bf16[256,512]{1,0:T(8,128)(2,1)S(1)} %get-tuple-element.18.own), channel_id=1, source_target_pairs={{0,2},{1,3},{2,0},{3,1},{4,6},{5,7},{6,4},{7,5},{8,10},{9,11},{10,... | collective-permute-start | bytes 786440 | tf_op jit(solution)/shard_map/ppermute | solution.py:283
  18.3 17.6 %collective-permute-start.2 = (bf16[256,512]{1,0:T(8,128)(2,1)S(1)}, bf16[256,512]{1,0:T(8,128)(2,1)S(1)}, u32[]{:S(2)}, u32[]{:S(2)}) collective-permute-start(bf16[256,512]{1,0:T(8,128)(2,1)S(1)} %get-tuple-element.31.own), channel_id=1, source_target_pairs={{1,2},{2,1},{5,6},{6,5},{9,10},{10,9},{13,14},{14,13},{17,18},{18,... | collective-permute-start | bytes 786440 | tf_op jit(solution)/shard_map/ppermute | solution.py:299
  20.2 15.8 %collective-permute-start = (bf16[256,512]{1,0:T(8,128)(2,1)S(1)}, bf16[256,512]{1,0:T(8,128)(2,1)}, u32[]{:S(2)}, u32[]{:S(2)}) collective-permute-start(bf16[256,512]{1,0:T(8,128)(2,1)S(1)} %get-tuple-element.31.own), channel_id=1, source_target_pairs={{0,1},{1,0},{2,3},{3,2},{4,5},{5,4},{6,7},{7,6},{8,9},{9,8},{10,11... | collective-permute-start | bytes 786440 | tf_op jit(solution)/shard_map/ppermute | solution.py:283
  20.3 16.0 %collective-permute-start.3 = (bf16[256,512]{1,0:T(8,128)(2,1)S(1)}, bf16[256,512]{1,0:T(8,128)(2,1)}, u32[]{:S(2)}, u32[]{:S(2)}) collective-permute-start(bf16[256,512]{1,0:T(8,128)(2,1)S(1)} %collective-permute-done.1.two), channel_id=1, source_target_pairs={{1,0},{2,3},{5,4},{6,7},{9,8},{10,11},{13,12},{14,15},{17,16},{18,... | collective-permute-start | bytes 786440 | tf_op jit(solution)/shard_map/ppermute | solution.py:300
  26.5 18.0 %collective-permute-start.7 = (bf16[256,512]{1,0:T(8,128)(2,1)S(1)}, bf16[256,512]{1,0:T(8,128)(2,1)S(1)}, u32[]{:S(2)}, u32[]{:S(2)}) collective-permute-start(bf16[256,512]{1,0:T(8,128)(2,1)S(1)} %collective-permute-done.5.two), channel_id=1, source_target_pairs={{1,0},{2,3},{5,4},{6,7},{9,8},{10,11},{13,12},{14,15},{17,16},{18,... | collective-permute-start | bytes 786440 | tf_op jit(solution)/shard_map/ppermute | solution.py:300
  34.0 21.0 %collective-permute-start.6 = (bf16[256,512]{1,0:T(8,128)(2,1)S(1)}, bf16[256,512]{1,0:T(8,128)(2,1)S(1)}, u32[]{:S(2)}, u32[]{:S(2)}) collective-permute-start(bf16[256,512]{1,0:T(8,128)(2,1)S(1)} %get-tuple-element.18.own), channel_id=1, source_target_pairs={{1,2},{2,1},{5,6},{6,5},{9,10},{10,9},{13,14},{14,13},{17,18},{18,... | collective-permute-start | bytes 786440 | tf_op jit(solution)/shard_map/ppermute | solution.py:299
  35.9 19.0 %collective-permute-start.4 = (bf16[256,512]{1,0:T(8,128)(2,1)S(1)}, bf16[256,512]{1,0:T(8,128)(2,1)S(1)}, u32[]{:S(2)}, u32[]{:S(2)}) collective-permute-start(bf16[256,512]{1,0:T(8,128)(2,1)S(1)} %get-tuple-element.18.own), channel_id=1, source_target_pairs={{0,1},{1,0},{2,3},{3,2},{4,5},{5,4},{6,7},{7,6},{8,9},{9,8},{10,11... | collective-permute-start | bytes 786440 | tf_op jit(solution)/shard_map/ppermute | solution.py:283
  41.1 13.9 %copy-start.2 = (bf16[2048,512]{1,0:T(8,128)(2,1)S(1)}, bf16[2048,512]{1,0:T(8,128)(2,1)}, u32[]{:S(2)}) copy-start(bf16[2048,512]{1,0:T(8,128)(2,1)} %w_q.3) | copy-start | bytes 6291460
  41.1 13.9 %copy-start.4 = (bf16[2048,512]{1,0:T(8,128)(2,1)S(1)}, bf16[2048,512]{1,0:T(8,128)(2,1)}, u32[]{:S(2)}) copy-start(bf16[2048,512]{1,0:T(8,128)(2,1)} %w_k.3) | copy-start | bytes 6291460
  41.1 14.0 %copy-start.6 = (bf16[2048,512]{1,0:T(8,128)(2,1)S(1)}, bf16[2048,512]{1,0:T(8,128)(2,1)}, u32[]{:S(2)}) copy-start(bf16[2048,512]{1,0:T(8,128)(2,1)} %w_v.3) | copy-start | bytes 6291460
  44.5 26.1 %collective-permute-start.13 = (bf16[512,512]{1,0:T(8,128)(2,1)S(1)}, bf16[512,512]{1,0:T(8,128)(2,1)S(1)}, u32[]{:S(2)}, u32[]{:S(2)}) collective-permute-start(bf16[512,512]{1,0:T(8,128)(2,1)S(1)} %constant_dynamic-slice_fusion), channel_id=1, source_target_pairs={{0,2},{1,3},{2,0},{3,1},{4,6},{5,7},{6,4},{7,5},{8,10},{9,11},{10,... | collective-permute-start | bytes 1572872 | tf_op jit(solution)/shard_map/ppermute | solution.py:283
  49.5 21.1 %copy-start.8 = (bf16[1536,512]{1,0:T(8,128)(2,1)S(1)}, bf16[1536,512]{1,0:T(8,128)(2,1)}, u32[]{:S(2)}) copy-start(bf16[1536,512]{1,0:T(8,128)(2,1)} %copy-done.7) | copy-start | bytes 4718596
  49.5 21.1 %copy-start.9 = (f32[4,128]{1,0:T(4,128)S(1)}, f32[4,128]{1,0:T(4,128)}, u32[]{:S(2)}) copy-start(f32[4,128]{1,0:T(4,128)} %bias_c.5) | copy-start | bytes 6148
  49.5 21.1 %copy-start.10 = (f32[4,128]{1,0:T(4,128)S(1)}, f32[4,128]{1,0:T(4,128)}, u32[]{:S(2)}) copy-start(f32[4,128]{1,0:T(4,128)} %bias_p.5) | copy-start | bytes 6148
  49.5 21.1 %collective-permute-start.11 = (bf16[256,1024]{1,0:T(8,128)(2,1)S(1)}, bf16[256,1024]{1,0:T(8,128)(2,1)S(1)}, u32[]{:S(2)}, u32[]{:S(2)}) collective-permute-start(bf16[256,1024]{1,0:T(8,128)(2,1)S(1)} %get-tuple-element.21.refs_4_), channel_id=1, source_target_pairs={{0,4},{4,8},{8,12},{12,16},{16,20},{20,24},{24,28},{1,5},{5,9},{9,... | collective-permute-start | bytes 1572872 | tf_op jit(solution)/shard_map/ppermute | solution.py:286
  51.6 19.1 %collective-permute-start.10 = (bf16[256,1024]{1,0:T(8,128)(2,1)S(1)}, bf16[256,1024]{1,0:T(8,128)(2,1)S(1)}, u32[]{:S(2)}, u32[]{:S(2)}) collective-permute-start(bf16[256,1024]{1,0:T(8,128)(2,1)S(1)} %get-tuple-element.21.refs_4_), channel_id=1, source_target_pairs={{0,8},{4,12},{8,16},{12,20},{16,24},{20,28},{1,9},{5,13},{9,17},{1... | collective-permute-start | bytes 1572872 | tf_op jit(solution)/shard_map/ppermute | solution.py:286
  57.6 25.9 %collective-permute-start.9 = (bf16[256,1024]{1,0:T(8,128)(2,1)S(1)}, bf16[256,1024]{1,0:T(8,128)(2,1)S(1)}, u32[]{:S(2)}, u32[]{:S(2)}) collective-permute-start(bf16[256,1024]{1,0:T(8,128)(2,1)S(1)} %get-tuple-element.19.refs_5_), channel_id=1, source_target_pairs={{0,4},{4,8},{8,12},{12,16},{16,20},{20,24},{24,28},{1,5},{5,9},{9,... | collective-permute-start | bytes 1572872 | tf_op jit(solution)/shard_map/ppermute | solution.py:286
  59.6 23.9 %collective-permute-start.8 = (bf16[256,1024]{1,0:T(8,128)(2,1)S(1)}, bf16[256,1024]{1,0:T(8,128)(2,1)S(1)}, u32[]{:S(2)}, u32[]{:S(2)}) collective-permute-start(bf16[256,1024]{1,0:T(8,128)(2,1)S(1)} %get-tuple-element.19.refs_5_), channel_id=1, source_target_pairs={{0,8},{4,12},{8,16},{12,20},{16,24},{20,28},{1,9},{5,13},{9,17},{1... | collective-permute-start | bytes 1572872 | tf_op jit(solution)/shard_map/ppermute | solution.py:286
  70.6 34.4 %collective-permute-start.14 = (bf16[512,512]{1,0:T(8,128)(2,1)S(1)}, bf16[512,512]{1,0:T(8,128)(2,1)S(1)}, u32[]{:S(2)}, u32[]{:S(2)}) collective-permute-start(bf16[512,512]{1,0:T(8,128)(2,1)S(1)} %collective-permute-done.13.got), channel_id=1, source_target_pairs={{0,4},{4,0},{8,12},{12,8},{16,20},{20,16},{24,28},{28,24},{1,5},{5... | collective-permute-start | bytes 1572872 | tf_op jit(solution)/shard_map/ppermute | solution.py:306
  88.5 16.5 %collective-permute-start.16 = (bf16[256,512]{1,0:T(8,128)(2,1)}, bf16[256,512]{1,0:T(8,128)(2,1)}, u32[]{:S(2)}, u32[]{:S(2)}) collective-permute-start(bf16[256,512]{1,0:T(8,128)(2,1)} %finish.3.own), channel_id=1, source_target_pairs={{0,2},{1,3},{2,0},{3,1},{4,6},{5,7},{6,4},{7,5},{8,10},{9,11},{10,... | collective-permute-start | bytes 786440 | tf_op jit(solution)/shard_map/ppermute | solution.py:283
  92.9 17.7 %collective-permute-start.12 = (bf16[256,512]{1,0:T(8,128)(2,1)S(1)}, bf16[256,512]{1,0:T(8,128)(2,1)}, u32[]{:S(2)}, u32[]{:S(2)}) collective-permute-start(bf16[256,512]{1,0:T(8,128)(2,1)S(1)} %finish.2.own), channel_id=1, source_target_pairs={{0,2},{1,3},{2,0},{3,1},{4,6},{5,7},{6,4},{7,5},{8,10},{9,11},{10,... | collective-permute-start | bytes 786440 | tf_op jit(solution)/shard_map/ppermute | solution.py:283
  107.4 15.2 %copy-start.12 = (bf16[512,512]{1,0:T(8,128)(2,1)S(1)}, bf16[512,512]{1,0:T(8,128)(2,1)}, u32[]{:S(2)}) copy-start(bf16[512,512]{1,0:T(8,128)(2,1)} %param.10) | copy-start | bytes 1572868
  107.4 9.2 %collective-permute-start.17 = (bf16[256,512]{1,0:T(8,128)(2,1)S(1)}, bf16[256,512]{1,0:T(8,128)(2,1)S(1)}, u32[]{:S(2)}, u32[]{:S(2)}) collective-permute-start(bf16[256,512]{1,0:T(8,128)(2,1)S(1)} %get-tuple-element.28), channel_id=1, source_target_pairs={{0,1},{1,0},{2,3},{3,2},{4,5},{5,4},{6,7},{7,6},{8,9},{9,8},{10,11... | collective-permute-start | bytes 786440 | tf_op jit(solution)/shard_map/ppermute | solution.py:283
  112.8 9.7 %collective-permute-start.15 = (bf16[256,512]{1,0:T(8,128)(2,1)S(1)}, bf16[256,512]{1,0:T(8,128)(2,1)S(1)}, u32[]{:S(2)}, u32[]{:S(2)}) collective-permute-start(bf16[256,512]{1,0:T(8,128)(2,1)S(1)} %get-tuple-element.26), channel_id=1, source_target_pairs={{0,1},{1,0},{2,3},{3,2},{4,5},{5,4},{6,7},{7,6},{8,9},{9,8},{10,11... | collective-permute-start | bytes 786440 | tf_op jit(solution)/shard_map/ppermute | solution.py:283
  122.5 8.9 %copy-start.13 = (f32[512]{0:T(512)S(1)}, f32[512]{0:T(512)}, u32[]{:S(2)}) copy-start(f32[512]{0:T(512)} %param.19) | copy-start | bytes 6148
  122.5 8.9 %copy-start.14 = (f32[512]{0:T(512)S(1)}, f32[512]{0:T(512)}, u32[]{:S(2)}) copy-start(f32[512]{0:T(512)} %param.18) | copy-start | bytes 6148
  123.2 4.6 %collective-permute-start.20 = (f32[2,512]{1,0:T(2,128)S(1)}, f32[2,512]{1,0:T(2,128)S(1)}, u32[]{:S(2)}, u32[]{:S(2)}) collective-permute-start(f32[2,512]{1,0:T(2,128)S(1)} %pad_maximum_fusion.1), channel_id=1, source_target_pairs={{0,3},{1,2},{2,1},{3,0},{4,7},{5,6},{6,5},{7,4},{8,11},{9,10},{10,... | collective-permute-start | bytes 12296 | tf_op jit(solution)/shard_map/ppermute | solution.py:283
  124.4 4.9 %collective-permute-start.19 = (f32[2,512]{1,0:T(2,128)S(1)}, f32[2,512]{1,0:T(2,128)S(1)}, u32[]{:S(2)}, u32[]{:S(2)}) collective-permute-start(f32[2,512]{1,0:T(2,128)S(1)} %pad_maximum_fusion.1), channel_id=1, source_target_pairs={{0,2},{1,3},{2,0},{3,1},{4,6},{5,7},{6,4},{7,5},{8,10},{9,11},{10,... | collective-permute-start | bytes 12296 | tf_op jit(solution)/shard_map/ppermute | solution.py:283
  127.7 3.6 %collective-permute-start.18 = (f32[2,512]{1,0:T(2,128)S(1)}, f32[2,512]{1,0:T(2,128)S(1)}, u32[]{:S(2)}, u32[]{:S(2)}) collective-permute-start(f32[2,512]{1,0:T(2,128)S(1)} %pad_maximum_fusion.1), channel_id=1, source_target_pairs={{0,1},{1,0},{2,3},{3,2},{4,5},{5,4},{6,7},{7,6},{8,9},{9,8},{10,11... | collective-permute-start | bytes 12296 | tf_op jit(solution)/shard_map/ppermute | solution.py:283
  (4 other events, 5.9 us)

commit v3 on v2

--- a/solution.py
+++ b/solution.py
@@ -7,10 +7,16 @@
 from jax.experimental.pallas import tpu as pltpu
 from jax.sharding import PartitionSpec as P
 
+
 TILE = 128
 ROWS = 256
 HP = 2
-VMEM = pltpu.CompilerParams(vmem_limit_bytes=16 * 2**20)
+
+
+def limit(mib):
+    return pltpu.CompilerParams(vmem_limit_bytes=mib * 2**20)
+
+
 NT = (((1,), (1,)), ((), ()))
 LOW = -1e30
 
@@ -46,7 +52,7 @@
         in_specs=[whole(a) for a in (far_sin, far_cos, near_sin, near_cos, w_pos)],
         out_specs=pl.BlockSpec((TILE, width), lambda b: (b, 0)),
         out_shape=jax.ShapeDtypeStruct((span, width), jnp.bfloat16),
-        compiler_params=VMEM,
+        compiler_params=limit(6),
         cost_estimate=pl.CostEstimate(
             flops=2 * span * model_width * width, transcendentals=0, bytes_accessed=4 * 2**20
         ),
@@ -54,51 +60,102 @@
     )(far_sin, far_cos, near_sin, near_cos, w_pos)
 
 
-def project_kernel(rank, own, one, two, near, relay, w_q, w_k, w_v, query, pairs, steps):
-    block = own.shape[1]
-    hidden = [own[...], one[...], two[...], near[...] + relay[...]]
+def pack_kernel(order, w_q, w_k, w_v, w_out, out, foreign, done):
+    step = pl.program_id(0)
+    block, width = out.shape[0], w_q.shape[1]
+    start = pl.multiple_of(order[step] * block, block)
+    copies = [
+        pltpu.make_async_copy(
+            weight.at[pl.ds(start, block), :], out.at[:, i * width : (i + 1) * width], done.at[i]
+        )
+        for i, weight in enumerate((w_k, w_v, w_q))
+    ]
+    for copy in copies:
+        copy.start()
+
+    @pl.when(step == 0)
+    def _():
+        rows, cols = foreign.shape
+        row = pl.multiple_of(order[pl.num_programs(0) + 1] * rows, rows)
+        column = pl.multiple_of(order[pl.num_programs(0)] * cols, cols)
+        extra = pltpu.make_async_copy(
+            w_out.at[pl.ds(row, rows), pl.ds(column, cols)], foreign, done.at[3]
+        )
+        extra.start()
+        extra.wait()
+
+    for copy in copies:
+        copy.wait()
+
+
+def pack(order, weights, w_out, block):
+    depth, width = weights[0].shape
+    rows = w_out.shape[0] // 2
+    grid_spec = pltpu.PrefetchScalarGridSpec(
+        num_scalar_prefetch=1,
+        grid=(depth // block,),
+        in_specs=[pl.BlockSpec(memory_space=pltpu.HBM) for _ in range(4)],
+        out_specs=[
+            pl.BlockSpec((block, 3 * width), lambda k, o: (k, 0)),
+            pl.BlockSpec((rows, block), lambda k, o: (0, 0)),
+        ],
+        scratch_shapes=[pltpu.SemaphoreType.DMA((4,))],
+    )
+    return pl.pallas_call(
+        pack_kernel,
+        grid_spec=grid_spec,
+        out_shape=[
+            jax.ShapeDtypeStruct((depth, 3 * width), jnp.bfloat16),
+            jax.ShapeDtypeStruct((rows, block), jnp.bfloat16),
+        ],
+        compiler_params=limit(10),
+        cost_estimate=pl.CostEstimate(
+            flops=2 * 10**9, transcendentals=0, bytes_accessed=12 * depth * width
+        ),
+        name="pack",
+    )(order, *weights, w_out)
+
+
+def project_kernel(own, one, two, *refs):
+    *three, w_k, w_v, w_q, query, pairs = refs
+    last = three[0][...]
+    if len(three) > 1:
+        last = last + three[1][...]
+    hidden = jnp.concatenate([own[...], one[...], two[...], last], 1)
     cols = query.shape[1]
     for weight, out in (
         (w_k, pairs.at[:, :cols]),
         (w_v, pairs.at[:, cols:]),
         (w_q, query),
     ):
-        total = None
-        for k, rows in enumerate(hidden):
-            piece = weight[pl.ds(pl.multiple_of((rank[0] ^ k) * block, block), block), :]
-            value = jnp.dot(rows, piece, preferred_element_type=jnp.float32)
-            total = value if total is None else total + value
+        total = jnp.dot(hidden, weight[...], preferred_element_type=jnp.float32)
         out[...] = total.astype(jnp.bfloat16)
 
 
-def project(rank, hidden, weights, steps=2):
+def project(hidden, packed, steps=2):
     rows, block = hidden[0].shape
-    depth, width = weights[0].shape
+    depth = packed.shape[0]
+    width = packed.shape[1] // 3
     cols = width // steps
-    out_specs = [pl.BlockSpec((rows, cols), lambda n, o: (0, n)) for _ in range(3)]
-    grid_spec = pltpu.PrefetchScalarGridSpec(
-        num_scalar_prefetch=1,
+    return pl.pallas_call(
+        project_kernel,
         grid=(steps,),
-        in_specs=[pl.BlockSpec((rows, block), lambda n, o: (0, 0)) for _ in hidden]
-        + [pl.BlockSpec((depth, cols), lambda n, o: (0, n)) for _ in weights],
+        in_specs=[pl.BlockSpec((rows, block), lambda n: (0, 0)) for _ in hidden]
+        + [pl.BlockSpec((depth, cols), lambda n, i=i: (0, i * steps + n)) for i in range(3)],
         out_specs=[
-            pl.BlockSpec((rows, cols), lambda n, o: (0, n)),
-            pl.BlockSpec((rows, 2 * cols), lambda n, o: (0, n)),
+            pl.BlockSpec((rows, cols), lambda n: (0, n)),
+            pl.BlockSpec((rows, 2 * cols), lambda n: (0, n)),
         ],
-    )
-    return pl.pallas_call(
-        functools.partial(project_kernel, steps=steps),
-        grid_spec=grid_spec,
         out_shape=[
             jax.ShapeDtypeStruct((rows, width), jnp.bfloat16),
             jax.ShapeDtypeStruct((rows, 2 * width), jnp.bfloat16),
         ],
-        compiler_params=VMEM,
+        compiler_params=limit(11),
         cost_estimate=pl.CostEstimate(
             flops=6 * rows * depth * width, transcendentals=0, bytes_accessed=6 * depth * width
         ),
         name="project",
-    )(rank, *hidden, *weights)
+    )(*hidden, packed, packed, packed)
 
 
 def attend_kernel(
@@ -108,7 +165,6 @@
     pairs = refs[count : count + len(pieces)]
     refs = refs[count + len(pieces) :]
     wide = HP * head_dim
-    span = 3 * seg
     log2 = 1.4426950408889634 / head_dim**0.5
     lane = lax.broadcasted_iota(jnp.int32, (ROWS, head_dim), 1)
     for local in range(HP):
@@ -215,7 +271,7 @@
         ),
         grid_spec=grid_spec,
         out_shape=shape(jnp.bfloat16) if final else [shape(jnp.float32), shape(jnp.float32)],
-        compiler_params=VMEM,
+        compiler_params=limit(8 if final else 12),
         cost_estimate=pl.CostEstimate(
             flops=16 * rows * size * heads * head_dim,
             transcendentals=rows * size * heads,
@@ -225,29 +281,39 @@
     )(place, bias_c, bias_p, rel, *queries, *pairs, *before)
 
 
-def output_kernel(where, own, other, w_mine, w_send, got, swapped, mine, send):
-    first = jnp.where(where[2] == 0, got[...], swapped[...])
-    second = jnp.where(where[2] == 0, swapped[...], got[...])
-
-    def both(a, b):
-        x = jnp.dot(own[...], a, preferred_element_type=jnp.float32).astype(jnp.bfloat16)
-        y = jnp.dot(other[...], b, preferred_element_type=jnp.float32).astype(jnp.bfloat16)
-        return x.astype(jnp.float32) + y.astype(jnp.float32)
-
-    send[...] = both(w_send[...], second).astype(jnp.bfloat16)
-    mine[...] = both(w_mine[...], first)
-
-
-def output(where, own, other, w_out, got, swapped):
+def output_kernel(where, own, other, w_mine, w_send, got, far, mine, send):
+    half = got.shape[1]
+
+    def partner(which):
+        near = jnp.where(where[2] == which, got[0], far[0])
+        away = jnp.where(where[2] == which, got[1], far[1])
+        top = jnp.where(where[3] == 0, near, away)
+        low = jnp.where(where[3] == 0, away, near)
+        return jnp.dot(
+            other[:, :half], top, preferred_element_type=jnp.float32
+        ) + jnp.dot(other[:, half:], low, preferred_element_type=jnp.float32)
+
+    def both(weight, which):
+        x = jnp.dot(own[...], weight[...], preferred_element_type=jnp.float32)
+        y = partner(which)
+        return x.astype(jnp.bfloat16).astype(jnp.float32) + y.astype(jnp.bfloat16).astype(
+            jnp.float32
+        )
+
+    send[...] = both(w_send, 1).astype(jnp.bfloat16)
+    mine[...] = both(w_mine, 0)
+
+
+def output(where, own, other, w_out, got, far):
     rows, depth = own.shape
-    block = got.shape[1]
-    whole = lambda a: pl.BlockSpec(a.shape, lambda i, o: (0, 0))
+    block = got.shape[2]
+    whole = lambda a: pl.BlockSpec(a.shape, lambda i, o: (0,) * len(a.shape))
     grid_spec = pltpu.PrefetchScalarGridSpec(
         num_scalar_prefetch=1,
         grid=(1,),
         in_specs=[whole(own), whole(other)]
         + [pl.BlockSpec((depth, block), lambda i, o, k=k: (0, o[k])) for k in (0, 1)]
-        + [whole(got), whole(swapped)],
+        + [whole(got), whole(far)],
         out_specs=[pl.BlockSpec((rows, block), lambda i, o: (0, 0)) for _ in range(2)],
     )
     return pl.pallas_call(
@@ -257,12 +323,12 @@
             jax.ShapeDtypeStruct((rows, block), jnp.float32),
             jax.ShapeDtypeStruct((rows, block), jnp.bfloat16),
         ],
-        compiler_params=VMEM,
+        compiler_params=limit(8),
         cost_estimate=pl.CostEstimate(
             flops=8 * rows * depth * block, transcendentals=0, bytes_accessed=10 * depth * block
         ),
         name="output",
-    )(where, own, other, w_out, w_out, got, swapped)
+    )(where, own, other, w_out, w_out, got, far)
 
 
 def shards(
@@ -273,62 +339,78 @@
     span = 3 * seg
     tp = lax.axis_size("tp")
     seqs = lax.axis_size("seq")
-    assert tp == 4 and seqs % 2 == 0
+    assert tp == 4 and seqs % 8 == 0
     place = lax.axis_index("seq").astype(jnp.int32)
     rank = lax.axis_index("tp").astype(jnp.int32)
     core = place % 2
     half = seg // 2
+    order = jnp.bitwise_xor(rank, jnp.arange(tp, dtype=jnp.int32))
+    side = (place // 4) % 2
+    order = jnp.concatenate([order, jnp.stack([rank ^ 2 ^ core, side])])
+    where = jnp.stack([rank, rank ^ 1, core, side])
+    first_core = jnp.full((1, 2 * bias_content.size), core == 0).astype(jnp.bfloat16)
+    spot = place.reshape(1)
+    hidden_in, order, where, first_core, spot = lax.optimization_barrier(
+        (hidden_in, order, where, first_core, spot)
+    )
 
     def across(x, k):
         return lax.ppermute(x, "tp", [(i, i ^ k) for i in range(tp)])
 
-    def later(x, k):
-        return lax.ppermute(x, "seq", [(i, i + k) for i in range(seqs - k)])
+    def swap(x):
+        return lax.ppermute(x, "seq", [(i, i ^ 1) for i in range(seqs)])
 
     def after(x, *others):
         return lax.optimization_barrier((x,) + others)[0]
 
-    rel = relative(span, w_pos)
-
     halves = [hidden_in[:half], hidden_in[half:]]
     gathered = []
-    for h in halves:
-        x = after(h, gathered[0][2], rel) if gathered else h
-        two = across(x, 2)
-        one = across(x, 1)
-        near = lax.ppermute(x, "tp", [(1, 2), (2, 1)])
-        relay = lax.ppermute(two, "tp", [(1, 0), (2, 3)])
-        gathered.append((h, one, two, near, relay))
-
-    foreign = lax.dynamic_slice_in_dim(w_out, (rank ^ 2 ^ core) * block, block, 1)
-    foreign = after(foreign, gathered[1][4])
+    for tag, h in zip("ab", halves):
+        two = across(h, 2)
+        one = across(h, 1)
+        if tag == "a":
+            near = lax.ppermute(h, "tp", [(1, 2), (2, 1)])
+            relay = lax.ppermute(two, "tp", [(1, 0), (2, 3)])
+            gathered.append((h, one, two, near, relay))
+        else:
+            gathered.append((h, one, two, across(h, 3)))
+
+    packed, foreign = pack(order, (w_query, w_key, w_value), w_out, block)
+    rel = relative(span, w_pos)
+
     got = across(foreign, 2)
-    swapped = lax.ppermute(got, "seq", [(i, i ^ 1) for i in range(seqs)])
-
-    spot = place.reshape(1)
-    query, pairs, early = [], [], []
-    for g in gathered:
-        q, kv = project(rank.reshape(1), g, (w_query, w_key, w_value))
+    got = jnp.stack([got, lax.ppermute(got, "seq", [(i, i ^ 4) for i in range(seqs)])])
+    far = swap(got)
+
+    query, pairs, back = [], [], []
+    for tag, g in zip("ab", gathered):
+        q, kv = project(g, packed)
         query.append(q)
         pairs.append(kv)
-        early.append([later(kv, d) for d in (2, 1)])
+        back.append(lax.ppermute(kv, "seq", [(i, i + 2) for i in range(seqs - 2)]))
+
+    def last(kv, back, mask):
+        return swap(jnp.where(mask > 0.5, kv, back))
+
+    before = [back[0], last(pairs[0], back[0], first_core)]
     state = attend(
         spot, query, bias_content, bias_pos, rel,
-        early[0] + pairs,
+        before + pairs,
         (0, seg, 2 * seg, 2 * seg + half), 0, seg,
     )
-    where = jnp.stack([rank, rank ^ 1, core])
+    first_core = after(first_core, *state)
+    before = [back[1], last(pairs[1], back[1], first_core)]
     summed = []
-    for i in range(2):
+    for i, tag in enumerate("ab"):
         attended = attend(
             spot, query[i : i + 1], bias_content, bias_pos, rel,
-            early[1],
+            before,
             (half, seg + half), i * half, seg,
             before=state,
         )
         other = across(attended, 2)
-        mine, send = output(where, attended, other, w_out, got, swapped)
-        received = across(send, 1)
+        mine, theirs = output(where, attended, other, w_out, got, far)
+        received = across(theirs, 1)
         summed.append(halves[i].astype(jnp.float32) + mine + received.astype(jnp.float32))
     summed = jnp.concatenate(summed, 0)
     total = jnp.sum(summed, axis=1)
@@ -357,4 +439,5 @@
         P("tp"),
     )
     out_specs = P("seq", "tp")
+
     return jax.shard_map(shards, mesh=mesh, in_specs=in_specs, out_specs=out_specs, check_vma=False)

time: 133 us -> 131 us (0.985)
  the two profiles are of different devices: /device:TPU:12 before, /device:TPU:0 now
where the time goes in v3:
time: 131 us
  waiting for transfers between devices  54.1 us (41%)
  starting transfers between devices  34.1 us (26%)
  Pallas kernels  30.6 us (23%)
  local copies, waits for them, and re-layouts  7.48 us (6%)
  other arithmetic  4.27 us (3%)
    ppermute x13, waiting for transfers between devices, across(): return lax.ppermute(x, 'tp', [(i, i ^ k) for i in range(tp)])  38.3 us
    ppermute x13, starting transfers between devices, across(): return lax.ppermute(x, 'tp', [(i, i ^ k) for i in range(tp)])  21.5 us
    pallas_call x3, Pallas kernels, attend(): pl.pallas_call(functools.partial(attend_kernel, first=first, count=len(qu...  15.4 us
    ppermute x2, starting transfers between devices, shards(): back.append(lax.ppermute(kv, 'seq', [(i, i + 2) for i in range(seqs - 2)]))  7.72 us
    ppermute x1, waiting for transfers between devices, shards(): lax.ppermute(got, 'seq', [(i, i ^ 4) for i in range(seqs)])  6.89 us
    pallas_call x1, Pallas kernels, relative(): pl.pallas_call(relative_kernel, grid=(blocks,), in_specs=[whole(a) for a...  6.4 us
    unnamed x22, local copies, waits for them, and re-layouts  6.4 us
    ppermute x2, waiting for transfers between devices, shards(): back.append(lax.ppermute(kv, 'seq', [(i, i + 2) for i in range(seqs - 2)]))  5.08 us
  transfers between devices with their start and end apart: 21, of which 10 were waited for; matrix products, arithmetic and copies ran while one was open for 2% of the time, Pallas kernels for 23%

profile of v3, /device:TPU:0, one launch (start us, length us, event | category | flops | bytes accessed | tf_op | source)
XLA Modules:
  0.0 131.0 jit_solution(2070664989229540700)
XLA Ops:
  1.2 4.1 %collective-permute-start.1 = (bf16[256,512]{1,0:T(8,128)(2,1)S(1)}, bf16[256,512]{1,0:T(8,128)(2,1)S(1)}, u32[]{:S(2)}, u32[]{:S(2)}) collective-permute-start(bf16[256,512]{1,0:T(8,128)(2,1)S(1)} %get-tuple-element.43.own), channel_id=1, source_target_pairs={{0,2},{1,3},{2,0},{3,1},{4,6},{5,7},{6,4},{7,5},{8,10},{9,11},{10,... | collective-permute-start | bytes 786440 | tf_op jit(solution)/shard_map/ppermute | solution.py:358
  5.4 1.6 %collective-permute-start = (bf16[256,512]{1,0:T(8,128)(2,1)S(1)}, bf16[256,512]{1,0:T(8,128)(2,1)S(1)}, u32[]{:S(2)}, u32[]{:S(2)}) collective-permute-start(bf16[256,512]{1,0:T(8,128)(2,1)S(1)} %get-tuple-element.43.own), channel_id=1, source_target_pairs={{0,1},{1,0},{2,3},{3,2},{4,5},{5,4},{6,7},{7,6},{8,9},{9,8},{10,11... | collective-permute-start | bytes 786440 | tf_op jit(solution)/shard_map/ppermute | solution.py:358
  7.6 2.2 %collective-permute-start.4 = (bf16[256,512]{1,0:T(8,128)(2,1)S(1)}, bf16[256,512]{1,0:T(8,128)(2,1)S(1)}, u32[]{:S(2)}, u32[]{:S(2)}) collective-permute-start(bf16[256,512]{1,0:T(8,128)(2,1)S(1)} %get-tuple-element.44.own), channel_id=1, source_target_pairs={{0,1},{1,0},{2,3},{3,2},{4,5},{5,4},{6,7},{7,6},{8,9},{9,8},{10,11... | collective-permute-start | bytes 786440 | tf_op jit(solution)/shard_map/ppermute | solution.py:358
  10.9 7.3 %collective-permute-done.1.two = bf16[256,512]{1,0:T(8,128)(2,1)S(1)} collective-permute-done((bf16[256,512]{1,0:T(8,128)(2,1)S(1)}, bf16[256,512]{1,0:T(8,128)(2,1)S(1)}, u32[]{:S(2)}, u32[]{:S(2)}) %collective-permute-start.1) | collective-permute-done | bytes 262176 | tf_op jit(solution)/shard_map/ppermute | solution.py:358
  19.5 1.6 %copy-done = bf16[512,2048]{1,0:T(8,128)(2,1)S(1)} copy-done((bf16[512,2048]{1,0:T(8,128)(2,1)S(1)}, bf16[512,2048]{1,0:T(8,128)(2,1)}, u32[]{:S(2)}) %copy-start) | copy-done | bytes 2097176
  21.1 1.6 %copy-done.2 = bf16[2048,512]{1,0:T(8,128)(2,1)S(1)} copy-done((bf16[2048,512]{1,0:T(8,128)(2,1)S(1)}, bf16[2048,512]{1,0:T(8,128)(2,1)}, u32[]{:S(2)}) %copy-start.2) | copy-done | bytes 2097176
  22.7 1.6 %copy-done.3 = bf16[2048,512]{1,0:T(8,128)(2,1)S(1)} copy-done((bf16[2048,512]{1,0:T(8,128)(2,1)S(1)}, bf16[2048,512]{1,0:T(8,128)(2,1)}, u32[]{:S(2)}) %copy-start.3) | copy-done | bytes 2097176
  24.3 1.6 %copy-done.4 = bf16[2048,512]{1,0:T(8,128)(2,1)S(1)} copy-done((bf16[2048,512]{1,0:T(8,128)(2,1)S(1)}, bf16[2048,512]{1,0:T(8,128)(2,1)}, u32[]{:S(2)}) %copy-start.4) | copy-done | bytes 2097176
  27.0 2.8 %collective-permute-start.6 = (bf16[256,512]{1,0:T(8,128)(2,1)S(1)}, bf16[256,512]{1,0:T(8,128)(2,1)S(1)}, u32[]{:S(2)}, u32[]{:S(2)}) collective-permute-start(bf16[256,512]{1,0:T(8,128)(2,1)S(1)} %get-tuple-element.44.own), channel_id=1, source_target_pairs={{0,3},{1,2},{2,1},{3,0},{4,7},{5,6},{6,5},{7,4},{8,11},{9,10},{10,... | collective-permute-start | bytes 786440 | tf_op jit(solution)/shard_map/ppermute | solution.py:358
  29.8 1.3 %collective-permute-start.12 = (bf16[256,512]{1,0:T(8,128)(2,1)S(1)}, bf16[256,512]{1,0:T(8,128)(2,1)S(1)}, u32[]{:S(2)}, u32[]{:S(2)}) collective-permute-start(bf16[256,512]{1,0:T(8,128)(2,1)S(1)} %get-tuple-element.36), channel_id=1, source_target_pairs={{0,2},{1,3},{2,0},{3,1},{4,6},{5,7},{6,4},{7,5},{8,10},{9,11},{10,... | collective-permute-start | bytes 786440 | tf_op jit(solution)/shard_map/ppermute | solution.py:358
  31.2 3.9 %collective-permute-done.3.refs_1_ = bf16[256,512]{1,0:T(8,128)(2,1)S(1)} collective-permute-done((bf16[256,512]{1,0:T(8,128)(2,1)S(1)}, bf16[256,512]{1,0:T(8,128)(2,1)S(1)}, u32[]{:S(2)}, u32[]{:S(2)}) %collective-permute-start.3) | collective-permute-done | bytes 262176 | tf_op jit(solution)/shard_map/ppermute | solution.py:373
  35.1 2.5 %project.2 = (bf16[256,512]{1,0:T(8,128)(2,1)S(1)}, bf16[256,1024]{1,0:T(8,128)(2,1)S(1)}) custom-call(bf16[256,512]{1,0:T(8,128)(2,1)S(1)} %get-tuple-element.43.own, bf16[256,512]{1,0:T(8,128)(2,1)S(1)} %collective-permute-done.one, bf16[256,512]{1,0:T(8,128)(2,1)S(1)} %collective-permute-done.1.two, bf16[256,512]{1,0:T(8,128)(2,1)S(1)} %collective-permute-done.2.refs_0_, ...), custom_call_target="tpu_custom_call" | custom-call | flops 1610612736 | bytes 6291456 | tf_op jit(solution)/shard_map/project/pallas_call | solution.py:140
  37.6 3.1 %collective-permute-start.8 = (bf16[256,1024]{1,0:T(8,128)(2,1)S(1)}, bf16[256,1024]{1,0:T(8,128)(2,1)S(1)}, u32[]{:S(2)}, u32[]{:S(2)}) collective-permute-start(bf16[256,1024]{1,0:T(8,128)(2,1)S(1)} %get-tuple-element.32.refs_4_), channel_id=1, source_target_pairs={{0,8},{4,12},{8,16},{12,20},{16,24},{20,28},{1,9},{5,13},{9,17},{1... | collective-permute-start | bytes 1572872 | tf_op jit(solution)/shard_map/ppermute | solution.py:390
  40.8 1.9 %multiply_cosine_fusion = (f32[128,1024]{1,0:T(8,128)S(1)}, f32[128,1024]{1,0:T(8,128)S(1)}) fusion(f32[1024]{0:T(1024)S(1)} %multiply_exponential_fusion, f32[128]{0:T(128)S(1)} %subtract_convert_fusion), kind=kLoop, calls=%fused_computation.3 | loop fusion | flops 131072 | bytes 1053184 | tf_op jit(solution)/shard_map/cos | solution.py:28
  42.7 5.1 %collective-permute-done.8.refs_2_ = bf16[256,1024]{1,0:T(8,128)(2,1)S(1)} collective-permute-done((bf16[256,1024]{1,0:T(8,128)(2,1)S(1)}, bf16[256,1024]{1,0:T(8,128)(2,1)S(1)}, u32[]{:S(2)}, u32[]{:S(2)}) %collective-permute-start.8) | collective-permute-done | bytes 524320 | tf_op jit(solution)/shard_map/ppermute | solution.py:390
  48.3 2.5 %project.3 = (bf16[256,512]{1,0:T(8,128)(2,1)S(1)}, bf16[256,1024]{1,0:T(8,128)(2,1)S(1)}) custom-call(bf16[256,512]{1,0:T(8,128)(2,1)S(1)} %get-tuple-element.44.own, bf16[256,512]{1,0:T(8,128)(2,1)S(1)} %collective-permute-done.4.one, bf16[256,512]{1,0:T(8,128)(2,1)S(1)} %collective-permute-done.5.two, ...), custom_call_target="tpu_custom_call" | custom-call | flops 1610612736 | bytes 6291456 | tf_op jit(solution)/shard_map/project/pallas_call | solution.py:140
  50.8 4.6 %collective-permute-start.7 = (bf16[256,1024]{1,0:T(8,128)(2,1)S(1)}, bf16[256,1024]{1,0:T(8,128)(2,1)S(1)}, u32[]{:S(2)}, u32[]{:S(2)}) collective-permute-start(bf16[256,1024]{1,0:T(8,128)(2,1)S(1)} %get-tuple-element.29.refs_5_), channel_id=1, source_target_pairs={{0,8},{4,12},{8,16},{12,20},{16,24},{20,28},{1,9},{5,13},{9,17},{1... | collective-permute-start | bytes 1572872 | tf_op jit(solution)/shard_map/ppermute | solution.py:390
  55.4 6.4 %relative.1.rel = bf16[1536,512]{1,0:T(8,128)(2,1)S(1)} custom-call(f32[12,1024]{1,0:T(8,128)S(1)} %get-tuple-element.50.far_sin, f32[12,1024]{1,0:T(8,128)S(1)} %get-tuple-element.49.far_cos, f32[128,1024]{1,0:T(8,128)S(1)} %get-tuple-element.48.near_sin, f32[128,1024]{1,0:T(8,128)S(1)} %get-tuple-element.47.near_cos, bf16[2048,512]{1,0:T(8,128)(2,1)S(1)} %copy-done.7), custom_call_target="tpu_custom_call" | custom-call | flops 3221225472 | bytes 4194304 | tf_op jit(solution)/shard_map/relative/pallas_call | solution.py:49
  61.9 6.7 %begin.1 = (f32[512,512]{1,0:T(8,128)S(1)}, f32[512,512]{1,0:T(8,128)S(1)}) custom-call(s32[1]{0:T(128)} %bitcast.5.place, f32[4,128]{1,0:T(4,128)S(1)} %copy-done.5, f32[4,128]{1,0:T(4,128)S(1)} %copy-done.6, bf16[1536,512]{1,0:T(8,128)(2,1)S(1)} %relative.1.rel, bf16[256,512]{1,0:T(8,128)(2,1)S(1)} %get-tuple-element.28.refs_0_, ...), custom_call_target="tpu_custom_call" | custom-call | flops 4294967296 | bytes 3145728 | tf_op jit(solution)/shard_map/begin/pallas_call | solution.py:262
  69.0 2.5 %collective-permute-start.13 = (bf16[256,512]{1,0:T(8,128)(2,1)S(1)}, bf16[256,512]{1,0:T(8,128)(2,1)S(1)}, u32[]{:S(2)}, u32[]{:S(2)}) collective-permute-start(bf16[256,512]{1,0:T(8,128)(2,1)S(1)} %collective-permute-done.12), channel_id=1, source_target_pairs={{0,16},{4,20},{8,24},{12,28},{16,0},{20,4},{24,8},{28,12},{1,17},{... | collective-permute-start | bytes 786440 | tf_op jit(solution)/shard_map/ppermute | solution.py:382
  71.5 6.9 %collective-permute-done.13 = bf16[256,512]{1,0:T(8,128)(2,1)S(1)} collective-permute-done((bf16[256,512]{1,0:T(8,128)(2,1)S(1)}, bf16[256,512]{1,0:T(8,128)(2,1)S(1)}, u32[]{:S(2)}, u32[]{:S(2)}) %collective-permute-start.13) | collective-permute-done | bytes 262176 | tf_op jit(solution)/shard_map/ppermute | solution.py:382
  78.6 4.3 %finish.3.own = bf16[256,512]{1,0:T(8,128)(2,1)S(1)} custom-call(s32[1]{0:T(128)} %bitcast.5.place, f32[4,128]{1,0:T(4,128)S(1)} %copy-done.5, f32[4,128]{1,0:T(4,128)S(1)} %copy-done.6, bf16[1536,512]{1,0:T(8,128)(2,1)S(1)} %relative.1.rel, bf16[256,512]{1,0:T(8,128)(2,1)S(1)} %get-tuple-element.31.refs_1_.refs_0_, ...), custom_call_target="tpu_custom_call" | custom-call | flops 1073741824 | bytes 1572864 | tf_op jit(solution)/shard_map/finish/pallas_call | solution.py:262
  82.9 3.7 %collective-permute-start.16 = (bf16[256,512]{1,0:T(8,128)(2,1)S(1)}, bf16[256,512]{1,0:T(8,128)(2,1)S(1)}, u32[]{:S(2)}, u32[]{:S(2)}) collective-permute-start(bf16[256,512]{1,0:T(8,128)(2,1)S(1)} %finish.3.own), channel_id=1, source_target_pairs={{0,2},{1,3},{2,0},{3,1},{4,6},{5,7},{6,4},{7,5},{8,10},{9,11},{10,... | collective-permute-start | bytes 786440 | tf_op jit(solution)/shard_map/ppermute | solution.py:358
  86.6 4.3 %finish.2.own = bf16[256,512]{1,0:T(8,128)(2,1)S(1)} custom-call(s32[1]{0:T(128)} %bitcast.5.place, f32[4,128]{1,0:T(4,128)S(1)} %copy-done.5, f32[4,128]{1,0:T(4,128)S(1)} %copy-done.6, bf16[1536,512]{1,0:T(8,128)(2,1)S(1)} %relative.1.rel, bf16[256,512]{1,0:T(8,128)(2,1)S(1)} %get-tuple-element.28.refs_0_, ...), custom_call_target="tpu_custom_call" | custom-call | flops 1073741824 | bytes 1572864 | tf_op jit(solution)/shard_map/finish/pallas_call | solution.py:262
  91.0 14.0 %collective-permute-done.16.other = bf16[256,512]{1,0:T(8,128)(2,1)S(1)} collective-permute-done((bf16[256,512]{1,0:T(8,128)(2,1)S(1)}, bf16[256,512]{1,0:T(8,128)(2,1)S(1)}, u32[]{:S(2)}, u32[]{:S(2)}) %collective-permute-start.16) | collective-permute-done | bytes 262176 | tf_op jit(solution)/shard_map/ppermute | solution.py:358
  106.4 4.1 %collective-permute-done.11.other = bf16[256,512]{1,0:T(8,128)(2,1)S(1)} collective-permute-done((bf16[256,512]{1,0:T(8,128)(2,1)S(1)}, bf16[256,512]{1,0:T(8,128)(2,1)S(1)}, u32[]{:S(2)}, u32[]{:S(2)}) %collective-permute-start.11) | collective-permute-done | bytes 262176 | tf_op jit(solution)/shard_map/ppermute | solution.py:358
  110.5 1.3 %output.2 = (f32[256,512]{1,0:T(8,128)S(1)}, bf16[256,512]{1,0:T(8,128)(2,1)S(1)}) custom-call(s32[4]{0:T(128)S(1)} %pad_add_fusion.1.where, bf16[256,512]{1,0:T(8,128)(2,1)S(1)} %finish.2.own, bf16[256,512]{1,0:T(8,128)(2,1)S(1)} %collective-permute-done.11.other, bf16[512,2048]{1,0:T(8,128)(2,1)S(1)} %copy-done.1, bf16[512,2048]{1,0:T(8,128)(2,1)S(1)} %copy-done.1, ...), custom_call_target="tpu_custom_call" | custom-call | flops 536870912 | bytes 2621440 | tf_op jit(solution)/shard_map/output/pallas_call | solution.py:319
  111.9 4.2 %collective-permute-done.17 = bf16[256,512]{1,0:T(8,128)(2,1)S(1)} collective-permute-done((bf16[256,512]{1,0:T(8,128)(2,1)S(1)}, bf16[256,512]{1,0:T(8,128)(2,1)S(1)}, u32[]{:S(2)}, u32[]{:S(2)}) %collective-permute-start.17) | collective-permute-done | bytes 262176 | tf_op jit(solution)/shard_map/ppermute | solution.py:358
  116.1 5.5 %collective-permute-done.15 = bf16[256,512]{1,0:T(8,128)(2,1)S(1)} collective-permute-done((bf16[256,512]{1,0:T(8,128)(2,1)S(1)}, bf16[256,512]{1,0:T(8,128)(2,1)S(1)}, u32[]{:S(2)}, u32[]{:S(2)}) %collective-permute-start.15) | collective-permute-done | bytes 262176 | tf_op jit(solution)/shard_map/ppermute | solution.py:358
  122.3 2.2 %collective-permute-start.19 = (f32[2,512]{1,0:T(2,128)S(1)}, f32[2,512]{1,0:T(2,128)S(1)}, u32[]{:S(2)}, u32[]{:S(2)}) collective-permute-start(f32[2,512]{1,0:T(2,128)S(1)} %pad_maximum_fusion.2), channel_id=1, source_target_pairs={{0,2},{1,3},{2,0},{3,1},{4,6},{5,7},{6,4},{7,5},{8,10},{9,11},{10,... | collective-permute-start | bytes 12296 | tf_op jit(solution)/shard_map/ppermute | solution.py:358
  124.5 2.2 %collective-permute-start.20 = (f32[2,512]{1,0:T(2,128)S(1)}, f32[2,512]{1,0:T(2,128)S(1)}, u32[]{:S(2)}, u32[]{:S(2)}) collective-permute-start(f32[2,512]{1,0:T(2,128)S(1)} %pad_maximum_fusion.2), channel_id=1, source_target_pairs={{0,3},{1,2},{2,1},{3,0},{4,7},{5,6},{6,5},{7,4},{8,11},{9,10},{10,... | collective-permute-start | bytes 12296 | tf_op jit(solution)/shard_map/ppermute | solution.py:358
  126.9 3.0 %collective-permute-done.20 = f32[2,512]{1,0:T(2,128)S(1)} collective-permute-done((f32[2,512]{1,0:T(2,128)S(1)}, f32[2,512]{1,0:T(2,128)S(1)}, u32[]{:S(2)}, u32[]{:S(2)}) %collective-permute-start.20) | collective-permute-done | bytes 4128 | tf_op jit(solution)/shard_map/ppermute | solution.py:358
  (66 shorter events, 10.0 us)
Async XLA Ops:
  1.2 16.9 %collective-permute-start.1 = (bf16[256,512]{1,0:T(8,128)(2,1)S(1)}, bf16[256,512]{1,0:T(8,128)(2,1)S(1)}, u32[]{:S(2)}, u32[]{:S(2)}) collective-permute-start(bf16[256,512]{1,0:T(8,128)(2,1)S(1)} %get-tuple-element.43.own), channel_id=1, source_target_pairs={{0,2},{1,3},{2,0},{3,1},{4,6},{5,7},{6,4},{7,5},{8,10},{9,11},{10,... | collective-permute-start | bytes 786440 | tf_op jit(solution)/shard_map/ppermute | solution.py:358
  5.4 21.6 %collective-permute-start = (bf16[256,512]{1,0:T(8,128)(2,1)S(1)}, bf16[256,512]{1,0:T(8,128)(2,1)S(1)}, u32[]{:S(2)}, u32[]{:S(2)}) collective-permute-start(bf16[256,512]{1,0:T(8,128)(2,1)S(1)} %get-tuple-element.43.own), channel_id=1, source_target_pairs={{0,1},{1,0},{2,3},{3,2},{4,5},{5,4},{6,7},{7,6},{8,9},{9,8},{10,11... | collective-permute-start | bytes 786440 | tf_op jit(solution)/shard_map/ppermute | solution.py:358
  6.9 22.9 %collective-permute-start.2 = (bf16[256,512]{1,0:T(8,128)(2,1)S(1)}, bf16[256,512]{1,0:T(8,128)(2,1)S(1)}, u32[]{:S(2)}, u32[]{:S(2)}) collective-permute-start(bf16[256,512]{1,0:T(8,128)(2,1)S(1)} %get-tuple-element.43.own), channel_id=1, source_target_pairs={{1,2},{2,1},{5,6},{6,5},{9,10},{10,9},{13,14},{14,13},{17,18},{18,... | collective-permute-start | bytes 786440 | tf_op jit(solution)/shard_map/ppermute | solution.py:372
  7.6 40.6 %collective-permute-start.4 = (bf16[256,512]{1,0:T(8,128)(2,1)S(1)}, bf16[256,512]{1,0:T(8,128)(2,1)S(1)}, u32[]{:S(2)}, u32[]{:S(2)}) collective-permute-start(bf16[256,512]{1,0:T(8,128)(2,1)S(1)} %get-tuple-element.44.own), channel_id=1, source_target_pairs={{0,1},{1,0},{2,3},{3,2},{4,5},{5,4},{6,7},{7,6},{8,9},{9,8},{10,11... | collective-permute-start | bytes 786440 | tf_op jit(solution)/shard_map/ppermute | solution.py:358
  9.8 38.4 %collective-permute-start.5 = (bf16[256,512]{1,0:T(8,128)(2,1)S(1)}, bf16[256,512]{1,0:T(8,128)(2,1)S(1)}, u32[]{:S(2)}, u32[]{:S(2)}) collective-permute-start(bf16[256,512]{1,0:T(8,128)(2,1)S(1)} %get-tuple-element.44.own), channel_id=1, source_target_pairs={{0,2},{1,3},{2,0},{3,1},{4,6},{5,7},{6,4},{7,5},{8,10},{9,11},{10,... | collective-permute-start | bytes 786440 | tf_op jit(solution)/shard_map/ppermute | solution.py:358
  18.2 16.9 %collective-permute-start.3 = (bf16[256,512]{1,0:T(8,128)(2,1)S(1)}, bf16[256,512]{1,0:T(8,128)(2,1)S(1)}, u32[]{:S(2)}, u32[]{:S(2)}) collective-permute-start(bf16[256,512]{1,0:T(8,128)(2,1)S(1)} %collective-permute-done.1.two), channel_id=1, source_target_pairs={{1,0},{2,3},{5,4},{6,7},{9,8},{10,11},{13,12},{14,15},{17,16},{18,... | collective-permute-start | bytes 786440 | tf_op jit(solution)/shard_map/ppermute | solution.py:373
  19.5 1.6 %copy-start = (bf16[512,2048]{1,0:T(8,128)(2,1)S(1)}, bf16[512,2048]{1,0:T(8,128)(2,1)}, u32[]{:S(2)}) copy-start(bf16[512,2048]{1,0:T(8,128)(2,1)} %w_send.3) | copy-start | bytes 6291460
  21.1 1.6 %copy-start.2 = (bf16[2048,512]{1,0:T(8,128)(2,1)S(1)}, bf16[2048,512]{1,0:T(8,128)(2,1)}, u32[]{:S(2)}) copy-start(bf16[2048,512]{1,0:T(8,128)(2,1)} %w_q.1) | copy-start | bytes 6291460
  22.7 1.6 %copy-start.3 = (bf16[2048,512]{1,0:T(8,128)(2,1)S(1)}, bf16[2048,512]{1,0:T(8,128)(2,1)}, u32[]{:S(2)}) copy-start(bf16[2048,512]{1,0:T(8,128)(2,1)} %w_k.1) | copy-start | bytes 6291460
  24.3 1.6 %copy-start.4 = (bf16[2048,512]{1,0:T(8,128)(2,1)S(1)}, bf16[2048,512]{1,0:T(8,128)(2,1)}, u32[]{:S(2)}) copy-start(bf16[2048,512]{1,0:T(8,128)(2,1)} %w_v.1) | copy-start | bytes 6291460
  27.0 21.3 %collective-permute-start.6 = (bf16[256,512]{1,0:T(8,128)(2,1)S(1)}, bf16[256,512]{1,0:T(8,128)(2,1)S(1)}, u32[]{:S(2)}, u32[]{:S(2)}) collective-permute-start(bf16[256,512]{1,0:T(8,128)(2,1)S(1)} %get-tuple-element.44.own), channel_id=1, source_target_pairs={{0,3},{1,2},{2,1},{3,0},{4,7},{5,6},{6,5},{7,4},{8,11},{9,10},{10,... | collective-permute-start | bytes 786440 | tf_op jit(solution)/shard_map/ppermute | solution.py:358
  29.8 39.2 %collective-permute-start.12 = (bf16[256,512]{1,0:T(8,128)(2,1)S(1)}, bf16[256,512]{1,0:T(8,128)(2,1)S(1)}, u32[]{:S(2)}, u32[]{:S(2)}) collective-permute-start(bf16[256,512]{1,0:T(8,128)(2,1)S(1)} %get-tuple-element.36), channel_id=1, source_target_pairs={{0,2},{1,3},{2,0},{3,1},{4,6},{5,7},{6,4},{7,5},{8,10},{9,11},{10,... | collective-permute-start | bytes 786440 | tf_op jit(solution)/shard_map/ppermute | solution.py:358
  37.6 10.1 %collective-permute-start.8 = (bf16[256,1024]{1,0:T(8,128)(2,1)S(1)}, bf16[256,1024]{1,0:T(8,128)(2,1)S(1)}, u32[]{:S(2)}, u32[]{:S(2)}) collective-permute-start(bf16[256,1024]{1,0:T(8,128)(2,1)S(1)} %get-tuple-element.32.refs_4_), channel_id=1, source_target_pairs={{0,8},{4,12},{8,16},{12,20},{16,24},{20,28},{1,9},{5,13},{9,17},{1... | collective-permute-start | bytes 1572872 | tf_op jit(solution)/shard_map/ppermute | solution.py:390
  47.8 14.0 %collective-permute-start.9 = (bf16[256,1024]{1,0:T(8,128)(2,1)S(1)}, bf16[256,1024]{1,0:T(8,128)(2,1)S(1)}, u32[]{:S(2)}, u32[]{:S(2)}) collective-permute-start(bf16[256,1024]{1,0:T(8,128)(2,1)S(1)} %broadcast_select_fusion.1), channel_id=1, source_target_pairs={{0,4},{4,0},{8,12},{12,8},{16,20},{20,16},{24,28},{28,24},{1,5},{5... | collective-permute-start | bytes 1572872 | tf_op jit(solution)/shard_map/ppermute | solution.py:361
  48.2 7.2 %copy-start.7 = (bf16[2048,512]{1,0:T(8,128)(2,1)S(1)}, bf16[2048,512]{1,0:T(8,128)(2,1)}, u32[]{:S(2)}) copy-start(bf16[2048,512]{1,0:T(8,128)(2,1)} %weight.1) | copy-start | bytes 6291460
  50.8 17.9 %collective-permute-start.7 = (bf16[256,1024]{1,0:T(8,128)(2,1)S(1)}, bf16[256,1024]{1,0:T(8,128)(2,1)S(1)}, u32[]{:S(2)}, u32[]{:S(2)}) collective-permute-start(bf16[256,1024]{1,0:T(8,128)(2,1)S(1)} %get-tuple-element.29.refs_5_), channel_id=1, source_target_pairs={{0,8},{4,12},{8,16},{12,20},{16,24},{20,28},{1,9},{5,13},{9,17},{1... | collective-permute-start | bytes 1572872 | tf_op jit(solution)/shard_map/ppermute | solution.py:390
  55.4 6.4 %copy-start.5 = (f32[4,128]{1,0:T(4,128)S(1)}, f32[4,128]{1,0:T(4,128)}, u32[]{:S(2)}) copy-start(f32[4,128]{1,0:T(4,128)} %bias_c.5) | copy-start | bytes 6148
  55.4 6.4 %copy-start.6 = (f32[4,128]{1,0:T(4,128)S(1)}, f32[4,128]{1,0:T(4,128)}, u32[]{:S(2)}) copy-start(f32[4,128]{1,0:T(4,128)} %bias_p.5) | copy-start | bytes 6148
  68.7 9.8 %collective-permute-start.10 = (bf16[256,1024]{1,0:T(8,128)(2,1)S(1)}, bf16[256,1024]{1,0:T(8,128)(2,1)S(1)}, u32[]{:S(2)}, u32[]{:S(2)}) collective-permute-start(bf16[256,1024]{1,0:T(8,128)(2,1)S(1)} %broadcast_select_fusion), channel_id=1, source_target_pairs={{0,4},{4,0},{8,12},{12,8},{16,20},{20,16},{24,28},{28,24},{1,5},{5... | collective-permute-start | bytes 1572872 | tf_op jit(solution)/shard_map/ppermute | solution.py:361
  69.0 9.4 %collective-permute-start.13 = (bf16[256,512]{1,0:T(8,128)(2,1)S(1)}, bf16[256,512]{1,0:T(8,128)(2,1)S(1)}, u32[]{:S(2)}, u32[]{:S(2)}) collective-permute-start(bf16[256,512]{1,0:T(8,128)(2,1)S(1)} %collective-permute-done.12), channel_id=1, source_target_pairs={{0,16},{4,20},{8,24},{12,28},{16,0},{20,4},{24,8},{28,12},{1,17},{... | collective-permute-start | bytes 786440 | tf_op jit(solution)/shard_map/ppermute | solution.py:382
  78.5 12.5 %collective-permute-start.14 = (bf16[2,256,512]{2,1,0:T(8,128)(2,1)S(1)}, bf16[2,256,512]{2,1,0:T(8,128)(2,1)S(1)}, u32[]{:S(2)}, u32[]{:S(2)}) collective-permute-start(bf16[2,256,512]{2,1,0:T(8,128)(2,1)S(1)} %pad_maximum_fusion.1.got), channel_id=1, source_target_pairs={{0,4},{4,0},{8,12},{12,8},{16,20},{20,16},{24,28},{28,24},{1,5},{5... | collective-permute-start | bytes 1572872 | tf_op jit(solution)/shard_map/ppermute | solution.py:361
  82.9 22.1 %copy-start.1 = (bf16[512,2048]{1,0:T(8,128)(2,1)S(1)}, bf16[512,2048]{1,0:T(8,128)(2,1)}, u32[]{:S(2)}) copy-start(bf16[512,2048]{1,0:T(8,128)(2,1)} %w_send.3) | copy-start | bytes 6291460
  82.9 22.1 %collective-permute-start.16 = (bf16[256,512]{1,0:T(8,128)(2,1)S(1)}, bf16[256,512]{1,0:T(8,128)(2,1)S(1)}, u32[]{:S(2)}, u32[]{:S(2)}) collective-permute-start(bf16[256,512]{1,0:T(8,128)(2,1)S(1)} %finish.3.own), channel_id=1, source_target_pairs={{0,2},{1,3},{2,0},{3,1},{4,6},{5,7},{6,4},{7,5},{8,10},{9,11},{10,... | collective-permute-start | bytes 786440 | tf_op jit(solution)/shard_map/ppermute | solution.py:358
  90.9 19.6 %collective-permute-start.11 = (bf16[256,512]{1,0:T(8,128)(2,1)S(1)}, bf16[256,512]{1,0:T(8,128)(2,1)S(1)}, u32[]{:S(2)}, u32[]{:S(2)}) collective-permute-start(bf16[256,512]{1,0:T(8,128)(2,1)S(1)} %finish.2.own), channel_id=1, source_target_pairs={{0,2},{1,3},{2,0},{3,1},{4,6},{5,7},{6,4},{7,5},{8,10},{9,11},{10,... | collective-permute-start | bytes 786440 | tf_op jit(solution)/shard_map/ppermute | solution.py:358
  106.3 15.3 %copy-start.8 = (bf16[512,512]{1,0:T(8,128)(2,1)S(1)}, bf16[512,512]{1,0:T(8,128)(2,1)}, u32[]{:S(2)}) copy-start(bf16[512,512]{1,0:T(8,128)(2,1)} %param.10) | copy-start | bytes 1572868
  106.3 9.8 %collective-permute-start.17 = (bf16[256,512]{1,0:T(8,128)(2,1)S(1)}, bf16[256,512]{1,0:T(8,128)(2,1)S(1)}, u32[]{:S(2)}, u32[]{:S(2)}) collective-permute-start(bf16[256,512]{1,0:T(8,128)(2,1)S(1)} %get-tuple-element.40), channel_id=1, source_target_pairs={{0,1},{1,0},{2,3},{3,2},{4,5},{5,4},{6,7},{7,6},{8,9},{9,8},{10,11... | collective-permute-start | bytes 786440 | tf_op jit(solution)/shard_map/ppermute | solution.py:358
  111.8 9.8 %collective-permute-start.15 = (bf16[256,512]{1,0:T(8,128)(2,1)S(1)}, bf16[256,512]{1,0:T(8,128)(2,1)S(1)}, u32[]{:S(2)}, u32[]{:S(2)}) collective-permute-start(bf16[256,512]{1,0:T(8,128)(2,1)S(1)} %get-tuple-element.38), channel_id=1, source_target_pairs={{0,1},{1,0},{2,3},{3,2},{4,5},{5,4},{6,7},{7,6},{8,9},{9,8},{10,11... | collective-permute-start | bytes 786440 | tf_op jit(solution)/shard_map/ppermute | solution.py:358
  121.6 8.3 %copy-start.9 = (f32[512]{0:T(512)S(1)}, f32[512]{0:T(512)}, u32[]{:S(2)}) copy-start(f32[512]{0:T(512)} %param.19) | copy-start | bytes 6148
  121.6 8.3 %copy-start.10 = (f32[512]{0:T(512)S(1)}, f32[512]{0:T(512)}, u32[]{:S(2)}) copy-start(f32[512]{0:T(512)} %param.18) | copy-start | bytes 6148
  122.3 4.5 %collective-permute-start.18 = (f32[2,512]{1,0:T(2,128)S(1)}, f32[2,512]{1,0:T(2,128)S(1)}, u32[]{:S(2)}, u32[]{:S(2)}) collective-permute-start(f32[2,512]{1,0:T(2,128)S(1)} %pad_maximum_fusion.2), channel_id=1, source_target_pairs={{0,1},{1,0},{2,3},{3,2},{4,5},{5,4},{6,7},{7,6},{8,9},{9,8},{10,11... | collective-permute-start | bytes 12296 | tf_op jit(solution)/shard_map/ppermute | solution.py:358
  122.3 4.6 %collective-permute-start.19 = (f32[2,512]{1,0:T(2,128)S(1)}, f32[2,512]{1,0:T(2,128)S(1)}, u32[]{:S(2)}, u32[]{:S(2)}) collective-permute-start(f32[2,512]{1,0:T(2,128)S(1)} %pad_maximum_fusion.2), channel_id=1, source_target_pairs={{0,2},{1,3},{2,0},{3,1},{4,6},{5,7},{6,4},{7,5},{8,10},{9,11},{10,... | collective-permute-start | bytes 12296 | tf_op jit(solution)/shard_map/ppermute | solution.py:358
  124.5 5.4 %collective-permute-start.20 = (f32[2,512]{1,0:T(2,128)S(1)}, f32[2,512]{1,0:T(2,128)S(1)}, u32[]{:S(2)}, u32[]{:S(2)}) collective-permute-start(f32[2,512]{1,0:T(2,128)S(1)} %pad_maximum_fusion.2), channel_id=1, source_target_pairs={{0,3},{1,2},{2,1},{3,0},{4,7},{5,6},{6,5},{7,4},{8,11},{9,10},{10,... | collective-permute-start | bytes 12296 | tf_op jit(solution)/shard_map/ppermute | solution.py:358

commit v4 on v3

--- a/solution.py
+++ b/solution.py
@@ -116,50 +116,44 @@
     )(order, *weights, w_out)
 
 
-def project_kernel(own, one, two, *refs):
-    *three, w_k, w_v, w_q, query, pairs = refs
+def project_kernel(own, one, two, *refs, count):
+    three, weights, outs = refs[: -count - 1], refs[-count - 1 : -1], refs[-1:]
     last = three[0][...]
     if len(three) > 1:
         last = last + three[1][...]
     hidden = jnp.concatenate([own[...], one[...], two[...], last], 1)
-    cols = query.shape[1]
-    for weight, out in (
-        (w_k, pairs.at[:, :cols]),
-        (w_v, pairs.at[:, cols:]),
-        (w_q, query),
-    ):
+    cols = weights[0].shape[1]
+    for i, weight in enumerate(weights):
         total = jnp.dot(hidden, weight[...], preferred_element_type=jnp.float32)
+        out = outs[0] if count == 1 else outs[0].at[:, i * cols : (i + 1) * cols]
         out[...] = total.astype(jnp.bfloat16)
 
 
-def project(hidden, packed, steps=2):
+def project(hidden, packed, parts, steps=2):
     rows, block = hidden[0].shape
     depth = packed.shape[0]
     width = packed.shape[1] // 3
     cols = width // steps
+    count = len(parts)
     return pl.pallas_call(
-        project_kernel,
+        functools.partial(project_kernel, count=count),
         grid=(steps,),
         in_specs=[pl.BlockSpec((rows, block), lambda n: (0, 0)) for _ in hidden]
-        + [pl.BlockSpec((depth, cols), lambda n, i=i: (0, i * steps + n)) for i in range(3)],
-        out_specs=[
-            pl.BlockSpec((rows, cols), lambda n: (0, n)),
-            pl.BlockSpec((rows, 2 * cols), lambda n: (0, n)),
-        ],
-        out_shape=[
-            jax.ShapeDtypeStruct((rows, width), jnp.bfloat16),
-            jax.ShapeDtypeStruct((rows, 2 * width), jnp.bfloat16),
-        ],
+        + [pl.BlockSpec((depth, cols), lambda n, i=i: (0, i * steps + n)) for i in parts],
+        out_specs=pl.BlockSpec((rows, count * cols), lambda n: (0, n)),
+        out_shape=jax.ShapeDtypeStruct((rows, count * width), jnp.bfloat16),
         compiler_params=limit(11),
         cost_estimate=pl.CostEstimate(
-            flops=6 * rows * depth * width, transcendentals=0, bytes_accessed=6 * depth * width
+            flops=2 * count * rows * depth * width,
+            transcendentals=0,
+            bytes_accessed=2 * count * depth * width,
         ),
         name="project",
-    )(*hidden, packed, packed, packed)
+    )(*hidden, *[packed for _ in parts])
 
 
 def attend_kernel(
-    place, bias_c, bias_p, rel, *refs, first, count, pieces, seg, final, head_dim
+    place, bias_c, bias_p, rel, *refs, first, count, pieces, seg, final, head_dim, group
 ):
     queries = refs[:count]
     pairs = refs[count : count + len(pieces)]
@@ -167,10 +161,12 @@
     wide = HP * head_dim
     log2 = 1.4426950408889634 / head_dim**0.5
     lane = lax.broadcasted_iota(jnp.int32, (ROWS, head_dim), 1)
-    for local in range(HP):
-        head = pl.program_id(0) * HP + local
+    for local in range(group):
+        head = pl.program_id(0) * group + local
         mine = slice(local * head_dim, (local + 1) * head_dim)
-        theirs = slice(wide + local * head_dim, wide + (local + 1) * head_dim)
+        base = local // HP * 2 * wide + local % HP * head_dim
+        key = slice(base, base + head_dim)
+        theirs = slice(base + wide, base + wide + head_dim)
         content_bias = bias_c[pl.ds(head, 1), :]
         pos_bias = bias_p[pl.ds(head, 1), :]
         for block, q in enumerate(queries):
@@ -194,7 +190,7 @@
                 )
                 position = pltpu.roll(position, window - (ROWS - 1), 1, stride=1, stride_axis=0)
                 content = lax.dot_general(
-                    content_q, pairs[part][:width, mine], NT, preferred_element_type=jnp.float32
+                    content_q, pairs[part][:width, key], NT, preferred_element_type=jnp.float32
                 )
                 score = content + position[:, :width]
                 back = 2 - start // seg
@@ -244,14 +240,15 @@
 def attend(place, queries, bias_c, bias_p, rel, pairs, pieces, first, seg, before=()):
     heads, head_dim = bias_c.shape
     rows = len(queries) * ROWS
-    wide = HP * head_dim
     final = len(before) > 0
+    group = heads if final else HP
+    wide = group * head_dim
     column = lambda n: pl.BlockSpec((n, wide), lambda h, p: (0, h))
     whole = pl.BlockSpec((heads, head_dim), lambda h, p: (0, 0))
     shape = lambda kind: jax.ShapeDtypeStruct((rows, heads * head_dim), kind)
     grid_spec = pltpu.PrefetchScalarGridSpec(
         num_scalar_prefetch=1,
-        grid=(heads // HP,),
+        grid=(heads // group,),
         in_specs=[whole, whole, column(3 * seg)]
         + [column(ROWS) for _ in queries]
         + [pl.BlockSpec((n.shape[0], 2 * wide), lambda h, p: (0, h)) for n in pairs]
@@ -268,10 +265,11 @@
             seg=seg,
             final=final,
             head_dim=head_dim,
+            group=group,
         ),
         grid_spec=grid_spec,
         out_shape=shape(jnp.bfloat16) if final else [shape(jnp.float32), shape(jnp.float32)],
-        compiler_params=limit(8 if final else 12),
+        compiler_params=limit(12),
         cost_estimate=pl.CostEstimate(
             flops=16 * rows * size * heads * head_dim,
             transcendentals=rows * size * heads,
@@ -384,7 +382,8 @@
 
     query, pairs, back = [], [], []
     for tag, g in zip("ab", gathered):
-        q, kv = project(g, packed)
+        kv = project(g, packed, (0, 1))
+        q = project(g, packed, (2,))
         query.append(q)
         pairs.append(kv)
         back.append(lax.ppermute(kv, "seq", [(i, i + 2) for i in range(seqs - 2)]))

time: 131 us -> 135 us (1.031)
  waiting for transfers between devices: 54.1 us -> 58.3 us
  Pallas kernels: 30.6 us -> 28.7 us
    ppermute x2, waiting for transfers between devices: 5.08 us -> 7.66 us  [shards(): back.append(lax.ppermute(kv, 'seq', [(i, i + 2) for i in range(seqs - 2)]))]
    ppermute x1, starting transfers between devices: 2.51 us -> 4.37 us  [shards(): lax.ppermute(got, 'seq', [(i, i ^ 4) for i in range(seqs)])]
    pallas_call x3, Pallas kernels: 15.4 us -> 13.7 us  [attend(): pl.pallas_call(functools.partial(attend_kernel, first=first, count=len(qu...]
    ppermute x13, waiting for transfers between devices: 38.3 us -> 39.9 us  [across(): return lax.ppermute(x, 'tp', [(i, i ^ k) for i in range(tp)])]
    pallas_call x2 -> x4, Pallas kernels: 5.06 us -> 5.74 us  [project(): pl.pallas_call(functools.partial(project_kernel, count=count), grid=(step...]
  transfers between devices with their start and end apart: 21 -> 21, of which waited for: 10 -> 11; matrix products, arithmetic and copies ran while one was open for 2% -> 2% of each run, Pallas kernels for 23% -> 21%
where the time goes in v4:
time: 135 us; the launch traced here: 134 us
  waiting for transfers between devices  58.3 us (43%)
  starting transfers between devices  35 us (26%)
  Pallas kernels  28.7 us (21%)
  local copies, waits for them, and re-layouts  7.48 us (6%)
  other arithmetic  4.32 us (3%)
    ppermute x13, waiting for transfers between devices, across(): return lax.ppermute(x, 'tp', [(i, i ^ k) for i in range(tp)])  39.9 us
    ppermute x13, starting transfers between devices, across(): return lax.ppermute(x, 'tp', [(i, i ^ k) for i in range(tp)])  20.8 us
    pallas_call x3, Pallas kernels, attend(): pl.pallas_call(functools.partial(attend_kernel, first=first, count=len(qu...  13.7 us
    ppermute x2, waiting for transfers between devices, shards(): back.append(lax.ppermute(kv, 'seq', [(i, i + 2) for i in range(seqs - 2)]))  7.66 us
    ppermute x2, starting transfers between devices, shards(): back.append(lax.ppermute(kv, 'seq', [(i, i + 2) for i in range(seqs - 2)]))  7.66 us
    ppermute x1, waiting for transfers between devices, shards(): lax.ppermute(got, 'seq', [(i, i ^ 4) for i in range(seqs)])  6.89 us
    unnamed x22, local copies, waits for them, and re-layouts  6.4 us
    pallas_call x4, Pallas kernels, project(): pl.pallas_call(functools.partial(project_kernel, count=count), grid=(step...  5.74 us
  transfers between devices with their start and end apart: 21, of which 11 were waited for; matrix products, arithmetic and copies ran while one was open for 2% of the time, Pallas kernels for 21%

profile of v4, /device:TPU:0, one launch (start us, length us, event | category | flops | bytes accessed | tf_op | source)
XLA Modules:
  0.0 134.2 jit_solution(16213670477104047029)
XLA Ops:
  1.2 4.1 %collective-permute-start.1 = (bf16[256,512]{1,0:T(8,128)(2,1)S(1)}, bf16[256,512]{1,0:T(8,128)(2,1)S(1)}, u32[]{:S(2)}, u32[]{:S(2)}) collective-permute-start(bf16[256,512]{1,0:T(8,128)(2,1)S(1)} %get-tuple-element.35.own), channel_id=1, source_target_pairs={{0,2},{1,3},{2,0},{3,1},{4,6},{5,7},{6,4},{7,5},{8,10},{9,11},{10,... | collective-permute-start | bytes 786440 | tf_op jit(solution)/shard_map/ppermute | solution.py:356
  5.4 1.6 %collective-permute-start = (bf16[256,512]{1,0:T(8,128)(2,1)S(1)}, bf16[256,512]{1,0:T(8,128)(2,1)S(1)}, u32[]{:S(2)}, u32[]{:S(2)}) collective-permute-start(bf16[256,512]{1,0:T(8,128)(2,1)S(1)} %get-tuple-element.35.own), channel_id=1, source_target_pairs={{0,1},{1,0},{2,3},{3,2},{4,5},{5,4},{6,7},{7,6},{8,9},{9,8},{10,11... | collective-permute-start | bytes 786440 | tf_op jit(solution)/shard_map/ppermute | solution.py:356
  7.6 2.2 %collective-permute-start.4 = (bf16[256,512]{1,0:T(8,128)(2,1)S(1)}, bf16[256,512]{1,0:T(8,128)(2,1)S(1)}, u32[]{:S(2)}, u32[]{:S(2)}) collective-permute-start(bf16[256,512]{1,0:T(8,128)(2,1)S(1)} %get-tuple-element.36.own), channel_id=1, source_target_pairs={{0,1},{1,0},{2,3},{3,2},{4,5},{5,4},{6,7},{7,6},{8,9},{9,8},{10,11... | collective-permute-start | bytes 786440 | tf_op jit(solution)/shard_map/ppermute | solution.py:356
  10.9 7.3 %collective-permute-done.1.two = bf16[256,512]{1,0:T(8,128)(2,1)S(1)} collective-permute-done((bf16[256,512]{1,0:T(8,128)(2,1)S(1)}, bf16[256,512]{1,0:T(8,128)(2,1)S(1)}, u32[]{:S(2)}, u32[]{:S(2)}) %collective-permute-start.1) | collective-permute-done | bytes 262176 | tf_op jit(solution)/shard_map/ppermute | solution.py:356
  19.5 1.6 %copy-done = bf16[512,2048]{1,0:T(8,128)(2,1)S(1)} copy-done((bf16[512,2048]{1,0:T(8,128)(2,1)S(1)}, bf16[512,2048]{1,0:T(8,128)(2,1)}, u32[]{:S(2)}) %copy-start) | copy-done | bytes 2097176
  21.1 1.6 %copy-done.2 = bf16[2048,512]{1,0:T(8,128)(2,1)S(1)} copy-done((bf16[2048,512]{1,0:T(8,128)(2,1)S(1)}, bf16[2048,512]{1,0:T(8,128)(2,1)}, u32[]{:S(2)}) %copy-start.2) | copy-done | bytes 2097176
  22.7 1.6 %copy-done.3 = bf16[2048,512]{1,0:T(8,128)(2,1)S(1)} copy-done((bf16[2048,512]{1,0:T(8,128)(2,1)S(1)}, bf16[2048,512]{1,0:T(8,128)(2,1)}, u32[]{:S(2)}) %copy-start.3) | copy-done | bytes 2097176
  24.3 1.6 %copy-done.4 = bf16[2048,512]{1,0:T(8,128)(2,1)S(1)} copy-done((bf16[2048,512]{1,0:T(8,128)(2,1)S(1)}, bf16[2048,512]{1,0:T(8,128)(2,1)}, u32[]{:S(2)}) %copy-start.4) | copy-done | bytes 2097176
  27.0 2.8 %collective-permute-start.6 = (bf16[256,512]{1,0:T(8,128)(2,1)S(1)}, bf16[256,512]{1,0:T(8,128)(2,1)S(1)}, u32[]{:S(2)}, u32[]{:S(2)}) collective-permute-start(bf16[256,512]{1,0:T(8,128)(2,1)S(1)} %get-tuple-element.36.own), channel_id=1, source_target_pairs={{0,3},{1,2},{2,1},{3,0},{4,7},{5,6},{6,5},{7,4},{8,11},{9,10},{10,... | collective-permute-start | bytes 786440 | tf_op jit(solution)/shard_map/ppermute | solution.py:356
  29.8 1.3 collective-permute-start.12
  31.2 3.9 %collective-permute-done.3.refs_1_ = bf16[256,512]{1,0:T(8,128)(2,1)S(1)} collective-permute-done((bf16[256,512]{1,0:T(8,128)(2,1)S(1)}, bf16[256,512]{1,0:T(8,128)(2,1)S(1)}, u32[]{:S(2)}, u32[]{:S(2)}) %collective-permute-start.3) | collective-permute-done | bytes 262176 | tf_op jit(solution)/shard_map/ppermute | solution.py:371
  35.1 1.8 %project.7.refs_4_ = bf16[256,1024]{1,0:T(8,128)(2,1)S(1)} custom-call(bf16[256,512]{1,0:T(8,128)(2,1)S(1)} %get-tuple-element.35.own, bf16[256,512]{1,0:T(8,128)(2,1)S(1)} %collective-permute-done.one, bf16[256,512]{1,0:T(8,128)(2,1)S(1)} %collective-permute-done.1.two, bf16[256,512]{1,0:T(8,128)(2,1)S(1)} %collective-permute-done.2.refs_0_, ...), custom_call_target="tpu_custom_call" | custom-call | flops 1073741824 | bytes 4194304 | tf_op jit(solution)/shard_map/project/pallas_call | solution.py:138
  36.9 3.3 %collective-permute-start.8 = (bf16[256,1024]{1,0:T(8,128)(2,1)S(1)}, bf16[256,1024]{1,0:T(8,128)(2,1)S(1)}, u32[]{:S(2)}, u32[]{:S(2)}) collective-permute-start(bf16[256,1024]{1,0:T(8,128)(2,1)S(1)} %project.7.refs_4_), channel_id=1, source_target_pairs={{0,8},{4,12},{8,16},{12,20},{16,24},{20,28},{1,9},{5,13},{9,17},{1... | collective-permute-start | bytes 1572872 | tf_op jit(solution)/shard_map/ppermute | solution.py:389
  40.2 1.9 %multiply_cosine_fusion = (f32[128,1024]{1,0:T(8,128)S(1)}, f32[128,1024]{1,0:T(8,128)S(1)}) fusion(f32[1024]{0:T(1024)S(1)} %multiply_exponential_fusion, f32[128]{0:T(128)S(1)} %subtract_convert_fusion), kind=kLoop, calls=%fused_computation.3 | loop fusion | flops 131072 | bytes 1053184 | tf_op jit(solution)/shard_map/cos | solution.py:28
  42.1 5.1 %collective-permute-done.8.refs_2_ = bf16[256,1024]{1,0:T(8,128)(2,1)S(1)} collective-permute-done((bf16[256,1024]{1,0:T(8,128)(2,1)S(1)}, bf16[256,1024]{1,0:T(8,128)(2,1)S(1)}, u32[]{:S(2)}, u32[]{:S(2)}) %collective-permute-start.8) | collective-permute-done | bytes 524320 | tf_op jit(solution)/shard_map/ppermute | solution.py:389
  47.6 5.5 %relative.1.rel = bf16[1536,512]{1,0:T(8,128)(2,1)S(1)} custom-call(f32[12,1024]{1,0:T(8,128)S(1)} %get-tuple-element.42.far_sin, f32[12,1024]{1,0:T(8,128)S(1)} %get-tuple-element.41.far_cos, f32[128,1024]{1,0:T(8,128)S(1)} %get-tuple-element.40.near_sin, f32[128,1024]{1,0:T(8,128)S(1)} %get-tuple-element.39.near_cos, bf16[2048,512]{1,0:T(8,128)(2,1)S(1)} %copy-done.7), custom_call_target="tpu_custom_call" | custom-call | flops 3221225472 | bytes 4194304 | tf_op jit(solution)/shard_map/relative/pallas_call | solution.py:49
  53.2 1.8 %project.5.refs_5_ = bf16[256,1024]{1,0:T(8,128)(2,1)S(1)} custom-call(bf16[256,512]{1,0:T(8,128)(2,1)S(1)} %get-tuple-element.36.own, bf16[256,512]{1,0:T(8,128)(2,1)S(1)} %collective-permute-done.4.one, bf16[256,512]{1,0:T(8,128)(2,1)S(1)} %collective-permute-done.5.two, bf16[256,512]{1,0:T(8,128)(2,1)S(1)} %collective-permute-done.6.refs_0_, ...), custom_call_target="tpu_custom_call" | custom-call | flops 1073741824 | bytes 4194304 | tf_op jit(solution)/shard_map/project/pallas_call | solution.py:138
  54.9 4.4 %collective-permute-start.7 = (bf16[256,1024]{1,0:T(8,128)(2,1)S(1)}, bf16[256,1024]{1,0:T(8,128)(2,1)S(1)}, u32[]{:S(2)}, u32[]{:S(2)}) collective-permute-start(bf16[256,1024]{1,0:T(8,128)(2,1)S(1)} %project.5.refs_5_), channel_id=1, source_target_pairs={{0,8},{4,12},{8,16},{12,20},{16,24},{20,28},{1,9},{5,13},{9,17},{1... | collective-permute-start | bytes 1572872 | tf_op jit(solution)/shard_map/ppermute | solution.py:389
  61.6 6.9 %begin.1 = (f32[512,512]{1,0:T(8,128)S(1)}, f32[512,512]{1,0:T(8,128)S(1)}) custom-call(s32[1]{0:T(128)} %bitcast.5.place, f32[4,128]{1,0:T(4,128)S(1)} %copy-done.5, f32[4,128]{1,0:T(4,128)S(1)} %copy-done.6, bf16[1536,512]{1,0:T(8,128)(2,1)S(1)} %relative.1.rel, bf16[256,512]{1,0:T(8,128)(2,1)S(1)} %project.4.refs_0_, ...), custom_call_target="tpu_custom_call" | custom-call | flops 4294967296 | bytes 3145728 | tf_op jit(solution)/shard_map/begin/pallas_call | solution.py:259
  68.6 2.6 %collective-permute-done.7.refs_1_ = bf16[256,1024]{1,0:T(8,128)(2,1)S(1)} collective-permute-done((bf16[256,1024]{1,0:T(8,128)(2,1)S(1)}, bf16[256,1024]{1,0:T(8,128)(2,1)S(1)}, u32[]{:S(2)}, u32[]{:S(2)}) %collective-permute-start.7) | collective-permute-done | bytes 524320 | tf_op jit(solution)/shard_map/ppermute | solution.py:389
  71.3 4.4 %collective-permute-start.13 = (bf16[256,512]{1,0:T(8,128)(2,1)S(1)}, bf16[256,512]{1,0:T(8,128)(2,1)S(1)}, u32[]{:S(2)}, u32[]{:S(2)}) collective-permute-start(bf16[256,512]{1,0:T(8,128)(2,1)S(1)} %collective-permute-done.12), channel_id=1, source_target_pairs={{0,16},{4,20},{8,24},{12,28},{16,0},{20,4},{24,8},{28,12},{1,17},{... | collective-permute-start | bytes 786440 | tf_op jit(solution)/shard_map/ppermute | solution.py:380
  75.7 6.9 %collective-permute-done.13 = bf16[256,512]{1,0:T(8,128)(2,1)S(1)} collective-permute-done((bf16[256,512]{1,0:T(8,128)(2,1)S(1)}, bf16[256,512]{1,0:T(8,128)(2,1)S(1)}, u32[]{:S(2)}, u32[]{:S(2)}) %collective-permute-start.13) | collective-permute-done | bytes 262176 | tf_op jit(solution)/shard_map/ppermute | solution.py:380
  82.7 3.4 %finish.3.own = bf16[256,512]{1,0:T(8,128)(2,1)S(1)} custom-call(s32[1]{0:T(128)} %bitcast.5.place, f32[4,128]{1,0:T(4,128)S(1)} %copy-done.5, f32[4,128]{1,0:T(4,128)S(1)} %copy-done.6, bf16[1536,512]{1,0:T(8,128)(2,1)S(1)} %relative.1.rel, bf16[256,512]{1,0:T(8,128)(2,1)S(1)} %project.6.refs_1_.refs_0_, ...), custom_call_target="tpu_custom_call" | custom-call | flops 1073741824 | bytes 1572864 | tf_op jit(solution)/shard_map/finish/pallas_call | solution.py:259
  86.1 1.7 %collective-permute-start.16 = (bf16[256,512]{1,0:T(8,128)(2,1)S(1)}, bf16[256,512]{1,0:T(8,128)(2,1)S(1)}, u32[]{:S(2)}, u32[]{:S(2)}) collective-permute-start(bf16[256,512]{1,0:T(8,128)(2,1)S(1)} %finish.3.own), channel_id=1, source_target_pairs={{0,2},{1,3},{2,0},{3,1},{4,6},{5,7},{6,4},{7,5},{8,10},{9,11},{10,... | collective-permute-start | bytes 786440 | tf_op jit(solution)/shard_map/ppermute | solution.py:356
  87.9 3.4 %finish.2.own = bf16[256,512]{1,0:T(8,128)(2,1)S(1)} custom-call(s32[1]{0:T(128)} %bitcast.5.place, f32[4,128]{1,0:T(4,128)S(1)} %copy-done.5, f32[4,128]{1,0:T(4,128)S(1)} %copy-done.6, bf16[1536,512]{1,0:T(8,128)(2,1)S(1)} %relative.1.rel, bf16[256,512]{1,0:T(8,128)(2,1)S(1)} %project.4.refs_0_, bf16[256,1024]{1,0:T(8,128)(2,1)S(1)} %collective-permute-done.7.refs_1_, ...), custom_call_target="tpu_custom_call" | custom-call | flops 1073741824 | bytes 1572864 | tf_op jit(solution)/shard_map/finish/pallas_call | solution.py:259
  91.3 1.3 %collective-permute-start.11 = (bf16[256,512]{1,0:T(8,128)(2,1)S(1)}, bf16[256,512]{1,0:T(8,128)(2,1)S(1)}, u32[]{:S(2)}, u32[]{:S(2)}) collective-permute-start(bf16[256,512]{1,0:T(8,128)(2,1)S(1)} %finish.2.own), channel_id=1, source_target_pairs={{0,2},{1,3},{2,0},{3,1},{4,6},{5,7},{6,4},{7,5},{8,10},{9,11},{10,... | collective-permute-start | bytes 786440 | tf_op jit(solution)/shard_map/ppermute | solution.py:356
  92.6 14.4 %collective-permute-done.16.other = bf16[256,512]{1,0:T(8,128)(2,1)S(1)} collective-permute-done((bf16[256,512]{1,0:T(8,128)(2,1)S(1)}, bf16[256,512]{1,0:T(8,128)(2,1)S(1)}, u32[]{:S(2)}, u32[]{:S(2)}) %collective-permute-start.16) | collective-permute-done | bytes 262176 | tf_op jit(solution)/shard_map/ppermute | solution.py:356
  108.4 4.3 %collective-permute-done.11.other = bf16[256,512]{1,0:T(8,128)(2,1)S(1)} collective-permute-done((bf16[256,512]{1,0:T(8,128)(2,1)S(1)}, bf16[256,512]{1,0:T(8,128)(2,1)S(1)}, u32[]{:S(2)}, u32[]{:S(2)}) %collective-permute-start.11) | collective-permute-done | bytes 262176 | tf_op jit(solution)/shard_map/ppermute | solution.py:356
  114.1 4.2 %collective-permute-done.17 = bf16[256,512]{1,0:T(8,128)(2,1)S(1)} collective-permute-done((bf16[256,512]{1,0:T(8,128)(2,1)S(1)}, bf16[256,512]{1,0:T(8,128)(2,1)S(1)}, u32[]{:S(2)}, u32[]{:S(2)}) %collective-permute-start.17) | collective-permute-done | bytes 262176 | tf_op jit(solution)/shard_map/ppermute | solution.py:356
  118.3 5.5 %collective-permute-done.15 = bf16[256,512]{1,0:T(8,128)(2,1)S(1)} collective-permute-done((bf16[256,512]{1,0:T(8,128)(2,1)S(1)}, bf16[256,512]{1,0:T(8,128)(2,1)S(1)}, u32[]{:S(2)}, u32[]{:S(2)}) %collective-permute-start.15) | collective-permute-done | bytes 262176 | tf_op jit(solution)/shard_map/ppermute | solution.py:356
  124.6 3.2 %collective-permute-start.19 = (f32[2,512]{1,0:T(2,128)S(1)}, f32[2,512]{1,0:T(2,128)S(1)}, u32[]{:S(2)}, u32[]{:S(2)}) collective-permute-start(f32[2,512]{1,0:T(2,128)S(1)} %pad_maximum_fusion.2), channel_id=1, source_target_pairs={{0,2},{1,3},{2,0},{3,1},{4,6},{5,7},{6,4},{7,5},{8,10},{9,11},{10,... | collective-permute-start | bytes 12296 | tf_op jit(solution)/shard_map/ppermute | solution.py:356
  129.4 3.8 %collective-permute-done.20 = f32[2,512]{1,0:T(2,128)S(1)} collective-permute-done((f32[2,512]{1,0:T(2,128)S(1)}, f32[2,512]{1,0:T(2,128)S(1)}, u32[]{:S(2)}, u32[]{:S(2)}) %collective-permute-start.20) | collective-permute-done | bytes 4128 | tf_op jit(solution)/shard_map/ppermute | solution.py:356
  (68 shorter events, 14.6 us)
Async XLA Ops:
  1.2 16.9 %collective-permute-start.1 = (bf16[256,512]{1,0:T(8,128)(2,1)S(1)}, bf16[256,512]{1,0:T(8,128)(2,1)S(1)}, u32[]{:S(2)}, u32[]{:S(2)}) collective-permute-start(bf16[256,512]{1,0:T(8,128)(2,1)S(1)} %get-tuple-element.35.own), channel_id=1, source_target_pairs={{0,2},{1,3},{2,0},{3,1},{4,6},{5,7},{6,4},{7,5},{8,10},{9,11},{10,... | collective-permute-start | bytes 786440 | tf_op jit(solution)/shard_map/ppermute | solution.py:356
  5.4 21.6 %collective-permute-start = (bf16[256,512]{1,0:T(8,128)(2,1)S(1)}, bf16[256,512]{1,0:T(8,128)(2,1)S(1)}, u32[]{:S(2)}, u32[]{:S(2)}) collective-permute-start(bf16[256,512]{1,0:T(8,128)(2,1)S(1)} %get-tuple-element.35.own), channel_id=1, source_target_pairs={{0,1},{1,0},{2,3},{3,2},{4,5},{5,4},{6,7},{7,6},{8,9},{9,8},{10,11... | collective-permute-start | bytes 786440 | tf_op jit(solution)/shard_map/ppermute | solution.py:356
  6.9 22.9 %collective-permute-start.2 = (bf16[256,512]{1,0:T(8,128)(2,1)S(1)}, bf16[256,512]{1,0:T(8,128)(2,1)S(1)}, u32[]{:S(2)}, u32[]{:S(2)}) collective-permute-start(bf16[256,512]{1,0:T(8,128)(2,1)S(1)} %get-tuple-element.35.own), channel_id=1, source_target_pairs={{1,2},{2,1},{5,6},{6,5},{9,10},{10,9},{13,14},{14,13},{17,18},{18,... | collective-permute-start | bytes 786440 | tf_op jit(solution)/shard_map/ppermute | solution.py:370
  7.6 45.5 %collective-permute-start.4 = (bf16[256,512]{1,0:T(8,128)(2,1)S(1)}, bf16[256,512]{1,0:T(8,128)(2,1)S(1)}, u32[]{:S(2)}, u32[]{:S(2)}) collective-permute-start(bf16[256,512]{1,0:T(8,128)(2,1)S(1)} %get-tuple-element.36.own), channel_id=1, source_target_pairs={{0,1},{1,0},{2,3},{3,2},{4,5},{5,4},{6,7},{7,6},{8,9},{9,8},{10,11... | collective-permute-start | bytes 786440 | tf_op jit(solution)/shard_map/ppermute | solution.py:356
  9.8 43.3 %collective-permute-start.5 = (bf16[256,512]{1,0:T(8,128)(2,1)S(1)}, bf16[256,512]{1,0:T(8,128)(2,1)S(1)}, u32[]{:S(2)}, u32[]{:S(2)}) collective-permute-start(bf16[256,512]{1,0:T(8,128)(2,1)S(1)} %get-tuple-element.36.own), channel_id=1, source_target_pairs={{0,2},{1,3},{2,0},{3,1},{4,6},{5,7},{6,4},{7,5},{8,10},{9,11},{10,... | collective-permute-start | bytes 786440 | tf_op jit(solution)/shard_map/ppermute | solution.py:356
  18.2 16.9 %collective-permute-start.3 = (bf16[256,512]{1,0:T(8,128)(2,1)S(1)}, bf16[256,512]{1,0:T(8,128)(2,1)S(1)}, u32[]{:S(2)}, u32[]{:S(2)}) collective-permute-start(bf16[256,512]{1,0:T(8,128)(2,1)S(1)} %collective-permute-done.1.two), channel_id=1, source_target_pairs={{1,0},{2,3},{5,4},{6,7},{9,8},{10,11},{13,12},{14,15},{17,16},{18,... | collective-permute-start | bytes 786440 | tf_op jit(solution)/shard_map/ppermute | solution.py:371
  19.5 1.6 %copy-start = (bf16[512,2048]{1,0:T(8,128)(2,1)S(1)}, bf16[512,2048]{1,0:T(8,128)(2,1)}, u32[]{:S(2)}) copy-start(bf16[512,2048]{1,0:T(8,128)(2,1)} %w_send.3) | copy-start | bytes 6291460
  21.1 1.6 %copy-start.2 = (bf16[2048,512]{1,0:T(8,128)(2,1)S(1)}, bf16[2048,512]{1,0:T(8,128)(2,1)}, u32[]{:S(2)}) copy-start(bf16[2048,512]{1,0:T(8,128)(2,1)} %w_q.1) | copy-start | bytes 6291460
  22.7 1.6 %copy-start.3 = (bf16[2048,512]{1,0:T(8,128)(2,1)S(1)}, bf16[2048,512]{1,0:T(8,128)(2,1)}, u32[]{:S(2)}) copy-start(bf16[2048,512]{1,0:T(8,128)(2,1)} %w_k.1) | copy-start | bytes 6291460
  24.3 1.6 %copy-start.4 = (bf16[2048,512]{1,0:T(8,128)(2,1)S(1)}, bf16[2048,512]{1,0:T(8,128)(2,1)}, u32[]{:S(2)}) copy-start(bf16[2048,512]{1,0:T(8,128)(2,1)} %w_v.1) | copy-start | bytes 6291460
  27.0 26.2 %collective-permute-start.6 = (bf16[256,512]{1,0:T(8,128)(2,1)S(1)}, bf16[256,512]{1,0:T(8,128)(2,1)S(1)}, u32[]{:S(2)}, u32[]{:S(2)}) collective-permute-start(bf16[256,512]{1,0:T(8,128)(2,1)S(1)} %get-tuple-element.36.own), channel_id=1, source_target_pairs={{0,3},{1,2},{2,1},{3,0},{4,7},{5,6},{6,5},{7,4},{8,11},{9,10},{10,... | collective-permute-start | bytes 786440 | tf_op jit(solution)/shard_map/ppermute | solution.py:356
  29.8 41.5 %collective-permute-start.12 = (bf16[256,512]{1,0:T(8,128)(2,1)S(1)}, bf16[256,512]{1,0:T(8,128)(2,1)S(1)}, u32[]{:S(2)}, u32[]{:S(2)}) collective-permute-start(bf16[256,512]{1,0:T(8,128)(2,1)S(1)} %get-tuple-element.28), channel_id=1, source_target_pairs={{0,2},{1,3},{2,0},{3,1},{4,6},{5,7},{6,4},{7,5},{8,10},{9,11},{10,... | collective-permute-start | bytes 786440 | tf_op jit(solution)/shard_map/ppermute | solution.py:356
  36.8 10.8 %copy-start.7 = (bf16[2048,512]{1,0:T(8,128)(2,1)S(1)}, bf16[2048,512]{1,0:T(8,128)(2,1)}, u32[]{:S(2)}) copy-start(bf16[2048,512]{1,0:T(8,128)(2,1)} %weight.1) | copy-start | bytes 6291460
  36.9 10.3 %collective-permute-start.8 = (bf16[256,1024]{1,0:T(8,128)(2,1)S(1)}, bf16[256,1024]{1,0:T(8,128)(2,1)S(1)}, u32[]{:S(2)}, u32[]{:S(2)}) collective-permute-start(bf16[256,1024]{1,0:T(8,128)(2,1)S(1)} %project.7.refs_4_), channel_id=1, source_target_pairs={{0,8},{4,12},{8,16},{12,20},{16,24},{20,28},{1,9},{5,13},{9,17},{1... | collective-permute-start | bytes 1572872 | tf_op jit(solution)/shard_map/ppermute | solution.py:389
  47.2 14.4 %collective-permute-start.9 = (bf16[256,1024]{1,0:T(8,128)(2,1)S(1)}, bf16[256,1024]{1,0:T(8,128)(2,1)S(1)}, u32[]{:S(2)}, u32[]{:S(2)}) collective-permute-start(bf16[256,1024]{1,0:T(8,128)(2,1)S(1)} %broadcast_select_fusion.1), channel_id=1, source_target_pairs={{0,4},{4,0},{8,12},{12,8},{16,20},{20,16},{24,28},{28,24},{1,5},{5... | collective-permute-start | bytes 1572872 | tf_op jit(solution)/shard_map/ppermute | solution.py:359
  54.9 16.2 %collective-permute-start.7 = (bf16[256,1024]{1,0:T(8,128)(2,1)S(1)}, bf16[256,1024]{1,0:T(8,128)(2,1)S(1)}, u32[]{:S(2)}, u32[]{:S(2)}) collective-permute-start(bf16[256,1024]{1,0:T(8,128)(2,1)S(1)} %project.5.refs_5_), channel_id=1, source_target_pairs={{0,8},{4,12},{8,16},{12,20},{16,24},{20,28},{1,9},{5,13},{9,17},{1... | collective-permute-start | bytes 1572872 | tf_op jit(solution)/shard_map/ppermute | solution.py:389
  60.5 1.2 copy-start.5
  60.5 1.2 copy-start.6
  71.2 11.5 %collective-permute-start.10 = (bf16[256,1024]{1,0:T(8,128)(2,1)S(1)}, bf16[256,1024]{1,0:T(8,128)(2,1)S(1)}, u32[]{:S(2)}, u32[]{:S(2)}) collective-permute-start(bf16[256,1024]{1,0:T(8,128)(2,1)S(1)} %broadcast_select_fusion), channel_id=1, source_target_pairs={{0,4},{4,0},{8,12},{12,8},{16,20},{20,16},{24,28},{28,24},{1,5},{5... | collective-permute-start | bytes 1572872 | tf_op jit(solution)/shard_map/ppermute | solution.py:359
  71.3 11.3 %collective-permute-start.13 = (bf16[256,512]{1,0:T(8,128)(2,1)S(1)}, bf16[256,512]{1,0:T(8,128)(2,1)S(1)}, u32[]{:S(2)}, u32[]{:S(2)}) collective-permute-start(bf16[256,512]{1,0:T(8,128)(2,1)S(1)} %collective-permute-done.12), channel_id=1, source_target_pairs={{0,16},{4,20},{8,24},{12,28},{16,0},{20,4},{24,8},{28,12},{1,17},{... | collective-permute-start | bytes 786440 | tf_op jit(solution)/shard_map/ppermute | solution.py:380
  82.6 10.0 %collective-permute-start.14 = (bf16[2,256,512]{2,1,0:T(8,128)(2,1)S(1)}, bf16[2,256,512]{2,1,0:T(8,128)(2,1)S(1)}, u32[]{:S(2)}, u32[]{:S(2)}) collective-permute-start(bf16[2,256,512]{2,1,0:T(8,128)(2,1)S(1)} %pad_maximum_fusion.1.got), channel_id=1, source_target_pairs={{0,4},{4,0},{8,12},{12,8},{16,20},{20,16},{24,28},{28,24},{1,5},{5... | collective-permute-start | bytes 1572872 | tf_op jit(solution)/shard_map/ppermute | solution.py:359
  86.1 20.9 %copy-start.1 = (bf16[512,2048]{1,0:T(8,128)(2,1)S(1)}, bf16[512,2048]{1,0:T(8,128)(2,1)}, u32[]{:S(2)}) copy-start(bf16[512,2048]{1,0:T(8,128)(2,1)} %w_send.3) | copy-start | bytes 6291460
  86.1 20.9 %collective-permute-start.16 = (bf16[256,512]{1,0:T(8,128)(2,1)S(1)}, bf16[256,512]{1,0:T(8,128)(2,1)S(1)}, u32[]{:S(2)}, u32[]{:S(2)}) collective-permute-start(bf16[256,512]{1,0:T(8,128)(2,1)S(1)} %finish.3.own), channel_id=1, source_target_pairs={{0,2},{1,3},{2,0},{3,1},{4,6},{5,7},{6,4},{7,5},{8,10},{9,11},{10,... | collective-permute-start | bytes 786440 | tf_op jit(solution)/shard_map/ppermute | solution.py:356
  91.3 21.4 %collective-permute-start.11 = (bf16[256,512]{1,0:T(8,128)(2,1)S(1)}, bf16[256,512]{1,0:T(8,128)(2,1)S(1)}, u32[]{:S(2)}, u32[]{:S(2)}) collective-permute-start(bf16[256,512]{1,0:T(8,128)(2,1)S(1)} %finish.2.own), channel_id=1, source_target_pairs={{0,2},{1,3},{2,0},{3,1},{4,6},{5,7},{6,4},{7,5},{8,10},{9,11},{10,... | collective-permute-start | bytes 786440 | tf_op jit(solution)/shard_map/ppermute | solution.py:356
  108.3 15.5 %copy-start.8 = (bf16[512,512]{1,0:T(8,128)(2,1)S(1)}, bf16[512,512]{1,0:T(8,128)(2,1)}, u32[]{:S(2)}) copy-start(bf16[512,512]{1,0:T(8,128)(2,1)} %param.10) | copy-start | bytes 1572868
  108.4 9.9 %collective-permute-start.17 = (bf16[256,512]{1,0:T(8,128)(2,1)S(1)}, bf16[256,512]{1,0:T(8,128)(2,1)S(1)}, u32[]{:S(2)}, u32[]{:S(2)}) collective-permute-start(bf16[256,512]{1,0:T(8,128)(2,1)S(1)} %get-tuple-element.32), channel_id=1, source_target_pairs={{0,1},{1,0},{2,3},{3,2},{4,5},{5,4},{6,7},{7,6},{8,9},{9,8},{10,11... | collective-permute-start | bytes 786440 | tf_op jit(solution)/shard_map/ppermute | solution.py:356
  114.0 9.8 %collective-permute-start.15 = (bf16[256,512]{1,0:T(8,128)(2,1)S(1)}, bf16[256,512]{1,0:T(8,128)(2,1)S(1)}, u32[]{:S(2)}, u32[]{:S(2)}) collective-permute-start(bf16[256,512]{1,0:T(8,128)(2,1)S(1)} %get-tuple-element.30), channel_id=1, source_target_pairs={{0,1},{1,0},{2,3},{3,2},{4,5},{5,4},{6,7},{7,6},{8,9},{9,8},{10,11... | collective-permute-start | bytes 786440 | tf_op jit(solution)/shard_map/ppermute | solution.py:356
  123.8 9.4 %copy-start.9 = (f32[512]{0:T(512)S(1)}, f32[512]{0:T(512)}, u32[]{:S(2)}) copy-start(f32[512]{0:T(512)} %param.19) | copy-start | bytes 6148
  123.8 9.4 %copy-start.10 = (f32[512]{0:T(512)S(1)}, f32[512]{0:T(512)}, u32[]{:S(2)}) copy-start(f32[512]{0:T(512)} %param.18) | copy-start | bytes 6148
  124.5 4.5 %collective-permute-start.18 = (f32[2,512]{1,0:T(2,128)S(1)}, f32[2,512]{1,0:T(2,128)S(1)}, u32[]{:S(2)}, u32[]{:S(2)}) collective-permute-start(f32[2,512]{1,0:T(2,128)S(1)} %pad_maximum_fusion.2), channel_id=1, source_target_pairs={{0,1},{1,0},{2,3},{3,2},{4,5},{5,4},{6,7},{7,6},{8,9},{9,8},{10,11... | collective-permute-start | bytes 12296 | tf_op jit(solution)/shard_map/ppermute | solution.py:356
  124.6 4.8 %collective-permute-start.19 = (f32[2,512]{1,0:T(2,128)S(1)}, f32[2,512]{1,0:T(2,128)S(1)}, u32[]{:S(2)}, u32[]{:S(2)}) collective-permute-start(f32[2,512]{1,0:T(2,128)S(1)} %pad_maximum_fusion.2), channel_id=1, source_target_pairs={{0,2},{1,3},{2,0},{3,1},{4,6},{5,7},{6,4},{7,5},{8,10},{9,11},{10,... | collective-permute-start | bytes 12296 | tf_op jit(solution)/shard_map/ppermute | solution.py:356
  127.8 5.4 %collective-permute-start.20 = (f32[2,512]{1,0:T(2,128)S(1)}, f32[2,512]{1,0:T(2,128)S(1)}, u32[]{:S(2)}, u32[]{:S(2)}) collective-permute-start(f32[2,512]{1,0:T(2,128)S(1)} %pad_maximum_fusion.2), channel_id=1, source_target_pairs={{0,3},{1,2},{2,1},{3,0},{4,7},{5,6},{6,5},{7,4},{8,11},{9,10},{10,... | collective-permute-start | bytes 12296 | tf_op jit(solution)/shard_map/ppermute | solution.py:356
